TPU v7x, 32 devices: a whole 2x2x4 slice. The times are simulated.
32 devices in a mesh: gx: 4 (over y, x), gy: 8 (over z, core).
Axes of the slice: x: 2, y: 2, z: 4, core: 2. Of those that a mesh axis runs over, the one named last changes fastest.
Arguments:
- features: bfloat16 [131072, 256], P(('gx', 'gy')), may hold values from -0.375 to 0.375
- inv_width: bfloat16 [131072], P(('gx', 'gy')), may hold values from 0.29882812 to 3
- start_block: float32 [32, 131072], P(None, ('gx', 'gy')), may hold values from -6 to 6
- neighbour_ids: int32 [1024, 16], P(('gx', 'gy')), may hold values from 0 to 1023, as said below
- slot_mask: int32 [1024, 16], P(('gx', 'gy')), may hold values from 0 to 1
Outputs:
- basis: float32 [32, 131072], P(None, ('gx', 'gy'))
- factor: float32 [32, 32], replicated
Inputs may be any that keep to these rules, and one draw needn't show every extreme that they name: `neighbour_ids`: entry j = 0 of every band b is b itself with slot_mask 1; wherever slot_mask is 0 the entry is b. Band c is held by device c // 32 (devices in the order gx, then gy). The entries with mask 1 of one device's bands name at most 2 distinct bands held by any one other device, and every device names exactly 2 bands of some other device.
All inputs are finite; a program needn't handle non-finite values.
Results may differ from a plain program's by a relative error of at most 0.0025.
Values may be sent and summed in bfloat16 or wider, within the bound.
No kernel may reach another device: no remote copies, remote signals or barrier semaphores. Data moves between devices by JAX's collectives and lax.ppermute only.
A program may use at most 128 MiB of HBM per device.

v0:
```python
import jax
import jax.numpy as jnp
from jax import lax
from jax.sharding import PartitionSpec as P

F = 256
VECTORS = 32
BAND = 128
MOST = 2
DEGREE = 4


LOW_EDGE = 0.2
HIGH_EDGE = 2.0


def chebyshev_terms():
    centre = 0.5 * (LOW_EDGE + HIGH_EDGE)
    halfwidth = 0.5 * (HIGH_EDGE - LOW_EDGE)
    anchor = -centre / halfwidth
    values = [1.0, anchor]
    for repeat in range(DEGREE - 1):
        values.append(2.0 * anchor * values[-1] - values[-2])
    return (centre, halfwidth, values)


def move_features(send_coords, send_widths):
    return (
        lax.all_to_all(send_coords, ("gx", "gy"), split_axis=0, concat_axis=0, tiled=True),
        lax.all_to_all(send_widths, ("gx", "gy"), split_axis=0, concat_axis=0, tiled=True),
    )


def move_vectors(send_rows):
    return lax.all_to_all(send_rows, ("gx", "gy"), split_axis=0, concat_axis=0, tiled=True)


def on_device(features, inv_width, start_block, neighbour_ids, slot_mask):
    band_count = neighbour_ids.shape[0]
    devices = lax.axis_size(("gx", "gy"))
    device = lax.axis_index(("gx", "gy"))
    all_bands = jnp.arange(devices * band_count, dtype=jnp.int32)
    owner_dev = neighbour_ids // band_count
    within = neighbour_ids % band_count
    remote = (slot_mask == 1) & (owner_dev != device)
    flat_ids = neighbour_ids.reshape(-1)
    flat_remote = remote.reshape(-1)
    matches = (flat_ids[:, None] == all_bands[None, :]) & flat_remote[:, None]
    need_mine = jnp.any(matches, axis=0).astype(jnp.int32).reshape(devices, band_count)
    rank_mine = jnp.cumsum(need_mine, axis=1) - 1
    rank_lookup = jnp.take(rank_mine.reshape(-1), neighbour_ids, axis=0)
    slot_pos = jnp.where(remote, band_count + owner_dev * MOST + rank_lookup, within)
    wanted = lax.all_to_all(need_mine, ("gx", "gy"), split_axis=0, concat_axis=0, tiled=True)
    rank_send = jnp.cumsum(wanted, axis=1) - 1
    picks = (wanted[:, None, :] == 1) & (
        rank_send[:, None, :] == jnp.arange(MOST, dtype=jnp.int32)[None, :, None]
    )
    send_index = jnp.sum(
        picks.astype(jnp.int32) * jnp.arange(band_count, dtype=jnp.int32)[None, None, :], axis=2
    )
    feature_bands = features.reshape(band_count, BAND, F)
    width_bands = inv_width.reshape(band_count, BAND)
    send_coords = jnp.take(feature_bands, send_index, axis=0)
    send_widths = jnp.take(width_bands, send_index, axis=0)
    got_coords, got_widths = move_features(send_coords, send_widths)
    table_coords = jnp.concatenate(
        [feature_bands, got_coords.reshape(devices * MOST, BAND, F)], axis=0
    )
    table_widths = jnp.concatenate([width_bands, got_widths.reshape(devices * MOST, BAND)], axis=0)
    table_squares = jnp.einsum(
        "tsf,tsf->ts", table_coords, table_coords, preferred_element_type=jnp.float32
    )
    slot_coords = jnp.take(table_coords, slot_pos, axis=0)
    near_sq = jnp.take(table_squares, slot_pos, axis=0)
    near_width = jnp.take(table_widths, slot_pos, axis=0).astype(jnp.float32)
    own_sq = table_squares[:band_count]
    own_width = width_bands.astype(jnp.float32)
    inner = jnp.einsum(
        "brf,bjsf->bjrs", feature_bands, slot_coords, preferred_element_type=jnp.float32
    )
    distance = own_sq[:, None, :, None] + near_sq[:, :, None, :] - 2.0 * inner
    spread = own_width[:, None, :, None] * near_width[:, :, None, :]
    weights = slot_mask.astype(jnp.float32)[:, :, None, None] * jnp.exp(-distance * spread)
    degree = jnp.sum(weights, axis=(1, 3))
    root_inv = 1.0 / jnp.sqrt(degree)
    tiles = weights.astype(jnp.bfloat16)

    def graph(block):
        scaled = (root_inv[:, None, :] * block).astype(jnp.bfloat16)
        send_rows = jnp.take(scaled, send_index, axis=0)
        got_rows = move_vectors(send_rows)
        table_rows = jnp.concatenate(
            [scaled, got_rows.reshape((devices * MOST,) + scaled.shape[1:])], axis=0
        )
        slot_rows = jnp.take(table_rows, slot_pos, axis=0)
        mixed = jnp.einsum("bjrs,bjks->bkr", tiles, slot_rows, preferred_element_type=jnp.float32)
        return root_inv[:, None, :] * mixed

    centre, halfwidth, values = chebyshev_terms()

    def shifted(block):
        return ((1.0 - centre) * block - graph(block)) / halfwidth

    previous = start_block.reshape(VECTORS, band_count, BAND).transpose(1, 0, 2)
    current = shifted(previous) / values[1]
    for power in range(1, DEGREE):
        following = (
            2.0 * values[power] / values[power + 1] * shifted(current)
            - values[power - 1] / values[power + 1] * previous
        )
        previous, current = (current, following)
    partial_gram = jnp.einsum("bkr,bmr->km", current, current, precision=lax.Precision.HIGHEST)
    total_rows = devices * band_count * BAND
    gram = lax.psum(partial_gram, ("gx", "gy")) / total_rows
    factor = jnp.linalg.cholesky(gram)
    flat = current.transpose(1, 0, 2).reshape(VECTORS, band_count * BAND)
    basis = jax.scipy.linalg.solve_triangular(factor, flat, lower=True)
    return (basis, factor)


def solution(mesh):
    placed = (
        P(("gx", "gy"), None),
        P(("gx", "gy")),
        P(None, ("gx", "gy")),
        P(("gx", "gy"), None),
        P(("gx", "gy"), None),
    )
    return jax.shard_map(
        on_device,
        mesh=mesh,
        in_specs=placed,
        out_specs=(P(None, ("gx", "gy")), P()),
        check_vma=False,
    )
```

profile of v0, /device:TPU:0, one launch (start us, length us, event | category | flops | bytes accessed | tf_op | source)
XLA Modules:
  0.0 368.0 jit_solution(85231813181627766)
XLA Ops:
  0.6 0.8 copy.167
  1.4 0.8 copy.168
  2.4 0.4 fusion.28
  2.8 14.3 %all_to_all.36 = s32[32,1,32]{2,1,0:T(1,128)S(1)} all-to-all(s32[32,1,32]{2,1,0:T(1,128)S(1)} %reshape.141), channel_id=1, replica_groups=mesh['gx'=4,'gy'=8] {'gx','gy'}, dimensions={0} | all-to-all | bytes 8192 | tf_op jit(solution)/shard_map/all_to_all | solution.py:53
  17.1 0.2 reduce_window_sum.20
  17.3 0.1 select_reduce_fusion
  17.5 0.1 copy.174
  17.7 0.1 reshape.209
  17.8 4.3 %gather_fusion = bf16[64,128,256]{2,1,0:T(8,128)(2,1)} fusion(bf16[32,128,256]{2,1,0:T(8,128)(2,1)} %bitcast.136, s32[1024]{0:T(1024)S(1)} %pad_clamp_fusion.3), kind=kCustom, calls=%fused_computation.8 | custom fusion | bytes 8388864 | tf_op jit(solution)/shard_map/jit(_take)/gather | solution.py:63
  22.1 0.6 gather_fusion.4
  22.8 0.7 broadcast_select_fusion.6
  23.5 2.5 all-to-all-start.2
  26.0 4.6 %broadcast_select_fusion = bf16[32,2,128,256]{3,2,1,0:T(8,128)(2,1)} fusion(bf16[32,2,128,256]{3,2,1,0:T(8,128)(2,1)} %bitcast.144, pred[32,2]{1,0:T(8,128)(4,1)S(1)} %copy.174), kind=kLoop, calls=%fused_computation.40 | loop fusion | flops 2097152 | bytes 8388672 | tf_op jit(solution)/shard_map/jit(_take)/select_n | solution.py:63
  30.6 2.5 all-to-all-done.2
  33.1 3.6 all-to-all-start.1
  36.8 0.2 reduce_window_sum.21
  37.2 2.3 gather_fusion.1
  40.1 1.3 gather_fusion.5
  41.5 0.1 select_convert_fusion
  41.6 90.0 %all-to-all-done.1 = bf16[32,2,128,256]{3,2,1,0:T(8,128)(2,1)} async-done(((bf16[32,2,128,256]{3,2,1,0:T(8,128)(2,1)}), bf16[32,2,128,256]{3,2,1,0:T(8,128)(2,1)}, u32[]{:S(2)}, u32[]{:S(2)}) %all-to-all-start.1) | async-done | bytes 4194336 | tf_op jit(solution)/shard_map/all_to_all | solution.py:29
  131.7 3.9 %fusion.10 = f32[96,128]{1,0:T(8,128)S(1)} fusion(bf16[64,128,256]{2,1,0:T(8,128)(2,1)} %bitcast.7, bf16[32,128,256]{2,1,0:T(8,128)(2,1)S(1)} %bitcast.137), kind=kLoop, calls=%fused_computation.26 | loop fusion | flops 12570624 | bytes 6340608 | tf_op jit(solution)/shard_map/tsf,tsf->ts/dot_general | solution.py:70
  135.6 5.3 %pad_maximum_fusion = bf16[96,128,256]{2,1,0:T(8,128)(2,1)} fusion(bf16[64,128,256]{2,1,0:T(8,128)(2,1)} %bitcast.7, bf16[32,128,256]{2,1,0:T(8,128)(2,1)S(1)} %bitcast.138), kind=kLoop, calls=%fused_computation.27 | loop fusion | flops 3145728 | bytes 12582912 | tf_op jit(solution)/shard_map/concatenate | solution.py:66
  140.9 1.0 gather_fusion.2
  141.9 0.1 broadcast_select_fusion.5
  142.1 18.9 %gather_fusion.3 = bf16[512,128,256]{2,1,0:T(8,128)(2,1)} fusion(bf16[96,128,256]{2,1,0:T(8,128)(2,1)} %pad_maximum_fusion, s32[1024]{0:T(1024)S(1)} %pad_clamp_fusion.1), kind=kCustom, calls=%fused_computation.11 | custom fusion | bytes 67110912 | tf_op jit(solution)/shard_map/jit(_take)/gather | solution.py:73
  161.0 23.7 %fusion.8 = (f32[32,128]{1,0:T(8,128)S(1)}, bf16[32,16,128,128]{2,3,1,0:T(8,128)(2,1)}) fusion(f32[32,16,128]{2,1,0:T(8,128)S(1)} %select_convert_fusion, f32[32,128]{1,0:T(8,128)S(1)} %bitcast_convert_fusion, f32[32,16,128]{2,1,0:T(8,128)S(1)} %broadcast_select_fusion.5, f32[32,128]{1,0:T(8,128)S(1)} %slice-done, f32[32,16]{1,0:T(8,128)S(1)} %copy.166, ...), kind=kOutput, calls=%fused_computation.23 | convolution fusion | flops 4387237888 | bytes 53004800 | tf_op jit(solution)/shard_map/brf,bjsf->bjrs/dot_general | solution.py:78
  184.7 0.9 bitcast_multiply_fusion.2
  185.6 0.1 copy.182
  185.7 0.7 gather_fusion.6
  186.4 0.1 broadcast_select_fusion.4
  186.5 18.2 %all_to_all.37 = bf16[32,2,32,128]{3,2,1,0:T(8,128)(2,1)S(1)} all-to-all(bf16[32,2,32,128]{3,2,1,0:T(8,128)(2,1)S(1)} %broadcast_select_fusion.4), channel_id=1, replica_groups=mesh['gx'=4,'gy'=8] {'gx','gy'}, dimensions={0} | all-to-all | bytes 1048576 | tf_op jit(solution)/shard_map/all_to_all | solution.py:35
  204.8 3.4 gather_fusion.7
  208.2 8.6 %fusion.44 = f32[32,32,128]{2,1,0:T(8,128)S(1)} fusion(bf16[32,16,128,128]{2,3,1,0:T(8,128)(2,1)} %get-tuple-element.11, bf16[32,16,32,128]{3,2,1,0:T(8,128)(2,1)} %bitcast.143, pred[32,16]{1,0:T(8,128)(4,1)S(1)} %get-tuple-element.8, f32[32,128]{1,0:T(8,128)S(1)} %get-tuple-element.18), kind=kOutput, calls=%fused_computation.53 | convolution fusion | flops 539099136 | bytes 21512704 | tf_op jit(solution)/shard_map/bjrs,bjks->bkr/dot_general | solution.py:96
  216.8 1.2 broadcast_multiply_fusion
  218.0 0.1 copy.189
  218.1 0.7 gather_fusion.8
  218.8 0.1 broadcast_select_fusion.3
  218.9 18.3 %all_to_all.38 = bf16[32,2,32,128]{3,2,1,0:T(8,128)(2,1)S(1)} all-to-all(bf16[32,2,32,128]{3,2,1,0:T(8,128)(2,1)S(1)} %broadcast_select_fusion.3), channel_id=1, replica_groups=mesh['gx'=4,'gy'=8] {'gx','gy'}, dimensions={0} | all-to-all | bytes 1048576 | tf_op jit(solution)/shard_map/all_to_all | solution.py:35
  237.3 3.4 gather_fusion.9
  240.8 9.8 %fusion.59 = (f32[32,32,128]{2,1,0:T(8,128)S(1)}, f32[32,32,128]{2,1,0:T(8,128)}) fusion(f32[32,32,128]{2,0,1:T(8,128)} %get-tuple-element.6, bf16[32,16,128,128]{2,3,1,0:T(8,128)(2,1)} %get-tuple-element.11, bf16[32,16,32,128]{3,2,1,0:T(8,128)(2,1)} %bitcast.142, pred[32,16]{1,0:T(8,128)(4,1)S(1)} %get-tuple-element.8, f32[32,128]{1,0:T(8,128)S(1)} %get-tuple-element.18), kind=kOutput, calls=%fused_computation.84 | convolution fusion | flops 539361280 | bytes 22561280 | tf_op jit(solution)/shard_map/bjrs,bjks->bkr/dot_general | solution.py:96
  250.6 0.4 multiply_convert_fusion.1
  250.9 0.1 copy.197
  251.0 0.7 gather_fusion.10
  251.7 0.1 broadcast_select_fusion.2
  251.8 18.3 %all_to_all.39 = bf16[32,2,32,128]{3,2,1,0:T(8,128)(2,1)S(1)} all-to-all(bf16[32,2,32,128]{3,2,1,0:T(8,128)(2,1)S(1)} %broadcast_select_fusion.2), channel_id=1, replica_groups=mesh['gx'=4,'gy'=8] {'gx','gy'}, dimensions={0} | all-to-all | bytes 1048576 | tf_op jit(solution)/shard_map/all_to_all | solution.py:35
  270.3 3.4 gather_fusion.11
  273.7 8.6 %fusion.35 = f32[32,32,128]{2,1,0:T(8,128)S(1)} fusion(bf16[32,16,128,128]{2,3,1,0:T(8,128)(2,1)} %get-tuple-element.11, bf16[32,16,32,128]{3,2,1,0:T(8,128)(2,1)} %bitcast.141, pred[32,16]{1,0:T(8,128)(4,1)S(1)} %get-tuple-element.8), kind=kOutput, calls=%fused_computation.50 | convolution fusion | flops 538968064 | bytes 21496320 | tf_op jit(solution)/shard_map/bjrs,bjks->bkr/dot_general | solution.py:96
  282.3 0.8 copy-done.2
  283.1 0.8 multiply_convert_fusion
  283.8 0.1 copy.203
  283.9 0.7 gather_fusion.12
  284.6 0.1 broadcast_select_fusion.1
  284.8 18.3 %all_to_all.40 = bf16[32,2,32,128]{3,2,1,0:T(8,128)(2,1)S(1)} all-to-all(bf16[32,2,32,128]{3,2,1,0:T(8,128)(2,1)S(1)} %broadcast_select_fusion.1), channel_id=1, replica_groups=mesh['gx'=4,'gy'=8] {'gx','gy'}, dimensions={0} | all-to-all | bytes 1048576 | tf_op jit(solution)/shard_map/all_to_all | solution.py:35
  303.2 3.4 gather_fusion.13
  306.6 8.7 %fusion.38 = f32[32,32,128]{2,1,0:T(8,128)S(1)} fusion(bf16[32,16,128,128]{2,3,1,0:T(8,128)(2,1)} %get-tuple-element.11, bf16[32,16,32,128]{3,2,1,0:T(8,128)(2,1)} %bitcast.140, pred[32,16]{1,0:T(8,128)(4,1)S(1)} %get-tuple-element.8), kind=kOutput, calls=%fused_computation.51 | convolution fusion | flops 538968064 | bytes 21496320 | tf_op jit(solution)/shard_map/bjrs,bjks->bkr/dot_general | solution.py:96
  315.3 2.5 multiply_subtract_fusion
  317.8 0.4 fusion.57
  318.2 0.8 convolution_bitcast_fusion
  319.0 37.3 %psum.7 = f32[32,32]{0,1:T(8,128)S(1)} all-reduce(f32[32,32]{0,1:T(8,128)S(1)} %convolution_bitcast_fusion), channel_id=1, replica_groups=mesh['gx'=4,'gy'=8] {'gx','gy'}, use_global_device_ids=true, to_apply=%region_5.8 | all-reduce | flops 1024 | bytes 8192 | tf_op jit(solution)/shard_map/psum | solution.py:114
  356.4 2.9 cholesky.16
  359.3 0.6 compare_reduce_fusion
  360.0 1.3 select_bitcast_fusion
  361.2 2.4 custom-call.7
  363.7 4.3 %fusion.48 = f32[32,4096]{1,0:T(8,128)} fusion(f32[1,32,32]{1,2,0:T(8,128)S(1)} %custom-call.7, f32[32,32,128]{2,1,0:T(8,128)} %get-tuple-element.14, f32[32,32,128]{2,1,0:T(8,128)} %get-tuple-element.13, f32[32,32,128]{2,1,0:T(8,128)S(1)} %fusion.57, f32[32,32,128]{2,1,0:T(8,128)S(1)} %fusion.44, f32[32,32,128]{2,1,0:T(8,128)S(1)} %copy-done.4), kind=kOutput, calls=%fused_computation.63 | convolution fusion | flops 51773440 | bytes 3149824 | tf_op jit(solution)/shard_map/jit(_solve_triangular)/triangular_solve | solution.py:117
  (59 shorter events, 1.7 us)
Async XLA Ops:
  17.8 4.4 %copy-start.5 = (bf16[4096]{0:T(1024)(128)(2,1)S(1)}, bf16[4096]{0:T(1024)(128)(2,1)}, u32[]{:S(2)}) copy-start(bf16[4096]{0:T(1024)(128)(2,1)} %param.10) | copy-start | bytes 24580
  23.5 9.6 %all-to-all-start.2 = ((bf16[32,2,128]{2,1,0:T(2,128)(2,1)}), bf16[32,2,128]{2,1,0:T(2,128)(2,1)S(1)}, u32[]{:S(2)}, u32[]{:S(2)}) async-start(bf16[32,2,128]{2,1,0:T(2,128)(2,1)} %broadcast_select_fusion.6), calls=%async_computation.2 | async-start | bytes 32768 | tf_op jit(solution)/shard_map/all_to_all | solution.py:30
  30.6 6.1 %copy-start.8 = (s32[32,16]{0,1:T(8,128)S(1)}, s32[32,16]{0,1:T(8,128)}, u32[]{:S(2)}) copy-start(s32[32,16]{0,1:T(8,128)} %param.13) | copy-start | bytes 6148
  33.1 98.5 %all-to-all-start.1 = ((bf16[32,2,128,256]{3,2,1,0:T(8,128)(2,1)}), bf16[32,2,128,256]{3,2,1,0:T(8,128)(2,1)}, u32[]{:S(2)}, u32[]{:S(2)}) async-start(bf16[32,2,128,256]{3,2,1,0:T(8,128)(2,1)} %broadcast_select_fusion), calls=%async_computation.1 | async-start | bytes 8388608 | tf_op jit(solution)/shard_map/all_to_all | solution.py:29
  37.2 2.6 copy-start.7
  39.5 92.2 %copy-start.1 = (bf16[4096,256]{1,0:T(8,128)(2,1)S(1)}, bf16[4096,256]{1,0:T(8,128)(2,1)}, u32[]{:S(2)}) copy-start(bf16[4096,256]{1,0:T(8,128)(2,1)} %param.9) | copy-start | bytes 6291460
  135.5 6.4 %copy-start = (f32[96,128]{1,0:T(8,128)}, f32[96,128]{1,0:T(8,128)S(1)}, u32[]{:S(2)}) copy-start(f32[96,128]{1,0:T(8,128)S(1)} %fusion.10) | copy-start | bytes 147460
  142.1 18.9 %slice-start = ((f32[96,128]{1,0:T(8,128)}), f32[32,128]{1,0:T(8,128)S(1)}, s32[]{:S(2)}) async-start(f32[96,128]{1,0:T(8,128)} %copy-done), calls=%async_computation.7 | async-start | bytes 32768 | tf_op jit(solution)/shard_map/slice | solution.py:76
  282.3 0.8 copy-start.2
  306.6 8.7 %copy-start.3 = (f32[32,32,128]{2,1,0:T(8,128)S(1)}, f32[32,32,128]{2,1,0:T(8,128)}, u32[]{:S(2)}) copy-start(f32[32,32,128]{2,1,0:T(8,128)} %copy-done.2) | copy-start | bytes 1572868
  306.6 8.7 %copy-start.4 = (f32[32,32,128]{2,1,0:T(8,128)S(1)}, f32[32,32,128]{2,1,0:T(8,128)}, u32[]{:S(2)}) copy-start(f32[32,32,128]{2,1,0:T(8,128)} %get-tuple-element.15) | copy-start | bytes 1572868
  306.6 8.7 %copy-start.6 = (f32[32,32,128]{2,1,0:T(8,128)S(1)}, f32[32,32,128]{2,1,0:T(8,128)}, u32[]{:S(2)}) copy-start(f32[32,32,128]{2,1,0:T(8,128)} %get-tuple-element.20) | copy-start | bytes 1572868
where the time goes:
time: 369 us; the launch traced here: 368 us
  blocking collectives  125 us (34%)
  waiting for transfers between devices  92.5 us (25%)
  matrix products  64.4 us (17%)
  local copies, waits for them, and re-layouts  49.1 us (13%)
  other arithmetic  30 us (8%)
  starting transfers between devices  6.11 us (2%)
    all_to_all x1, waiting for transfers between devices, move_features(): lax.all_to_all(send_coords, ('gx', 'gy'), split_axis=0, concat_axis=0, ti...  90 us
    all_to_all x4, blocking collectives, move_vectors(): lax.all_to_all(send_rows, ('gx', 'gy'), split_axis=0, concat_axis=0, tile...  73.2 us
    psum x1, blocking collectives, on_device(): gram = lax.psum(partial_gram, ('gx', 'gy')) / total_rows  37.3 us
    dot_general x4, matrix products, graph(): jnp.einsum('bjrs,bjks->bkr', tiles, slot_rows, preferred_element_type=jnp...  35.6 us
    dot_general x1, matrix products, on_device(): jnp.einsum('brf,bjsf->bjrs', feature_bands, slot_coords, preferred_elemen...  23.7 us
    gather x1, local copies, waits for them, and re-layouts, on_device(): slot_coords = jnp.take(table_coords, slot_pos, axis=0)  18.9 us
    all_to_all x1, blocking collectives, on_device(): lax.all_to_all(need_mine, ('gx', 'gy'), split_axis=0, concat_axis=0, tile...  14.3 us
    gather x4, local copies, waits for them, and re-layouts, graph(): slot_rows = jnp.take(table_rows, slot_pos, axis=0)  13.7 us
  transfers between devices with their start and end apart: 2, of which 2 were waited for; matrix products, arithmetic and copies ran while one was open for 3% of the time, Pallas kernels for 0%

commit v1 on v0

v1 whole, which is shorter than its diff:
```python
import functools
import math

import jax
import jax.numpy as jnp
from jax import lax
from jax.experimental import pallas as pl
from jax.experimental.pallas import tpu as pltpu
from jax.sharding import PartitionSpec as P

AXES = ("gx", "gy")
BAND = 128
MOST = 2
DEGREE = 4
GROUP = 8
STEP_BANDS = 4

LOW_EDGE = 0.2
HIGH_EDGE = 2.0

VMEM = pltpu.VMEM
SMEM = pltpu.SMEM


def chebyshev_terms():
    centre = 0.5 * (LOW_EDGE + HIGH_EDGE)
    halfwidth = 0.5 * (HIGH_EDGE - LOW_EDGE)
    anchor = -centre / halfwidth
    values = [1.0, anchor]
    for repeat in range(DEGREE - 1):
        values.append(2.0 * anchor * values[-1] - values[-2])
    return (centre, halfwidth, values)


def exchange(blocks):
    return lax.all_to_all(blocks, AXES, split_axis=0, concat_axis=0, tiled=True)


def whole(space=VMEM):
    return pl.BlockSpec(memory_space=space)


def tile_groups(work, count, rows, coords, wcol, pcol, rvec, tiles, deg, stage, sems):
    groups = (count[0] + GROUP - 1) // GROUP

    def copies(group, slot):
        return [
            pltpu.make_async_copy(
                stage.at[slot, u], tiles.at[work[0, group * GROUP + u]], sems.at[slot, u]
            )
            for u in range(GROUP)
        ]

    def body(group, carry):
        slot = lax.rem(group, 2)

        @pl.when(group >= 2)
        def _():
            for copy in copies(group - 2, slot):
                copy.wait()

        for u in range(GROUP):
            at = group * GROUP + u
            band = work[1, at]
            entry = work[2, at]
            keep = work[3, at].astype(jnp.float32)
            inner = lax.dot_general(
                coords[entry], rows[band], (((1,), (1,)), ((), ())),
                preferred_element_type=jnp.float32,
            )
            half_sq = rvec[band, 0:1, :]
            row_width = rvec[band, 1:2, :]
            power = ((inner - half_sq) * wcol[entry] - pcol[entry]) * row_width
            weights = jnp.exp2(power) * keep
            stage[slot, u] = weights.astype(jnp.bfloat16)
            deg[band] += jnp.sum(weights.reshape(BAND // 8, 8, BAND), axis=0)
        for copy in copies(group, slot):
            copy.start()
        return carry

    lax.fori_loop(0, groups, body, 0)
    for back in (2, 1):
        @pl.when(groups >= back)
        def _():
            group = groups - back
            for copy in copies(group, lax.rem(group, 2)):
                copy.wait()


def local_kernel(work, count, rows, wcol, pcol, rvec, tiles, deg, stage, sems):
    deg[...] = jnp.zeros(deg.shape, deg.dtype)
    tile_groups(work, count, rows, rows, wcol, pcol, rvec, tiles, deg, stage, sems)


def pack_rows(send_index, scaled, send):
    def one(at, carry):
        send[at] = scaled[send_index[at]]
        return carry

    lax.fori_loop(0, send.shape[0], one, 0, unroll=8)


def remote_kernel(work, count, send_index, rows, coords, wcol, pcol, rvec, deg_in, start, tiles_in,
                  tiles, root, scaled, send, deg, stage, sems):
    deg[...] = deg_in[...]
    tile_groups(work, count, rows, coords, wcol, pcol, rvec, tiles, deg, stage, sems)
    for band in range(deg.shape[0]):
        total = jnp.sum(deg[band], axis=0, keepdims=True)
        inverse = 1.0 / jnp.sqrt(total)
        root[band : band + 1, :] = inverse
        block = start[:, band * BAND : (band + 1) * BAND]
        scaled[band] = (block * inverse).astype(jnp.bfloat16)
    pack_rows(send_index, scaled, send)


def round_kernel(first, last, gains, slots, send_index, slot_pos, scaled_in, got, tiles, root, cur, prev,
                 following, *rest):
    if last:
        gram, table = rest
    else:
        scaled, send, table = rest
    step = pl.program_id(0)
    bands = scaled_in.shape[0]

    @pl.when(step == 0)
    def _():
        table[0:bands] = scaled_in[...]
        table[bands:] = got[...]
        if last:
            gram[...] = jnp.zeros(gram.shape, gram.dtype)

    own, mixed_gain, old = gains
    for sub in range(STEP_BANDS):
        band = step * STEP_BANDS + sub
        lhs = jnp.concatenate([table[slot_pos[band * slots + j]] for j in range(slots)], axis=1)
        rhs = tiles[sub * slots : (sub + 1) * slots].reshape(slots * BAND, BAND)
        mixed = jnp.dot(lhs, rhs, preferred_element_type=jnp.float32)
        inverse = root[pl.ds(band, 1), :]
        lanes = slice(sub * BAND, (sub + 1) * BAND)
        block = own * cur[:, lanes] + (mixed_gain * inverse) * mixed
        if not first:
            block = block - old * prev[:, lanes]
        following[:, lanes] = block
        if not last:
            scaled[band] = (inverse * block).astype(jnp.bfloat16)
    if last:
        piece = following[...]
        gram[...] += lax.dot_general(
            piece, piece, (((1,), (1,)), ((), ())),
            precision=lax.Precision.HIGHEST, preferred_element_type=jnp.float32,
        )
    else:
        @pl.when(step == pl.num_programs(0) - 1)
        def _():
            pack_rows(send_index, scaled, send)


def finish_kernel(total_rows, parts, flat, basis, factor):
    vectors = flat.shape[0]
    gram = jnp.sum(parts[...], axis=0) / total_rows
    row_ids = lax.broadcasted_iota(jnp.int32, (vectors, vectors), 0)
    col_ids = lax.broadcasted_iota(jnp.int32, (vectors, vectors), 1)
    left = gram
    right = jnp.where(row_ids == col_ids, 1.0, 0.0).astype(jnp.float32)
    lower = jnp.zeros((vectors, vectors), jnp.float32)
    scale = jnp.zeros((vectors, 1), jnp.float32)
    rows = lax.broadcasted_iota(jnp.int32, (vectors, 1), 0)
    for j in range(vectors):
        pivot = left[j : j + 1, j : j + 1]
        inverse = 1.0 / pivot
        column = left[:, j : j + 1]
        ratio = jnp.where(rows > j, column * inverse, 0.0)
        spread = lax.rsqrt(pivot)
        spread = 1.0 / jnp.sqrt(pivot)
        scale = jnp.where(rows == j, spread, scale)
        lower = jnp.where((col_ids == j) & (row_ids >= j), column * spread, lower)
        left_row = left[j : j + 1, :]
        right_row = right[j : j + 1, :]
        left = left - ratio * left_row
        right = right - ratio * right_row
    factor[...] = lower
    basis[...] = jnp.dot(
        right * scale, flat[...], precision=lax.Precision.HIGHEST, preferred_element_type=jnp.float32
    )


def on_device(features, inv_width, start_block, neighbour_ids, slot_mask):
    bands, slots = neighbour_ids.shape
    dims = features.shape[1]
    vectors = start_block.shape[0]
    devices = lax.axis_size(AXES)
    device = lax.axis_index(AXES)
    entries = devices * MOST
    count_all = bands * slots
    listed = count_all + GROUP

    owner_dev = neighbour_ids // bands
    within = neighbour_ids % bands
    remote = (slot_mask == 1) & (owner_dev != device)
    flat_remote = remote.reshape(-1)
    all_bands = jnp.arange(devices * bands, dtype=jnp.int32)
    matches = (neighbour_ids.reshape(-1)[:, None] == all_bands[None, :]) & flat_remote[:, None]
    need_mine = jnp.any(matches, axis=0).astype(jnp.int32).reshape(devices, bands)
    wanted = exchange(need_mine)
    rank_send = jnp.cumsum(wanted, axis=1) - 1
    picks = (wanted[:, None, :] == 1) & (
        rank_send[:, None, :] == jnp.arange(MOST, dtype=jnp.int32)[None, :, None]
    )
    send_index = jnp.sum(
        picks.astype(jnp.int32) * jnp.arange(bands, dtype=jnp.int32)[None, None, :], axis=2
    ).reshape(-1)

    feature_bands = features.reshape(bands, BAND, dims)
    widths = inv_width.reshape(bands, BAND).astype(jnp.float32)
    squares = jnp.sum(jnp.square(feature_bands.astype(jnp.float32)), axis=2)
    sides = jnp.stack([widths, 0.5 * squares * widths], axis=1)
    got_sides = exchange(
        jnp.take(sides, send_index, axis=0, mode="clip").reshape(devices, MOST * 2, BAND)
    ).reshape(entries, 2, BAND)
    send_coords = jnp.take(feature_bands, send_index, axis=0, mode="clip")
    got_coords = exchange(send_coords.reshape(devices, MOST, BAND, dims)).reshape(entries, BAND, dims)

    rank_mine = jnp.cumsum(need_mine, axis=1) - 1
    rank_lookup = jnp.take(rank_mine.reshape(-1), neighbour_ids, axis=0, mode="clip")
    got_pos = owner_dev * MOST + rank_lookup
    slot_pos = jnp.where(remote, bands + got_pos, within).reshape(-1)
    entry_of = jnp.where(remote, got_pos, within).reshape(-1)
    mask_of = slot_mask.reshape(-1)

    where_at = jnp.arange(listed, dtype=jnp.int32)
    order = jnp.arange(count_all, dtype=jnp.int32)

    def work_list(chosen):
        count = jnp.sum(chosen.astype(jnp.int32))
        place = jnp.cumsum(chosen.astype(jnp.int32)) - 1
        hit = ((place[None, :] == where_at[:, None]) & chosen[None, :]).astype(jnp.int32)
        tile_id = jnp.sum(hit * order[None, :], axis=1)
        entry = jnp.sum(hit * entry_of[None, :], axis=1)
        keep = jnp.sum(hit * mask_of[None, :], axis=1)
        used = where_at < count
        target = jnp.where(used, tile_id, count_all + where_at % GROUP)
        return jnp.stack([target, tile_id // slots, entry, keep]), count.reshape(1)

    local_work, local_count = work_list(~flat_remote)
    remote_work, remote_count = work_list(flat_remote)

    rvec = jnp.stack([0.5 * squares, (2.0 * math.log2(math.e)) * widths], axis=1)

    def columns(rows):
        return jnp.broadcast_to(rows[:, :, None], rows.shape + (BAND,))

    tile_shape = jax.ShapeDtypeStruct((count_all + GROUP, BAND, BAND), jnp.bfloat16)
    stage = [
        pltpu.VMEM((2, GROUP, BAND, BAND), jnp.bfloat16),
        pltpu.SemaphoreType.DMA((2, GROUP)),
    ]
    build_flops = 2 * count_all * BAND * BAND * dims
    tiles, deg = pl.pallas_call(
        local_kernel,
        out_shape=(tile_shape, jax.ShapeDtypeStruct((bands, 8, BAND), jnp.float32)),
        in_specs=[whole(SMEM)] * 2 + [whole()] * 4,
        out_specs=(whole(pl.ANY), whole()),
        scratch_shapes=stage,
        cost_estimate=pl.CostEstimate(
            flops=build_flops, bytes_accessed=2 * count_all * BAND * BAND, transcendentals=count_all * BAND * BAND
        ),
        name="local_tiles",
    )(local_work, local_count, feature_bands, columns(sides[:, 0]), columns(sides[:, 1]), rvec)

    row_shape = jax.ShapeDtypeStruct((bands, vectors, BAND), jnp.bfloat16)
    send_shape = jax.ShapeDtypeStruct((entries, vectors, BAND), jnp.bfloat16)
    tiles, root, scaled, send = pl.pallas_call(
        remote_kernel,
        out_shape=(tile_shape, jax.ShapeDtypeStruct((bands, BAND), jnp.float32), row_shape, send_shape),
        in_specs=[whole(SMEM)] * 3 + [whole()] * 7 + [whole(pl.ANY)],
        out_specs=(whole(pl.ANY), whole(), whole(), whole()),
        scratch_shapes=[pltpu.VMEM((bands, 8, BAND), jnp.float32)] + stage,
        input_output_aliases={10: 0},
        cost_estimate=pl.CostEstimate(
            flops=build_flops // 2, bytes_accessed=count_all * BAND * BAND, transcendentals=count_all * BAND * BAND
        ),
        name="remote_tiles",
    )(remote_work, remote_count, send_index, feature_bands, got_coords, columns(got_sides[:, 0]),
      columns(got_sides[:, 1]), rvec, deg, start_block, tiles)

    centre, halfwidth, values = chebyshev_terms()
    flat_shape = jax.ShapeDtypeStruct((vectors, bands * BAND), jnp.float32)
    flat_spec = pl.BlockSpec((vectors, STEP_BANDS * BAND), lambda i: (0, i))
    fixed3 = lambda i: (0, 0, 0)
    previous, current = start_block, start_block
    for power in range(DEGREE):
        first, last = power == 0, power == DEGREE - 1
        if first:
            lead, old = 1.0 / values[1], 0.0
        else:
            lead = 2.0 * values[power] / values[power + 1]
            old = values[power - 1] / values[power + 1]
        gains = (lead * (1.0 - centre) / halfwidth, -lead / halfwidth, old)
        got = exchange(send.reshape(devices, MOST, vectors, BAND)).reshape(entries, vectors, BAND)
        if last:
            outs = (flat_shape, jax.ShapeDtypeStruct((vectors, vectors), jnp.float32))
            out_specs = (flat_spec, pl.BlockSpec((vectors, vectors), lambda i: (0, 0)))
        else:
            outs = (flat_shape, row_shape, send_shape)
            out_specs = (
                flat_spec,
                pl.BlockSpec(row_shape.shape, fixed3),
                pl.BlockSpec(send_shape.shape, fixed3),
            )
        results = pl.pallas_call(
            functools.partial(round_kernel, first, last, gains, slots),
            grid=(bands // STEP_BANDS,),
            out_shape=outs,
            in_specs=[
                whole(SMEM),
                whole(SMEM),
                pl.BlockSpec(row_shape.shape, fixed3),
                pl.BlockSpec(send_shape.shape, fixed3),
                pl.BlockSpec((STEP_BANDS * slots, BAND, BAND), lambda i: (i, 0, 0)),
                pl.BlockSpec((bands, BAND), lambda i: (0, 0)),
                flat_spec,
                flat_spec,
            ],
            out_specs=out_specs,
            scratch_shapes=[pltpu.VMEM((bands + entries, vectors, BAND), jnp.bfloat16)],
            cost_estimate=pl.CostEstimate(
                flops=2 * count_all * BAND * BAND * vectors,
                bytes_accessed=2 * count_all * BAND * BAND,
                transcendentals=0,
            ),
            name="round" + str(power),
        )(send_index, slot_pos, scaled, got, tiles, root, current, previous)
        previous, current = current, results[0]
        if last:
            partial_gram = results[1]
        else:
            scaled, send = results[1], results[2]

    parts = exchange(jnp.broadcast_to(partial_gram[None], (devices, vectors, vectors)))
    basis, factor = pl.pallas_call(
        functools.partial(finish_kernel, devices * bands * BAND),
        out_shape=(flat_shape, jax.ShapeDtypeStruct((vectors, vectors), jnp.float32)),
        in_specs=[whole()] * 2,
        out_specs=(whole(), whole()),
        name="finish",
    )(parts, current)
    return (basis, factor)


def solution(mesh):
    placed = (P(AXES, None), P(AXES), P(None, AXES), P(AXES, None), P(AXES, None))
    return jax.shard_map(
        on_device,
        mesh=mesh,
        in_specs=placed,
        out_specs=(P(None, AXES), P()),
        check_vma=False,
    )
```

time: 369 us -> 297 us (0.80)
  Pallas kernels: 0 us -> 94.3 us
  matrix products: 64.4 us -> 0 us
  blocking collectives: 125 us -> 68.8 us
  local copies, waits for them, and re-layouts: 49.1 us -> 23.1 us
  other arithmetic: 30 us -> 10.7 us
  starting transfers between devices: 6.11 us -> 17.2 us
  waiting for transfers between devices: 92.5 us -> 81.7 us
    pallas_call x0 -> x7, Pallas kernels: none -> 94.3 us  [the longest x4 44 us: on_device(): pl.pallas_call(functools.partial(round_kernel, first, last, gains, slots)...]
    dot_general x6 -> x0, matrix products: 60.1 us -> none  [the longest x4 35.6 us: graph(): jnp.einsum('bjrs,bjks->bkr', tiles, slot_rows, preferred_element_type=jnp...]
    gather x15 -> x4, local copies, waits for them, and re-layouts: 45 us -> 6.42 us  [the longest x1 2.78 us: on_device(): send_coords = jnp.take(feature_bands, send_index, axis=0, mode='clip')]
    psum x1 -> x0, blocking collectives: 37.3 us -> none  [on_device(): gram = lax.psum(partial_gram, ('gx', 'gy')) / total_rows]
    all_to_all x5 -> x4, blocking collectives: 87.5 us -> 68.8 us  [exchange(): return lax.all_to_all(blocks, AXES, split_axis=0, concat_axis=0, tiled=True)]
    all_to_all x2 -> x4, starting transfers between devices: 6.11 us -> 17.2 us  [exchange(): return lax.all_to_all(blocks, AXES, split_axis=0, concat_axis=0, tiled=True)]
    all_to_all x2 -> x4, waiting for transfers between devices: 92.5 us -> 81.7 us  [exchange(): return lax.all_to_all(blocks, AXES, split_axis=0, concat_axis=0, tiled=True)]
    broadcast_in_dim x3 -> x5, local copies, waits for them, and re-layouts: 0.26 us -> 9.81 us  [the longest x4 9.04 us: columns(): return jnp.broadcast_to(rows[:, :, None], rows.shape + (BAND,))]
  transfers between devices with their start and end apart: 2 -> 4, of which waited for: 2 -> 4; matrix products, arithmetic and copies ran while one was open for 3% -> 7% of each run, Pallas kernels for 0% -> 8%
where the time goes in v1:
time: 297 us
  Pallas kernels  94.3 us (32%)
  waiting for transfers between devices  81.7 us (28%)
  blocking collectives  68.8 us (23%)
  local copies, waits for them, and re-layouts  23.1 us (8%)
  starting transfers between devices  17.2 us (6%)
  other arithmetic  10.7 us (4%)
    all_to_all x4, waiting for transfers between devices, exchange(): return lax.all_to_all(blocks, AXES, split_axis=0, concat_axis=0, tiled=True)  81.7 us
    all_to_all x4, blocking collectives, exchange(): return lax.all_to_all(blocks, AXES, split_axis=0, concat_axis=0, tiled=True)  68.8 us
    pallas_call x4, Pallas kernels, on_device(): pl.pallas_call(functools.partial(round_kernel, first, last, gains, slots)...  44 us
    pallas_call x1, Pallas kernels, on_device(): pl.pallas_call(local_kernel, out_shape=(tile_shape, jax.ShapeDtypeStruct(...  24.2 us
    pallas_call x1, Pallas kernels, on_device(): pl.pallas_call(remote_kernel, out_shape=(tile_shape, jax.ShapeDtypeStruct...  20.9 us
    all_to_all x4, starting transfers between devices, exchange(): return lax.all_to_all(blocks, AXES, split_axis=0, concat_axis=0, tiled=True)  17.2 us
    broadcast_in_dim x4, local copies, waits for them, and re-layouts, columns(): return jnp.broadcast_to(rows[:, :, None], rows.shape + (BAND,))  9.04 us
  transfers between devices with their start and end apart: 4, of which 4 were waited for; matrix products, arithmetic and copies ran while one was open for 7% of the time, Pallas kernels for 8%

profile of v1, /device:TPU:0, one launch (start us, length us, event | category | flops | bytes accessed | tf_op | source)
XLA Modules:
  0.0 296.8 jit_solution(3602940521526103420)
XLA Ops:
  0.6 0.9 copy.38
  1.6 0.1 eq.73
  1.6 0.8 copy.39
  2.4 0.1 and.118
  2.5 0.4 fusion.1
  2.9 0.7 reshape.389
  3.6 7.3 %all-to-all-start = ((s32[32,1,32]{2,1,0:T(1,128)}), s32[32,1,32]{2,1,0:T(1,128)S(1)}, u32[]{:S(2)}, u32[]{:S(2)}) async-start(s32[32,1,32]{2,1,0:T(1,128)} %reshape.389), calls=%async_computation | async-start | bytes 32768 | tf_op jit(solution)/shard_map/all_to_all | solution.py:36
  10.9 0.7 convert_bitcast_fusion
  11.6 2.2 multiply_reduce_fusion
  13.9 4.1 %all-to-all-done = s32[32,1,32]{2,1,0:T(1,128)S(1)} async-done(((s32[32,1,32]{2,1,0:T(1,128)}), s32[32,1,32]{2,1,0:T(1,128)S(1)}, u32[]{:S(2)}, u32[]{:S(2)}) %all-to-all-start) | async-done | bytes 4128 | tf_op jit(solution)/shard_map/all_to_all | solution.py:36
  18.0 0.2 reduce_window_sum.49
  18.2 0.1 select_reduce_fusion.6
  18.3 0.1 copy.45
  18.4 0.1 reshape.370.send_index
  18.6 1.3 gather_fusion.2
  19.8 2.6 all-to-all-start.2
  22.4 2.8 gather_fusion.1
  25.2 4.6 %all-to-all-done.2 = f32[32,4,128]{2,1,0:T(4,128)S(1)} async-done(((f32[32,4,128]{2,1,0:T(4,128)}), f32[32,4,128]{2,1,0:T(4,128)S(1)}, u32[]{:S(2)}, u32[]{:S(2)}) %all-to-all-start.2) | async-done | bytes 65568 | tf_op jit(solution)/shard_map/all_to_all | solution.py:36
  29.8 3.6 %all-to-all-start.1 = ((bf16[32,2,128,256]{3,2,1,0:T(8,128)(2,1)}), bf16[32,2,128,256]{3,2,1,0:T(8,128)(2,1)}, u32[]{:S(2)}, u32[]{:S(2)}) async-start(bf16[32,2,128,256]{3,2,1,0:T(8,128)(2,1)} %bitcast.40), calls=%async_computation.1 | async-start | bytes 8388608 | tf_op jit(solution)/shard_map/all_to_all | solution.py:36
  33.5 0.1 mul.129
  33.6 0.2 reduce_window_sum.50
  33.8 0.1 sub.37
  33.9 2.3 gather_fusion
  36.2 0.1 reshape.396
  36.2 0.1 reshape.393
  36.3 0.3 reduce-window.24
  36.6 0.1 slice.24
  36.7 0.7 fusion.8
  37.4 0.1 mul.126
  37.5 0.1 reshape.391
  37.5 0.3 reduce-window.16
  37.9 0.1 slice.20
  38.0 0.1 slice_reduce_fusion
  38.1 0.1 slice_reduce_fusion.1
  38.3 1.3 select_reduce_fusion.2
  39.6 1.2 compare_select_fusion
  40.9 0.6 pad_add_fusion.work
  41.5 0.6 pad_add_fusion.1.work
  42.1 0.6 pad_maximum_fusion.1.rvec
  42.8 2.0 broadcast_in_dim.30.wcol
  44.7 1.9 broadcast_in_dim.31.pcol
  46.7 24.2 %local_tiles.1 = (bf16[520,128,128]{2,1,0:T(8,128)(2,1)}, f32[32,8,128]{2,1,0:T(8,128)}) custom-call(s32[4,520]{1,0:T(4,128)} %pad_add_fusion.1.work, s32[1]{0:T(128)} %bitcast.15.count, bf16[32,128,256]{2,1,0:T(8,128)(2,1)} %bitcast.37, f32[32,128,128]{2,1,0:T(8,128)} %broadcast_in_dim.30.wcol, f32[32,128,128]{2,1,0:T(8,128)} %broadcast_in_dim.31.pcol, ...), custom_call_target="tpu_custom_call" | custom-call | flops 4294967296 | bytes 16777216 | tf_op jit(solution)/shard_map/local_tiles/pallas_call | solution.py:258
  70.9 57.5 %all-to-all-done.1 = bf16[32,2,128,256]{3,2,1,0:T(8,128)(2,1)} async-done(((bf16[32,2,128,256]{3,2,1,0:T(8,128)(2,1)}), bf16[32,2,128,256]{3,2,1,0:T(8,128)(2,1)}, u32[]{:S(2)}, u32[]{:S(2)}) %all-to-all-start.1) | async-done | bytes 4194336 | tf_op jit(solution)/shard_map/all_to_all | solution.py:36
  128.4 2.6 broadcast_in_dim.27.wcol
  130.9 2.6 broadcast_in_dim.29.pcol
  133.5 20.9 %remote_tiles.1 = (bf16[520,128,128]{2,1,0:T(8,128)(2,1)}, f32[32,128]{1,0:T(8,128)}, bf16[32,32,128]{2,1,0:T(8,128)(2,1)}, bf16[64,32,128]{2,1,0:T(8,128)(2,1)}) custom-call(s32[4,520]{1,0:T(4,128)} %pad_add_fusion.work, s32[1]{0:T(128)} %bitcast.4.count, s32[64]{0:T(128)} %copy-done.3, ...), custom_call_target="tpu_custom_call", output_to_operand_aliasing={{0}: (10, {})} | custom-call | flops 2147483648 | bytes 8388608 | tf_op jit(solution)/shard_map/remote_tiles/pallas_call | solution.py:272
  154.4 3.7 %all-to-all-start.3 = ((bf16[32,2,32,128]{3,2,1,0:T(8,128)(2,1)}), bf16[32,2,32,128]{3,2,1,0:T(8,128)(2,1)S(1)}, u32[]{:S(2)}, u32[]{:S(2)}) async-start(bf16[32,2,32,128]{3,2,1,0:T(8,128)(2,1)} %bitcast.45), calls=%async_computation.3 | async-start | bytes 1048576 | tf_op jit(solution)/shard_map/all_to_all | solution.py:36
  158.1 0.7 reshape.371.slot_pos
  158.8 15.6 %all-to-all-done.3 = bf16[32,2,32,128]{3,2,1,0:T(8,128)(2,1)S(1)} async-done(((bf16[32,2,32,128]{3,2,1,0:T(8,128)(2,1)}), bf16[32,2,32,128]{3,2,1,0:T(8,128)(2,1)S(1)}, u32[]{:S(2)}, u32[]{:S(2)}) %all-to-all-start.3) | async-done | bytes 524320 | tf_op jit(solution)/shard_map/all_to_all | solution.py:36
  174.4 0.8 copy-done.1
  175.2 10.9 %round0.1 = (f32[32,4096]{1,0:T(8,128)}, bf16[32,32,128]{2,1,0:T(8,128)(2,1)}, bf16[64,32,128]{2,1,0:T(8,128)(2,1)}) custom-call(s32[64]{0:T(128)} %copy-done.3, s32[512]{0:T(512)} %reshape.371.slot_pos, bf16[32,32,128]{2,1,0:T(8,128)(2,1)} %get-tuple-element.21.scaled_in, bf16[64,32,128]{2,1,0:T(8,128)(2,1)} %bitcast.41, ...), custom_call_target="tpu_custom_call" | custom-call | flops 536870912 | bytes 16777216 | tf_op jit(solution)/shard_map/round0/pallas_call | solution.py:310
  186.1 19.6 %all_to_all.41 = bf16[32,2,32,128]{3,2,1,0:T(8,128)(2,1)} all-to-all(bf16[32,2,32,128]{3,2,1,0:T(8,128)(2,1)} %bitcast.47), channel_id=1, replica_groups=mesh['gx'=4,'gy'=8] {'gx','gy'}, dimensions={0} | all-to-all | bytes 1048576 | tf_op jit(solution)/shard_map/all_to_all | solution.py:36
  205.6 10.9 %round1.1 = (f32[32,4096]{1,0:T(8,128)}, bf16[32,32,128]{2,1,0:T(8,128)(2,1)}, bf16[64,32,128]{2,1,0:T(8,128)(2,1)}) custom-call(s32[64]{0:T(128)} %copy-done.3, s32[512]{0:T(512)} %reshape.371.slot_pos, bf16[32,32,128]{2,1,0:T(8,128)(2,1)} %get-tuple-element.25.scaled_in, bf16[64,32,128]{2,1,0:T(8,128)(2,1)} %bitcast.44, ...), custom_call_target="tpu_custom_call" | custom-call | flops 536870912 | bytes 16777216 | tf_op jit(solution)/shard_map/round1/pallas_call | solution.py:310
  216.6 19.6 %all_to_all.42 = bf16[32,2,32,128]{3,2,1,0:T(8,128)(2,1)} all-to-all(bf16[32,2,32,128]{3,2,1,0:T(8,128)(2,1)} %bitcast.48), channel_id=1, replica_groups=mesh['gx'=4,'gy'=8] {'gx','gy'}, dimensions={0} | all-to-all | bytes 1048576 | tf_op jit(solution)/shard_map/all_to_all | solution.py:36
  236.1 11.0 %round2.1 = (f32[32,4096]{1,0:T(8,128)}, bf16[32,32,128]{2,1,0:T(8,128)(2,1)}, bf16[64,32,128]{2,1,0:T(8,128)(2,1)}) custom-call(s32[64]{0:T(128)} %copy-done.3, s32[512]{0:T(512)} %reshape.371.slot_pos, bf16[32,32,128]{2,1,0:T(8,128)(2,1)} %get-tuple-element.28.scaled_in, bf16[64,32,128]{2,1,0:T(8,128)(2,1)} %bitcast.43, ...), custom_call_target="tpu_custom_call" | custom-call | flops 536870912 | bytes 16777216 | tf_op jit(solution)/shard_map/round2/pallas_call | solution.py:310
  247.1 19.5 %all_to_all.43 = bf16[32,2,32,128]{3,2,1,0:T(8,128)(2,1)} all-to-all(bf16[32,2,32,128]{3,2,1,0:T(8,128)(2,1)} %bitcast.46), channel_id=1, replica_groups=mesh['gx'=4,'gy'=8] {'gx','gy'}, dimensions={0} | all-to-all | bytes 1048576 | tf_op jit(solution)/shard_map/all_to_all | solution.py:36
  266.6 11.1 %round3.1 = (f32[32,4096]{1,0:T(8,128)}, f32[32,32]{1,0:T(8,128)}) custom-call(s32[64]{0:T(128)} %copy-done.3, s32[512]{0:T(512)} %reshape.371.slot_pos, bf16[32,32,128]{2,1,0:T(8,128)(2,1)} %get-tuple-element.31.scaled_in, bf16[64,32,128]{2,1,0:T(8,128)(2,1)} %bitcast.42, bf16[520,128,128]{2,1,0:T(8,128)(2,1)} %get-tuple-element.23.tiles, ...), custom_call_target="tpu_custom_call" | custom-call | flops 536870912 | bytes 16777216 | tf_op jit(solution)/shard_map/round3/pallas_call | solution.py:310
  277.8 0.8 broadcast_in_dim.32
  278.5 0.3 reshape.425
  278.8 10.2 %all_to_all.44 = f32[32,1,1024]{2,1,0:T(1,128)S(1)} all-to-all(f32[32,1,1024]{2,1,0:T(1,128)S(1)} %reshape.425), channel_id=1, replica_groups=mesh['gx'=4,'gy'=8] {'gx','gy'}, dimensions={0} | all-to-all | bytes 262144 | tf_op jit(solution)/shard_map/all_to_all | solution.py:36
  289.0 0.5 broadcast.335
  289.5 0.9 reduce.7
  290.5 1.0 reshape.426.parts
  291.4 5.3 %finish.1 = (f32[32,4096]{1,0:T(8,128)}, f32[32,32]{1,0:T(8,128)}) custom-call(f32[32,32,32]{2,1,0:T(8,128)} %reshape.426.parts, f32[32,4096]{1,0:T(8,128)} %get-tuple-element.35.flat), custom_call_target="tpu_custom_call" | custom-call | tf_op jit(solution)/shard_map/finish/pallas_call | solution.py:340
  (30 shorter events, 0.5 us)
Async XLA Ops:
  0.6 21.8 %copy-start = (bf16[4096,256]{1,0:T(8,128)(2,1)S(1)}, bf16[4096,256]{1,0:T(8,128)(2,1)}, u32[]{:S(2)}) copy-start(bf16[4096,256]{1,0:T(8,128)(2,1)} %param.5) | copy-start | bytes 6291460
  3.6 14.4 %all-to-all-start = ((s32[32,1,32]{2,1,0:T(1,128)}), s32[32,1,32]{2,1,0:T(1,128)S(1)}, u32[]{:S(2)}, u32[]{:S(2)}) async-start(s32[32,1,32]{2,1,0:T(1,128)} %reshape.389), calls=%async_computation | async-start | bytes 32768 | tf_op jit(solution)/shard_map/all_to_all | solution.py:36
  18.5 6.7 %copy-start.3 = (s32[64]{0:T(128)}, s32[64]{0:T(128)S(1)}, u32[]{:S(2)}) copy-start(s32[64]{0:T(128)S(1)} %reshape.370.send_index) | copy-start | bytes 772
  19.8 10.0 %all-to-all-start.2 = ((f32[32,4,128]{2,1,0:T(4,128)}), f32[32,4,128]{2,1,0:T(4,128)S(1)}, u32[]{:S(2)}, u32[]{:S(2)}) async-start(f32[32,4,128]{2,1,0:T(4,128)} %bitcast.10), calls=%async_computation.2 | async-start | bytes 131072 | tf_op jit(solution)/shard_map/all_to_all | solution.py:36
  29.8 98.5 %all-to-all-start.1 = ((bf16[32,2,128,256]{3,2,1,0:T(8,128)(2,1)}), bf16[32,2,128,256]{3,2,1,0:T(8,128)(2,1)}, u32[]{:S(2)}, u32[]{:S(2)}) async-start(bf16[32,2,128,256]{3,2,1,0:T(8,128)(2,1)} %bitcast.40), calls=%async_computation.1 | async-start | bytes 8388608 | tf_op jit(solution)/shard_map/all_to_all | solution.py:36
  33.8 8.9 %copy-start.2 = (bf16[4096]{0:T(1024)(128)(2,1)S(1)}, bf16[4096]{0:T(1024)(128)(2,1)}, u32[]{:S(2)}) copy-start(bf16[4096]{0:T(1024)(128)(2,1)} %param.6) | copy-start | bytes 24580
  154.4 20.0 %all-to-all-start.3 = ((bf16[32,2,32,128]{3,2,1,0:T(8,128)(2,1)}), bf16[32,2,32,128]{3,2,1,0:T(8,128)(2,1)S(1)}, u32[]{:S(2)}, u32[]{:S(2)}) async-start(bf16[32,2,32,128]{3,2,1,0:T(8,128)(2,1)} %bitcast.45), calls=%async_computation.3 | async-start | bytes 1048576 | tf_op jit(solution)/shard_map/all_to_all | solution.py:36
  174.4 0.8 copy-start.1

commit v2 on v1

v2 whole, which is shorter than its diff:
```python
import functools
import math

import jax
import jax.numpy as jnp
from jax import lax
from jax.experimental import pallas as pl
from jax.experimental.pallas import tpu as pltpu
from jax.sharding import PartitionSpec as P

AXES = ("gx", "gy")
BAND = 128
MOST = 2
DEGREE = 4
GROUP = 16
STAGES = 4
EXTRA = 8

LOW_EDGE = 0.2
HIGH_EDGE = 2.0

VMEM = pltpu.VMEM
SMEM = pltpu.SMEM


def chebyshev_terms():
    centre = 0.5 * (LOW_EDGE + HIGH_EDGE)
    halfwidth = 0.5 * (HIGH_EDGE - LOW_EDGE)
    anchor = -centre / halfwidth
    values = [1.0, anchor]
    for repeat in range(DEGREE - 1):
        values.append(2.0 * anchor * values[-1] - values[-2])
    return (centre, halfwidth, values)


def exchange(blocks):
    return lax.all_to_all(blocks, AXES, split_axis=0, concat_axis=0, tiled=True)


def whole(space=VMEM):
    return pl.BlockSpec(memory_space=space)


def need_kernel(ids, mask, need):
    slots, bands = ids.shape
    devices = need.shape[0]
    device_ids = lax.broadcasted_iota(jnp.int32, (devices, bands), 0)
    band_ids = lax.broadcasted_iota(jnp.int32, (bands, bands), 0)
    owners, withins = [], []
    for j in range(slots):
        row = ids[j : j + 1, :]
        keep = mask[j : j + 1, :] == 1
        owners.append(jnp.where((row // bands == device_ids) & keep, 1.0, 0.0))
        withins.append(jnp.where(row % bands == band_ids, 1.0, 0.0))
    count = lax.dot_general(
        jnp.concatenate(owners, axis=1).astype(jnp.bfloat16),
        jnp.concatenate(withins, axis=1).astype(jnp.bfloat16),
        (((1,), (1,)), ((), ())),
        preferred_element_type=jnp.float32,
    )
    need[...] = jnp.where(count > 0.0, 1, 0).astype(jnp.int32)


def pack_kernel(send_index, features, sides, send, tails, sems):
    devices = send.shape[0]

    def bands_of(d):
        return [
            pltpu.make_async_copy(
                features.at[send_index[d * MOST + h]],
                send.at[d, pl.ds(h * BAND, BAND)],
                sems.at[h, d],
            )
            for h in range(MOST)
        ]

    def tail_of(d):
        return pltpu.make_async_copy(
            tails.at[d], send.at[d, pl.ds(MOST * BAND, EXTRA)], sems.at[MOST, d]
        )

    def first(d, carry):
        for copy in bands_of(d):
            copy.start()
        tails[d] = jnp.concatenate([sides[send_index[d * MOST + h]] for h in range(MOST)], axis=1)
        return carry

    def second(d, carry):
        tail_of(d).start()
        return carry

    def third(d, carry):
        for copy in bands_of(d):
            copy.wait()
        tail_of(d).wait()
        return carry

    lax.fori_loop(0, devices, first, 0)
    lax.fori_loop(0, devices, second, 0)
    lax.fori_loop(0, devices, third, 0)


def spread_column(side):
    row = lax.broadcasted_iota(jnp.int32, (EXTRA, 2 * BAND), 0)
    lane = lax.broadcasted_iota(jnp.int32, (EXTRA, 2 * BAND), 1)
    left = jnp.where((row == 0) & (lane < BAND), 1.0, 0.0)
    right = jnp.where((row > 0) & (row < 4) & (lane >= BAND), 1.0, 0.0)
    return lax.dot_general(
        side, (left + right).astype(jnp.bfloat16), (((0,), (0,)), ((), ())),
        preferred_element_type=jnp.float32,
    )


def tile_groups(work, count, rows, coords_of, cols, rvec, tiles, deg, stage, sems):
    groups = (count[0] + GROUP - 1) // GROUP

    def copy_of(group):
        slot = lax.rem(group, STAGES)
        return pltpu.make_async_copy(
            stage.at[slot], tiles.at[pl.ds(group * GROUP, GROUP)], sems.at[slot]
        )

    def body(group, carry):
        slot = lax.rem(group, STAGES)

        @pl.when(group >= STAGES)
        def _():
            copy_of(group - STAGES).wait()

        for u in range(GROUP):
            at = group * GROUP + u
            band = work[0, at]
            entry = work[1, at]
            keep = work[2, at].astype(jnp.float32)
            inner = lax.dot_general(
                coords_of(entry), rows[band], (((1,), (1,)), ((), ())),
                preferred_element_type=jnp.float32,
            )
            half_sq = rvec[band, 0:1, :]
            row_width = rvec[band, 1:2, :]
            power = ((inner - half_sq) * cols[entry, :, 0:BAND] - cols[entry, :, BAND:]) * row_width
            weights = jnp.exp2(power) * keep
            stage[slot, u] = weights.astype(jnp.bfloat16)
            deg[band] += jnp.sum(weights.reshape(BAND // 8, 8, BAND), axis=0)
        copy_of(group).start()
        return carry

    lax.fori_loop(0, groups, body, 0)
    for back in range(STAGES, 0, -1):
        @pl.when(groups >= back)
        def _():
            copy_of(groups - back).wait()


def local_kernel(work, count, rows, sides, rvec, tiles, deg, cols, stage, sems):
    deg[...] = jnp.zeros(deg.shape, deg.dtype)

    def fill(band, carry):
        cols[band] = spread_column(sides[band])
        return carry

    lax.fori_loop(0, rows.shape[0], fill, 0, unroll=4)
    tile_groups(work, count, rows, lambda entry: rows[entry], cols, rvec, tiles, deg, stage, sems)


def pack_rows(send_index, scaled, send):
    def one(at, carry):
        send[at] = scaled[send_index[at]]
        return carry

    lax.fori_loop(0, send.shape[0], one, 0, unroll=8)


def remote_kernel(work, count, send_index, rows, got, rvec, deg_in, start,
                  tiles, root, scaled, send, deg, cols, stage, sems):
    deg[...] = deg_in[...]
    tail = MOST * BAND

    def fill(owner, carry):
        for h in range(MOST):
            side = got[owner, tail : tail + EXTRA, h * BAND : (h + 1) * BAND]
            cols[owner * MOST + h] = spread_column(side)
        return carry

    lax.fori_loop(0, got.shape[0], fill, 0, unroll=4)

    def coords_of(entry):
        at = pl.multiple_of(lax.rem(entry, MOST) * BAND, BAND)
        return got[entry // MOST, pl.ds(at, BAND), :]

    tile_groups(work, count, rows, coords_of, cols, rvec, tiles, deg, stage, sems)
    for band in range(deg.shape[0]):
        total = jnp.sum(deg[band], axis=0, keepdims=True)
        inverse = 1.0 / jnp.sqrt(total)
        root[band : band + 1, :] = inverse
        block = start[:, band * BAND : (band + 1) * BAND]
        scaled[band] = (block * inverse).astype(jnp.bfloat16)
    pack_rows(send_index, scaled, send)


def gather_product(work, count, table, tiles, total, held, sems):
    groups = (count[0] + GROUP - 1) // GROUP

    def copy_of(group):
        part = pl.ds(group * GROUP, GROUP)
        return pltpu.make_async_copy(tiles.at[part], held.at[part], sems.at[group])

    def begin(group, carry):
        copy_of(group).start()
        return carry

    def body(group, carry):
        copy_of(group).wait()
        for u in range(GROUP):
            at = group * GROUP + u
            total[work[0, at]] += jnp.dot(
                table[work[1, at]], held[at], preferred_element_type=jnp.float32
            )
        return carry

    lax.fori_loop(0, groups, begin, 0)
    lax.fori_loop(0, groups, body, 0)


def own_kernel(work, count, scaled, tiles, total, held, sems):
    total[...] = jnp.zeros(total.shape, total.dtype)
    gather_product(work, count, scaled, tiles, total, held, sems)


def fold(square):
    return jnp.concatenate([square[8 * q : 8 * q + 8, :] for q in range(square.shape[0] // 8)], axis=1)


def unfold(packed, side):
    return jnp.concatenate([packed[:, side * q : side * (q + 1)] for q in range(side // 8)], axis=0)


def round_kernel(first, last, gains, work, count, send_index, got, total_in, root, cur, prev, tiles,
                 following, *rest):
    if last:
        gram, total, held, sems = rest
    else:
        scaled, send, total, held, sems = rest
    total[...] = total_in[...]
    gather_product(work, count, got, tiles, total, held, sems)
    own, mixed_gain, old = gains
    for band in range(total.shape[0]):
        inverse = root[band : band + 1, :]
        lanes = slice(band * BAND, (band + 1) * BAND)
        block = own * cur[:, lanes] + (mixed_gain * inverse) * total[band]
        if not first:
            block = block - old * prev[:, lanes]
        following[:, lanes] = block
        if not last:
            scaled[band] = (inverse * block).astype(jnp.bfloat16)
    if last:
        piece = following[...]
        square = lax.dot_general(
            piece, piece, (((1,), (1,)), ((), ())),
            precision=lax.Precision.HIGHEST, preferred_element_type=jnp.float32,
        )
        gram[...] = jnp.broadcast_to(fold(square)[None], gram.shape)
    else:
        pack_rows(send_index, scaled, send)


def finish_kernel(total_rows, parts, flat, basis, factor):
    vectors = flat.shape[0]
    gram = unfold(jnp.sum(parts[...], axis=0), vectors) / total_rows
    row_ids = lax.broadcasted_iota(jnp.int32, (vectors, vectors), 0)
    col_ids = lax.broadcasted_iota(jnp.int32, (vectors, vectors), 1)
    left = gram
    right = jnp.where(row_ids == col_ids, 1.0, 0.0).astype(jnp.float32)
    lower = jnp.zeros((vectors, vectors), jnp.float32)
    scale = jnp.zeros((vectors, 1), jnp.float32)
    rows = lax.broadcasted_iota(jnp.int32, (vectors, 1), 0)
    for j in range(vectors):
        pivot = left[j : j + 1, j : j + 1]
        inverse = 1.0 / pivot
        column = left[:, j : j + 1]
        ratio = jnp.where(rows > j, column * inverse, 0.0)
        spread = 1.0 / jnp.sqrt(pivot)
        scale = jnp.where(rows == j, spread, scale)
        lower = jnp.where((col_ids == j) & (row_ids >= j), column * spread, lower)
        left_row = left[j : j + 1, :]
        right_row = right[j : j + 1, :]
        left = left - ratio * left_row
        right = right - ratio * right_row
    factor[...] = lower
    basis[...] = jnp.dot(
        right * scale, flat[...], precision=lax.Precision.HIGHEST, preferred_element_type=jnp.float32
    )


def on_device(features, inv_width, start_block, neighbour_ids, slot_mask):
    bands, slots = neighbour_ids.shape
    dims = features.shape[1]
    vectors = start_block.shape[0]
    devices = lax.axis_size(AXES)
    device = lax.axis_index(AXES)
    entries = devices * MOST
    count_all = bands * slots

    ids = neighbour_ids.T
    mask = slot_mask.T
    need_mine = pl.pallas_call(
        need_kernel,
        out_shape=jax.ShapeDtypeStruct((devices, bands), jnp.int32),
        in_specs=[whole()] * 2,
        out_specs=whole(),
        name="need",
    )(ids, mask)
    wanted = exchange(need_mine)
    rank_send = jnp.cumsum(wanted, axis=1) - 1
    picks = (wanted[:, None, :] == 1) & (
        rank_send[:, None, :] == jnp.arange(MOST, dtype=jnp.int32)[None, :, None]
    )
    send_index = jnp.sum(
        picks.astype(jnp.int32) * jnp.arange(bands, dtype=jnp.int32)[None, None, :], axis=2
    ).reshape(-1)

    feature_bands = features.reshape(bands, BAND, dims)
    widths = inv_width.reshape(bands, BAND).astype(jnp.float32)
    squares = jnp.sum(jnp.square(feature_bands.astype(jnp.float32)), axis=2)
    product = 0.5 * squares * widths
    high = lax.reduce_precision(product, 8, 7)
    rest = product - high
    middle = lax.reduce_precision(rest, 8, 7)
    blank = jnp.zeros_like(widths)
    sides = jnp.stack(
        [widths, high, middle, rest - middle] + [blank] * (EXTRA - 4), axis=1
    ).astype(jnp.bfloat16)
    send_coords = pl.pallas_call(
        pack_kernel,
        out_shape=jax.ShapeDtypeStruct((devices, MOST * BAND + EXTRA, dims), jnp.bfloat16),
        in_specs=[whole(SMEM)] + [whole()] * 2,
        out_specs=whole(pl.ANY),
        scratch_shapes=[
            pltpu.VMEM((devices, EXTRA, dims), jnp.bfloat16),
            pltpu.SemaphoreType.DMA((MOST + 1, devices)),
        ],
        name="pack",
    )(send_index, feature_bands, sides)
    got_coords = exchange(send_coords)

    flat_ids = ids.reshape(-1)
    active = mask.reshape(-1) == 1
    owner_dev = flat_ids // bands
    within = flat_ids % bands
    far = active & (owner_dev != device)
    rank_mine = jnp.cumsum(need_mine, axis=1) - 1
    rank_lookup = jnp.take(rank_mine.reshape(-1), flat_ids, axis=0, mode="clip")
    entry_of = jnp.where(far, owner_dev * MOST + rank_lookup, within)
    order = jnp.arange(count_all, dtype=jnp.int32)

    def work_list(chosen):
        ones = chosen.astype(jnp.int32)
        place = jnp.cumsum(ones) - 1
        hit = ((place[None, :] == order[:, None]) & chosen[None, :]).astype(jnp.int32)
        tile_id = jnp.sum(hit * order[None, :], axis=1)
        entry = jnp.sum(hit * entry_of[None, :], axis=1)
        count = jnp.sum(ones)
        keep = (order < count).astype(jnp.int32)
        return jnp.stack([tile_id % bands, entry, keep]), count.reshape(1)

    near_work, near_count = work_list(active & ~far)
    far_work, far_count = work_list(far)

    rvec = jnp.stack([0.5 * squares, (2.0 * math.log2(math.e)) * widths], axis=1)

    tile_shape = jax.ShapeDtypeStruct((count_all, BAND, BAND), jnp.bfloat16)

    def building(columns):
        return [
            pltpu.VMEM((columns, BAND, 2 * BAND), jnp.float32),
            pltpu.VMEM((STAGES, GROUP, BAND, BAND), jnp.bfloat16),
            pltpu.SemaphoreType.DMA((STAGES,)),
        ]

    tile_area = count_all * BAND * BAND
    build_cost = pl.CostEstimate(
        flops=tile_area * dims, bytes_accessed=tile_area, transcendentals=tile_area // 2
    )
    near_tiles, deg = pl.pallas_call(
        local_kernel,
        out_shape=(tile_shape, jax.ShapeDtypeStruct((bands, 8, BAND), jnp.float32)),
        in_specs=[whole(SMEM)] * 2 + [whole()] * 3,
        out_specs=(whole(pl.ANY), whole()),
        scratch_shapes=building(bands),
        cost_estimate=build_cost,
        name="local_tiles",
    )(near_work, near_count, feature_bands, sides, rvec)

    row_shape = jax.ShapeDtypeStruct((bands, vectors, BAND), jnp.bfloat16)
    send_shape = jax.ShapeDtypeStruct((entries, vectors, BAND), jnp.bfloat16)
    far_tiles, root, scaled, send = pl.pallas_call(
        remote_kernel,
        out_shape=(tile_shape, jax.ShapeDtypeStruct((bands, BAND), jnp.float32), row_shape, send_shape),
        in_specs=[whole(SMEM)] * 3 + [whole()] * 5,
        out_specs=(whole(pl.ANY), whole(), whole(), whole()),
        scratch_shapes=[pltpu.VMEM((bands, 8, BAND), jnp.float32)] + building(entries),
        cost_estimate=build_cost,
        name="remote_tiles",
    )(far_work, far_count, send_index, feature_bands, got_coords, rvec, deg, start_block)

    centre, halfwidth, values = chebyshev_terms()
    flat_shape = jax.ShapeDtypeStruct((vectors, bands * BAND), jnp.float32)
    total_shape = jax.ShapeDtypeStruct((bands, vectors, BAND), jnp.float32)
    gram_shape = jax.ShapeDtypeStruct((devices, 8, vectors * vectors // 8), jnp.float32)
    fetching = [
        pltpu.VMEM((count_all, BAND, BAND), jnp.bfloat16),
        pltpu.SemaphoreType.DMA((count_all // GROUP,)),
    ]
    product_cost = pl.CostEstimate(
        flops=tile_area * vectors, bytes_accessed=tile_area, transcendentals=0
    )
    previous, current = start_block, start_block
    for power in range(DEGREE):
        first, last = power == 0, power == DEGREE - 1
        if first:
            lead, old = 1.0 / values[1], 0.0
        else:
            lead = 2.0 * values[power] / values[power + 1]
            old = values[power - 1] / values[power + 1]
        gains = (lead * (1.0 - centre) / halfwidth, -lead / halfwidth, old)
        got = exchange(send.reshape(devices, MOST, vectors, BAND)).reshape(entries, vectors, BAND)
        own_total = pl.pallas_call(
            own_kernel,
            out_shape=total_shape,
            in_specs=[whole(SMEM)] * 2 + [whole(), whole(pl.ANY)],
            out_specs=whole(),
            scratch_shapes=fetching,
            cost_estimate=product_cost,
            name="own" + str(power),
        )(near_work, near_count, scaled, near_tiles)
        outs = (flat_shape, gram_shape) if last else (flat_shape, row_shape, send_shape)
        results = pl.pallas_call(
            functools.partial(round_kernel, first, last, gains),
            out_shape=outs,
            in_specs=[whole(SMEM)] * 3 + [whole()] * 5 + [whole(pl.ANY)],
            out_specs=tuple([whole()] * len(outs)),
            scratch_shapes=[pltpu.VMEM((bands, vectors, BAND), jnp.float32)] + fetching,
            cost_estimate=product_cost,
            name="round" + str(power),
        )(far_work, far_count, send_index, got, own_total, root, current, previous, far_tiles)
        previous, current = current, results[0]
        if last:
            parts = exchange(results[1])
        else:
            scaled, send = results[1], results[2]

    basis, factor = pl.pallas_call(
        functools.partial(finish_kernel, devices * bands * BAND),
        out_shape=(flat_shape, jax.ShapeDtypeStruct((vectors, vectors), jnp.float32)),
        in_specs=[whole()] * 2,
        out_specs=(whole(), whole()),
        name="finish",
    )(parts, current)
    return (basis, factor)


def solution(mesh):
    placed = (P(AXES, None), P(AXES), P(None, AXES), P(AXES, None), P(AXES, None))
    return jax.shard_map(
        on_device,
        mesh=mesh,
        in_specs=placed,
        out_specs=(P(None, AXES), P()),
        check_vma=False,
    )
```

time: 297 us -> 268 us (0.902)
  blocking collectives: 68.8 us -> 11.4 us
  waiting for transfers between devices: 81.7 us -> 114 us
  local copies, waits for them, and re-layouts: 23.1 us -> 8.43 us
  Pallas kernels: 94.3 us -> 101 us
  starting transfers between devices: 17.2 us -> 21.4 us
    all_to_all x4 -> x1, blocking collectives: 68.8 us -> 11.4 us  [exchange(): return lax.all_to_all(blocks, AXES, split_axis=0, concat_axis=0, tiled=True)]
    all_to_all x4 -> x6, waiting for transfers between devices: 81.7 us -> 114 us  [exchange(): return lax.all_to_all(blocks, AXES, split_axis=0, concat_axis=0, tiled=True)]
    pallas_call x4 -> x10, Pallas kernels: 44 us -> 68.5 us  [the longest x4 32.8 us: on_device(): pl.pallas_call(functools.partial(round_kernel, first, last, gains), out_s...]
    pallas_call x1, Pallas kernels: 24.2 us -> 12.4 us  [on_device(): pl.pallas_call(local_kernel, out_shape=(tile_shape, jax.ShapeDtypeStruct(...]
    broadcast_in_dim x5 -> x0, local copies, waits for them, and re-layouts: 9.81 us -> none  [the longest x4 9.04 us: columns(): return jnp.broadcast_to(rows[:, :, None], rows.shape + (BAND,))]
    pallas_call x1, Pallas kernels: 20.9 us -> 14.6 us  [on_device(): pl.pallas_call(remote_kernel, out_shape=(tile_shape, jax.ShapeDtypeStruct...]
    all_to_all x4 -> x6, starting transfers between devices: 17.2 us -> 21.4 us  [exchange(): return lax.all_to_all(blocks, AXES, split_axis=0, concat_axis=0, tiled=True)]
    gather x4 -> x1, local copies, waits for them, and re-layouts: 6.42 us -> 2.28 us  [on_device(): rank_lookup = jnp.take(rank_mine.reshape(-1), flat_ids, axis=0, mode='clip')]
  transfers between devices with their start and end apart: 4 -> 6, of which waited for: 4 -> 6; matrix products, arithmetic and copies ran while one was open for 7% -> 5% of each run, Pallas kernels for 8% -> 16%
where the time goes in v2:
time: 268 us; the launch traced here: 266 us
  waiting for transfers between devices  114 us (43%)
  Pallas kernels  101 us (38%)
  starting transfers between devices  21.4 us (8%)
  blocking collectives  11.4 us (4%)
  other arithmetic  9.08 us (3%)
  local copies, waits for them, and re-layouts  8.43 us (3%)
    all_to_all x6, waiting for transfers between devices, exchange(): return lax.all_to_all(blocks, AXES, split_axis=0, concat_axis=0, tiled=True)  114 us
    pallas_call x4, Pallas kernels, on_device(): pl.pallas_call(functools.partial(round_kernel, first, last, gains), out_s...  32.8 us
    pallas_call x4, Pallas kernels, on_device(): pl.pallas_call(own_kernel, out_shape=total_shape, in_specs=[whole(SMEM)]...  29.5 us
    all_to_all x6, starting transfers between devices, exchange(): return lax.all_to_all(blocks, AXES, split_axis=0, concat_axis=0, tiled=True)  21.4 us
    pallas_call x1, Pallas kernels, on_device(): pl.pallas_call(remote_kernel, out_shape=(tile_shape, jax.ShapeDtypeStruct...  14.6 us
    pallas_call x1, Pallas kernels, on_device(): pl.pallas_call(local_kernel, out_shape=(tile_shape, jax.ShapeDtypeStruct(...  12.4 us
    all_to_all x1, blocking collectives, exchange(): return lax.all_to_all(blocks, AXES, split_axis=0, concat_axis=0, tiled=True)  11.4 us
  transfers between devices with their start and end apart: 6, of which 6 were waited for; matrix products, arithmetic and copies ran while one was open for 5% of the time, Pallas kernels for 16%

profile of v2, /device:TPU:0, one launch (start us, length us, event | category | flops | bytes accessed | tf_op | source)
XLA Modules:
  0.0 266.5 jit_solution(2279631585862593882)
XLA Ops:
  0.6 1.6 need.1
  2.2 7.3 %all-to-all-start = ((s32[32,1,32]{2,1,0:T(1,128)}), s32[32,1,32]{2,1,0:T(1,128)S(1)}, u32[]{:S(2)}, u32[]{:S(2)}) async-start(s32[32,1,32]{2,1,0:T(1,128)} %bitcast.53), calls=%async_computation | async-start | bytes 32768 | tf_op jit(solution)/shard_map/all_to_all | solution.py:37
  9.6 2.2 multiply_reduce_fusion
  11.8 0.7 bitcast_convert_fusion
  12.5 0.7 copy.25
  13.3 0.7 stack.35.sides
  14.0 2.6 all-to-all-done
  16.7 0.2 reduce_window_sum.51
  16.9 0.1 select_reduce_fusion.4
  17.0 0.1 copy.23
  17.1 0.6 reshape.395.send_index
  17.7 4.6 %pack.1 = bf16[32,264,256]{2,1,0:T(8,128)(2,1)} custom-call(s32[64]{0:T(128)} %reshape.395.send_index, bf16[32,128,256]{2,1,0:T(8,128)(2,1)} %bitcast.38, bf16[32,8,128]{2,1,0:T(8,128)(2,1)} %stack.35.sides), custom_call_target="tpu_custom_call" | custom-call | tf_op jit(solution)/shard_map/pack/pallas_call | solution.py:333
  22.3 0.0 copy-start.5
  22.3 0.0 copy-start.7
  22.3 0.0 copy-start.4
  22.3 0.0 copy-start.6
  22.4 3.6 %all-to-all-start.1 = ((bf16[32,264,256]{2,1,0:T(8,128)(2,1)}), bf16[32,264,256]{2,1,0:T(8,128)(2,1)}, u32[]{:S(2)}, u32[]{:S(2)}) async-start(bf16[32,264,256]{2,1,0:T(8,128)(2,1)} %pack.1), calls=%async_computation.1 | async-start | bytes 8650752 | tf_op jit(solution)/shard_map/all_to_all | solution.py:37
  25.9 0.0 copy-done.5
  26.0 0.1 reshape.393
  26.0 0.1 reshape.391
  26.1 0.0 copy-done.7
  26.1 0.1 eq.79
  26.2 0.1 eq.75
  26.3 0.2 reduce_window_sum.49
  26.5 0.3 reduce-window.24
  26.8 0.1 slice.16
  26.9 0.3 reduce-window.16
  27.2 0.1 slice.14
  27.4 0.1 sub.57
  27.4 2.3 gather_fusion
  29.7 0.7 convert_reduce_fusion
  30.4 1.3 compare_convert_fusion
  31.7 0.1 slice_reduce_fusion
  31.8 0.1 slice_reduce_fusion.1
  31.9 0.1 add_bitcast_fusion
  32.0 1.0 select_reduce_fusion.1
  33.0 0.6 pad_add_fusion.1.work
  33.6 0.6 pad_add_fusion.work
  34.3 0.6 pad_maximum_fusion.rvec
  34.9 12.4 %local_tiles.1 = (bf16[512,128,128]{2,1,0:T(8,128)(2,1)}, f32[32,8,128]{2,1,0:T(8,128)}) custom-call(s32[3,512]{1,0:T(4,128)} %pad_add_fusion.1.work, s32[1]{0:T(128)} %bitcast.20.count, bf16[32,128,256]{2,1,0:T(8,128)(2,1)} %bitcast.39, bf16[32,8,128]{2,1,0:T(8,128)(2,1)} %stack.35.sides, f32[32,2,128]{2,1,0:T(2,128)} %pad_maximum_fusion.rvec), custom_call_target="tpu_custom_call" | custom-call | flops 2147483648 | bytes 8388608 | tf_op jit(solution)/shard_map/local_tiles/pallas_call | solution.py:384
  47.4 76.3 %all-to-all-done.1.got = bf16[32,264,256]{2,1,0:T(8,128)(2,1)} async-done(((bf16[32,264,256]{2,1,0:T(8,128)(2,1)}), bf16[32,264,256]{2,1,0:T(8,128)(2,1)}, u32[]{:S(2)}, u32[]{:S(2)}) %all-to-all-start.1) | async-done | bytes 4325408 | tf_op jit(solution)/shard_map/all_to_all | solution.py:37
  123.7 14.6 %remote_tiles.1 = (bf16[512,128,128]{2,1,0:T(8,128)(2,1)}, f32[32,128]{1,0:T(8,128)}, bf16[32,32,128]{2,1,0:T(8,128)(2,1)}, bf16[64,32,128]{2,1,0:T(8,128)(2,1)}) custom-call(s32[3,512]{1,0:T(4,128)} %pad_add_fusion.work, s32[1]{0:T(128)} %bitcast.5.count, s32[64]{0:T(128)} %reshape.395.send_index, bf16[32,128,256]{2,1,0:T(8,128)(2,1)} %bitcast.40, ...), custom_call_target="tpu_custom_call" | custom-call | flops 2147483648 | bytes 8388608 | tf_op jit(solution)/shard_map/remote_tiles/pallas_call | solution.py:396
  138.3 2.6 all-to-all-start.2
  140.9 7.4 %own0.1.total_in = f32[32,32,128]{2,1,0:T(8,128)} custom-call(s32[3,512]{1,0:T(4,128)} %pad_add_fusion.1.work, s32[1]{0:T(128)} %bitcast.20.count, bf16[32,32,128]{2,1,0:T(8,128)(2,1)} %get-tuple-element.21.scaled, bf16[512,128,128]{2,1,0:T(8,128)(2,1)} %get-tuple-element.22.tiles), custom_call_target="tpu_custom_call" | custom-call | flops 268435456 | bytes 8388608 | tf_op jit(solution)/shard_map/own0/pallas_call | solution.py:427
  148.3 8.9 %all-to-all-done.2 = bf16[32,2,32,128]{3,2,1,0:T(8,128)(2,1)S(1)} async-done(((bf16[32,2,32,128]{3,2,1,0:T(8,128)(2,1)}), bf16[32,2,32,128]{3,2,1,0:T(8,128)(2,1)S(1)}, u32[]{:S(2)}, u32[]{:S(2)}) %all-to-all-start.2) | async-done | bytes 524320 | tf_op jit(solution)/shard_map/all_to_all | solution.py:37
  157.2 0.8 copy-done.1
  158.0 8.2 %round0.1 = (f32[32,4096]{1,0:T(8,128)}, bf16[32,32,128]{2,1,0:T(8,128)(2,1)}, bf16[64,32,128]{2,1,0:T(8,128)(2,1)}) custom-call(s32[3,512]{1,0:T(4,128)} %pad_add_fusion.work, s32[1]{0:T(128)} %bitcast.5.count, s32[64]{0:T(128)} %reshape.395.send_index, bf16[64,32,128]{2,1,0:T(8,128)(2,1)} %bitcast.42, f32[32,32,128]{2,1,0:T(8,128)} %own0.1.total_in, ...), custom_call_target="tpu_custom_call" | custom-call | flops 268435456 | bytes 8388608 | tf_op jit(solution)/shard_map/round0/pallas_call | solution.py:437
  166.2 2.6 all-to-all-start.3
  168.8 7.4 %own1.1.total_in = f32[32,32,128]{2,1,0:T(8,128)} custom-call(s32[3,512]{1,0:T(4,128)} %pad_add_fusion.1.work, s32[1]{0:T(128)} %bitcast.20.count, bf16[32,32,128]{2,1,0:T(8,128)(2,1)} %get-tuple-element.26.scaled, bf16[512,128,128]{2,1,0:T(8,128)(2,1)} %get-tuple-element.22.tiles), custom_call_target="tpu_custom_call" | custom-call | flops 268435456 | bytes 8388608 | tf_op jit(solution)/shard_map/own1/pallas_call | solution.py:427
  176.2 8.8 %all-to-all-done.3 = bf16[32,2,32,128]{3,2,1,0:T(8,128)(2,1)S(1)} async-done(((bf16[32,2,32,128]{3,2,1,0:T(8,128)(2,1)}), bf16[32,2,32,128]{3,2,1,0:T(8,128)(2,1)S(1)}, u32[]{:S(2)}, u32[]{:S(2)}) %all-to-all-start.3) | async-done | bytes 524320 | tf_op jit(solution)/shard_map/all_to_all | solution.py:37
  185.0 0.8 copy-done.3
  185.8 8.2 %round1.1 = (f32[32,4096]{1,0:T(8,128)}, bf16[32,32,128]{2,1,0:T(8,128)(2,1)}, bf16[64,32,128]{2,1,0:T(8,128)(2,1)}) custom-call(s32[3,512]{1,0:T(4,128)} %pad_add_fusion.work, s32[1]{0:T(128)} %bitcast.5.count, s32[64]{0:T(128)} %reshape.395.send_index, bf16[64,32,128]{2,1,0:T(8,128)(2,1)} %bitcast.44, f32[32,32,128]{2,1,0:T(8,128)} %own1.1.total_in, ...), custom_call_target="tpu_custom_call" | custom-call | flops 268435456 | bytes 8388608 | tf_op jit(solution)/shard_map/round1/pallas_call | solution.py:437
  194.0 2.6 all-to-all-start.4
  196.7 7.4 %own2.1.total_in = f32[32,32,128]{2,1,0:T(8,128)} custom-call(s32[3,512]{1,0:T(4,128)} %pad_add_fusion.1.work, s32[1]{0:T(128)} %bitcast.20.count, bf16[32,32,128]{2,1,0:T(8,128)(2,1)} %get-tuple-element.29.scaled, bf16[512,128,128]{2,1,0:T(8,128)(2,1)} %get-tuple-element.22.tiles), custom_call_target="tpu_custom_call" | custom-call | flops 268435456 | bytes 8388608 | tf_op jit(solution)/shard_map/own2/pallas_call | solution.py:427
  204.1 8.8 %all-to-all-done.4 = bf16[32,2,32,128]{3,2,1,0:T(8,128)(2,1)S(1)} async-done(((bf16[32,2,32,128]{3,2,1,0:T(8,128)(2,1)}), bf16[32,2,32,128]{3,2,1,0:T(8,128)(2,1)S(1)}, u32[]{:S(2)}, u32[]{:S(2)}) %all-to-all-start.4) | async-done | bytes 524320 | tf_op jit(solution)/shard_map/all_to_all | solution.py:37
  212.9 0.8 copy-done.2
  213.7 8.2 %round2.1 = (f32[32,4096]{1,0:T(8,128)}, bf16[32,32,128]{2,1,0:T(8,128)(2,1)}, bf16[64,32,128]{2,1,0:T(8,128)(2,1)}) custom-call(s32[3,512]{1,0:T(4,128)} %pad_add_fusion.work, s32[1]{0:T(128)} %bitcast.5.count, s32[64]{0:T(128)} %reshape.395.send_index, bf16[64,32,128]{2,1,0:T(8,128)(2,1)} %bitcast.43, f32[32,32,128]{2,1,0:T(8,128)} %own2.1.total_in, ...), custom_call_target="tpu_custom_call" | custom-call | flops 268435456 | bytes 8388608 | tf_op jit(solution)/shard_map/round2/pallas_call | solution.py:437
  221.9 2.6 all-to-all-start.5
  224.5 7.4 %own3.1.total_in = f32[32,32,128]{2,1,0:T(8,128)} custom-call(s32[3,512]{1,0:T(4,128)} %pad_add_fusion.1.work, s32[1]{0:T(128)} %bitcast.20.count, bf16[32,32,128]{2,1,0:T(8,128)(2,1)} %get-tuple-element.32.scaled, bf16[512,128,128]{2,1,0:T(8,128)(2,1)} %get-tuple-element.22.tiles), custom_call_target="tpu_custom_call" | custom-call | flops 268435456 | bytes 8388608 | tf_op jit(solution)/shard_map/own3/pallas_call | solution.py:427
  231.9 8.8 %all-to-all-done.5 = bf16[32,2,32,128]{3,2,1,0:T(8,128)(2,1)S(1)} async-done(((bf16[32,2,32,128]{3,2,1,0:T(8,128)(2,1)}), bf16[32,2,32,128]{3,2,1,0:T(8,128)(2,1)S(1)}, u32[]{:S(2)}, u32[]{:S(2)}) %all-to-all-start.5) | async-done | bytes 524320 | tf_op jit(solution)/shard_map/all_to_all | solution.py:37
  240.7 0.8 copy-done
  241.5 8.2 %round3.1 = (f32[32,4096]{1,0:T(8,128)}, f32[32,8,128]{2,1,0:T(8,128)}) custom-call(s32[3,512]{1,0:T(4,128)} %pad_add_fusion.work, s32[1]{0:T(128)} %bitcast.5.count, s32[64]{0:T(128)} %reshape.395.send_index, bf16[64,32,128]{2,1,0:T(8,128)(2,1)} %bitcast.41, f32[32,32,128]{2,1,0:T(8,128)} %own3.1.total_in, f32[32,128]{1,0:T(8,128)} %get-tuple-element.23.root, ...), custom_call_target="tpu_custom_call" | custom-call | flops 268435456 | bytes 8388608 | tf_op jit(solution)/shard_map/round3/pallas_call | solution.py:437
  249.7 11.4 %all_to_all.39.parts = f32[32,8,128]{2,1,0:T(8,128)} all-to-all(f32[32,8,128]{2,1,0:T(8,128)} %get-tuple-element.34), channel_id=1, replica_groups=mesh['gx'=4,'gy'=8] {'gx','gy'}, dimensions={0} | all-to-all | bytes 262144 | tf_op jit(solution)/shard_map/all_to_all | solution.py:37
  261.2 5.3 %finish.1 = (f32[32,4096]{1,0:T(8,128)}, f32[32,32]{1,0:T(8,128)}) custom-call(f32[32,8,128]{2,1,0:T(8,128)} %all_to_all.39.parts, f32[32,4096]{1,0:T(8,128)} %get-tuple-element.35.flat), custom_call_target="tpu_custom_call" | custom-call | tf_op jit(solution)/shard_map/finish/pallas_call | solution.py:452
  (24 shorter events, 0.3 us)
Async XLA Ops:
  2.2 14.4 %all-to-all-start = ((s32[32,1,32]{2,1,0:T(1,128)}), s32[32,1,32]{2,1,0:T(1,128)S(1)}, u32[]{:S(2)}, u32[]{:S(2)}) async-start(s32[32,1,32]{2,1,0:T(1,128)} %bitcast.53), calls=%async_computation | async-start | bytes 32768 | tf_op jit(solution)/shard_map/all_to_all | solution.py:37
  22.3 3.6 %copy-start.5 = (s32[32,16]{0,1:T(8,128)S(1)}, s32[32,16]{0,1:T(8,128)}, u32[]{:S(2)}) copy-start(s32[32,16]{0,1:T(8,128)} %param.8) | copy-start | bytes 6148
  22.3 3.8 %copy-start.7 = (s32[32,16]{0,1:T(8,128)S(1)}, s32[32,16]{0,1:T(8,128)}, u32[]{:S(2)}) copy-start(s32[32,16]{0,1:T(8,128)} %param.9) | copy-start | bytes 6148
  22.3 4.0 %copy-start.4 = (s32[32,32]{1,0:T(8,128)S(1)}, s32[32,32]{1,0:T(8,128)}, u32[]{:S(2)}) copy-start(s32[32,32]{1,0:T(8,128)} %need.1) | copy-start | bytes 12292
  22.3 11.9 %copy-start.6 = (bf16[4096]{0:T(1024)(128)(2,1)S(1)}, bf16[4096]{0:T(1024)(128)(2,1)}, u32[]{:S(2)}) copy-start(bf16[4096]{0:T(1024)(128)(2,1)} %param.6) | copy-start | bytes 24580
  22.4 101.4 %all-to-all-start.1 = ((bf16[32,264,256]{2,1,0:T(8,128)(2,1)}), bf16[32,264,256]{2,1,0:T(8,128)(2,1)}, u32[]{:S(2)}, u32[]{:S(2)}) async-start(bf16[32,264,256]{2,1,0:T(8,128)(2,1)} %pack.1), calls=%async_computation.1 | async-start | bytes 8650752 | tf_op jit(solution)/shard_map/all_to_all | solution.py:37
  138.3 18.9 %all-to-all-start.2 = ((bf16[32,2,32,128]{3,2,1,0:T(8,128)(2,1)}), bf16[32,2,32,128]{3,2,1,0:T(8,128)(2,1)S(1)}, u32[]{:S(2)}, u32[]{:S(2)}) async-start(bf16[32,2,32,128]{3,2,1,0:T(8,128)(2,1)} %bitcast.46), calls=%async_computation.2 | async-start | bytes 1048576 | tf_op jit(solution)/shard_map/all_to_all | solution.py:37
  157.2 0.8 copy-start.1
  166.2 18.9 %all-to-all-start.3 = ((bf16[32,2,32,128]{3,2,1,0:T(8,128)(2,1)}), bf16[32,2,32,128]{3,2,1,0:T(8,128)(2,1)S(1)}, u32[]{:S(2)}, u32[]{:S(2)}) async-start(bf16[32,2,32,128]{3,2,1,0:T(8,128)(2,1)} %bitcast.47), calls=%async_computation.3 | async-start | bytes 1048576 | tf_op jit(solution)/shard_map/all_to_all | solution.py:37
  185.0 0.8 copy-start.3
  194.0 18.9 %all-to-all-start.4 = ((bf16[32,2,32,128]{3,2,1,0:T(8,128)(2,1)}), bf16[32,2,32,128]{3,2,1,0:T(8,128)(2,1)S(1)}, u32[]{:S(2)}, u32[]{:S(2)}) async-start(bf16[32,2,32,128]{3,2,1,0:T(8,128)(2,1)} %bitcast.48), calls=%async_computation.4 | async-start | bytes 1048576 | tf_op jit(solution)/shard_map/all_to_all | solution.py:37
  212.9 0.8 copy-start.2
  221.9 18.9 %all-to-all-start.5 = ((bf16[32,2,32,128]{3,2,1,0:T(8,128)(2,1)}), bf16[32,2,32,128]{3,2,1,0:T(8,128)(2,1)S(1)}, u32[]{:S(2)}, u32[]{:S(2)}) async-start(bf16[32,2,32,128]{3,2,1,0:T(8,128)(2,1)} %bitcast.45), calls=%async_computation.5 | async-start | bytes 1048576 | tf_op jit(solution)/shard_map/all_to_all | solution.py:37
  240.7 0.8 copy-start

commit v3 on v2

--- a/solution.py
+++ b/solution.py
@@ -15,6 +15,7 @@
 GROUP = 16
 STAGES = 4
 EXTRA = 8
+LIMIT = 50 * 1024 * 1024
 
 LOW_EDGE = 0.2
 HIGH_EDGE = 2.0
@@ -377,6 +378,7 @@
             pltpu.SemaphoreType.DMA((STAGES,)),
         ]
 
+    remote_bytes = entries * BAND * (8 * BAND + 3 * dims) + 10 * 1024 * 1024
     tile_area = count_all * BAND * BAND
     build_cost = pl.CostEstimate(
         flops=tile_area * dims, bytes_accessed=tile_area, transcendentals=tile_area // 2
@@ -388,6 +390,7 @@
         out_specs=(whole(pl.ANY), whole()),
         scratch_shapes=building(bands),
         cost_estimate=build_cost,
+        compiler_params=pltpu.CompilerParams(vmem_limit_bytes=LIMIT),
         name="local_tiles",
     )(near_work, near_count, feature_bands, sides, rvec)
 
@@ -400,6 +403,7 @@
         out_specs=(whole(pl.ANY), whole(), whole(), whole()),
         scratch_shapes=[pltpu.VMEM((bands, 8, BAND), jnp.float32)] + building(entries),
         cost_estimate=build_cost,
+        compiler_params=pltpu.CompilerParams(vmem_limit_bytes=max(LIMIT, remote_bytes)),
         name="remote_tiles",
     )(far_work, far_count, send_index, feature_bands, got_coords, rvec, deg, start_block)
 
@@ -431,6 +435,7 @@
             out_specs=whole(),
             scratch_shapes=fetching,
             cost_estimate=product_cost,
+            compiler_params=pltpu.CompilerParams(vmem_limit_bytes=LIMIT),
             name="own" + str(power),
         )(near_work, near_count, scaled, near_tiles)
         outs = (flat_shape, gram_shape) if last else (flat_shape, row_shape, send_shape)
@@ -441,6 +446,7 @@
             out_specs=tuple([whole()] * len(outs)),
             scratch_shapes=[pltpu.VMEM((bands, vectors, BAND), jnp.float32)] + fetching,
             cost_estimate=product_cost,
+            compiler_params=pltpu.CompilerParams(vmem_limit_bytes=LIMIT),
             name="round" + str(power),
         )(far_work, far_count, send_index, got, own_total, root, current, previous, far_tiles)
         previous, current = current, results[0]
@@ -454,6 +460,7 @@
         out_shape=(flat_shape, jax.ShapeDtypeStruct((vectors, vectors), jnp.float32)),
         in_specs=[whole()] * 2,
         out_specs=(whole(), whole()),
+        compiler_params=pltpu.CompilerParams(vmem_limit_bytes=LIMIT),
         name="finish",
     )(parts, current)
     return (basis, factor)

time: 268 us -> 257 us (0.959)
  Pallas kernels: 101 us -> 88.7 us
  waiting for transfers between devices: 114 us -> 122 us
  local copies, waits for them, and re-layouts: 8.43 us -> 5.32 us
    all_to_all x6, waiting for transfers between devices: 114 us -> 122 us  [exchange(): return lax.all_to_all(blocks, AXES, split_axis=0, concat_axis=0, tiled=True)]
    pallas_call x4, Pallas kernels: 32.8 us -> 27.9 us  [on_device(): pl.pallas_call(functools.partial(round_kernel, first, last, gains), out_s...]
    pallas_call x4, Pallas kernels: 29.5 us -> 25.2 us  [on_device(): pl.pallas_call(own_kernel, out_shape=total_shape, in_specs=[whole(SMEM)]...]
    unnamed x16, local copies, waits for them, and re-layouts: 3.2 us -> 0.05 us
  transfers between devices with their start and end apart: 6 -> 6, of which waited for: 6 -> 6; matrix products, arithmetic and copies ran while one was open for 5% -> 5% of each run, Pallas kernels for 16% -> 14%
where the time goes in v3:
time: 257 us; the launch traced here: 256 us
  waiting for transfers between devices  122 us (47%)
  Pallas kernels  88.7 us (35%)
  starting transfers between devices  21.5 us (8%)
  blocking collectives  10.4 us (4%)
  other arithmetic  7.34 us (3%)
  local copies, waits for them, and re-layouts  5.32 us (2%)
    all_to_all x6, waiting for transfers between devices, exchange(): return lax.all_to_all(blocks, AXES, split_axis=0, concat_axis=0, tiled=True)  122 us
    pallas_call x4, Pallas kernels, on_device(): pl.pallas_call(functools.partial(round_kernel, first, last, gains), out_s...  27.9 us
    pallas_call x4, Pallas kernels, on_device(): pl.pallas_call(own_kernel, out_shape=total_shape, in_specs=[whole(SMEM)]...  25.2 us
    all_to_all x6, starting transfers between devices, exchange(): return lax.all_to_all(blocks, AXES, split_axis=0, concat_axis=0, tiled=True)  21.5 us
    pallas_call x1, Pallas kernels, on_device(): pl.pallas_call(remote_kernel, out_shape=(tile_shape, jax.ShapeDtypeStruct...  13.9 us
    pallas_call x1, Pallas kernels, on_device(): pl.pallas_call(local_kernel, out_shape=(tile_shape, jax.ShapeDtypeStruct(...  11.3 us
    all_to_all x1, blocking collectives, exchange(): return lax.all_to_all(blocks, AXES, split_axis=0, concat_axis=0, tiled=True)  10.4 us
  transfers between devices with their start and end apart: 6, of which 6 were waited for; matrix products, arithmetic and copies ran while one was open for 5% of the time, Pallas kernels for 14%

profile of v3, /device:TPU:0, one launch (start us, length us, event | category | flops | bytes accessed | tf_op | source)
XLA Modules:
  0.0 255.8 jit_solution(4257724498261790995)
XLA Ops:
  0.6 1.6 need.1
  2.2 7.3 %all-to-all-start = ((s32[32,1,32]{2,1,0:T(1,128)}), s32[32,1,32]{2,1,0:T(1,128)S(1)}, u32[]{:S(2)}, u32[]{:S(2)}) async-start(s32[32,1,32]{2,1,0:T(1,128)} %bitcast.49), calls=%async_computation | async-start | bytes 32768 | tf_op jit(solution)/shard_map/all_to_all | solution.py:38
  9.6 2.2 multiply_reduce_fusion
  11.8 0.7 bitcast_convert_fusion
  12.5 0.7 copy.25
  13.3 0.7 stack.35.sides
  14.0 2.6 %all-to-all-done = s32[32,1,32]{2,1,0:T(1,128)S(1)} async-done(((s32[32,1,32]{2,1,0:T(1,128)}), s32[32,1,32]{2,1,0:T(1,128)S(1)}, u32[]{:S(2)}, u32[]{:S(2)}) %all-to-all-start) | async-done | bytes 4128 | tf_op jit(solution)/shard_map/all_to_all | solution.py:38
  16.7 0.2 reduce_window_sum.51
  16.9 0.1 select_reduce_fusion.4
  17.0 0.1 copy.23
  17.1 0.6 reshape.395.send_index
  17.7 4.6 %pack.1 = bf16[32,264,256]{2,1,0:T(8,128)(2,1)} custom-call(s32[64]{0:T(128)} %reshape.395.send_index, bf16[32,128,256]{2,1,0:T(8,128)(2,1)} %bitcast.38, bf16[32,8,128]{2,1,0:T(8,128)(2,1)} %stack.35.sides), custom_call_target="tpu_custom_call" | custom-call | tf_op jit(solution)/shard_map/pack/pallas_call | solution.py:334
  22.3 0.0 copy-start.5
  22.3 0.0 copy-start.7
  22.4 0.0 copy-start.4
  22.4 0.0 copy-start.6
  22.4 0.0 copy-start
  22.4 0.0 copy-start.2
  22.4 3.7 %all-to-all-start.1 = ((bf16[32,264,256]{2,1,0:T(8,128)(2,1)}), bf16[32,264,256]{2,1,0:T(8,128)(2,1)}, u32[]{:S(2)}, u32[]{:S(2)}) async-start(bf16[32,264,256]{2,1,0:T(8,128)(2,1)} %pack.1), calls=%async_computation.1 | async-start | bytes 8650752 | tf_op jit(solution)/shard_map/all_to_all | solution.py:38
  26.1 0.0 copy-done.5
  26.1 0.1 reshape.393
  26.2 0.1 reshape.391
  26.3 0.0 copy-done.7
  26.3 0.1 eq.79
  26.4 0.1 eq.75
  26.5 0.0 copy-done.4
  26.5 0.2 reduce_window_sum.49
  26.7 0.3 reduce-window.24
  27.0 0.1 slice.16
  27.1 0.3 reduce-window.16
  27.4 0.1 slice.14
  27.5 0.1 sub.57
  27.6 2.3 gather_fusion
  29.9 0.0 copy-start.1
  29.9 0.0 copy-start.3
  29.9 0.7 convert_reduce_fusion
  30.6 1.3 compare_convert_fusion
  31.9 0.1 slice_reduce_fusion
  32.0 0.1 slice_reduce_fusion.1
  32.2 0.1 add_bitcast_fusion
  32.2 1.0 select_reduce_fusion.1
  33.3 0.0 copy-done.6
  33.4 11.3 %local_tiles.1 = (bf16[512,128,128]{2,1,0:T(8,128)(2,1)}, f32[32,8,128]{2,1,0:T(8,128)S(1)}) custom-call(s32[3,512]{1,0:T(4,128)S(1)} %pad_add_fusion.1.work, s32[1]{0:T(128)} %bitcast.20.count, bf16[32,128,256]{2,1,0:T(8,128)(2,1)S(1)} %bitcast.39, bf16[32,8,128]{2,1,0:T(8,128)(2,1)S(1)} %copy-done.2, f32[32,2,128]{2,1,0:T(2,128)S(1)} %pad_maximum_fusion.rvec), custom_call_target="tpu_custom_call" | custom-call | flops 2147483648 | bytes 8388608 | tf_op jit(solution)/shard_map/local_tiles/pallas_call | solution.py:386
  44.7 79.2 %all-to-all-done.1.got = bf16[32,264,256]{2,1,0:T(8,128)(2,1)} async-done(((bf16[32,264,256]{2,1,0:T(8,128)(2,1)}), bf16[32,264,256]{2,1,0:T(8,128)(2,1)}, u32[]{:S(2)}, u32[]{:S(2)}) %all-to-all-start.1) | async-done | bytes 4325408 | tf_op jit(solution)/shard_map/all_to_all | solution.py:38
  123.9 0.0 copy-done.3
  123.9 13.9 %remote_tiles.1 = (bf16[512,128,128]{2,1,0:T(8,128)(2,1)}, f32[32,128]{1,0:T(8,128)S(1)}, bf16[32,32,128]{2,1,0:T(8,128)(2,1)S(1)}, bf16[64,32,128]{2,1,0:T(8,128)(2,1)}) custom-call(s32[3,512]{1,0:T(4,128)S(1)} %pad_add_fusion.work, s32[1]{0:T(128)} %bitcast.5.count, s32[64]{0:T(128)S(1)} %copy-done.3, bf16[32,128,256]{2,1,0:T(8,128)(2,1)S(1)} %bitcast.40, ...), custom_call_target="tpu_custom_call" | custom-call | flops 2147483648 | bytes 8388608 | tf_op jit(solution)/shard_map/remote_tiles/pallas_call | solution.py:399
  137.8 2.6 %all-to-all-start.2 = ((bf16[32,2,32,128]{3,2,1,0:T(8,128)(2,1)}), bf16[32,2,32,128]{3,2,1,0:T(8,128)(2,1)S(1)}, u32[]{:S(2)}, u32[]{:S(2)}) async-start(bf16[32,2,32,128]{3,2,1,0:T(8,128)(2,1)} %bitcast.21), calls=%async_computation.2 | async-start | bytes 1048576 | tf_op jit(solution)/shard_map/all_to_all | solution.py:38
  140.5 6.3 %own0.1.total_in = f32[32,32,128]{2,1,0:T(8,128)S(1)} custom-call(s32[3,512]{1,0:T(4,128)S(1)} %pad_add_fusion.1.work, s32[1]{0:T(128)} %bitcast.20.count, bf16[32,32,128]{2,1,0:T(8,128)(2,1)S(1)} %get-tuple-element.21.scaled, bf16[512,128,128]{2,1,0:T(8,128)(2,1)} %get-tuple-element.22.tiles), custom_call_target="tpu_custom_call" | custom-call | flops 268435456 | bytes 8388608 | tf_op jit(solution)/shard_map/own0/pallas_call | solution.py:431
  146.8 9.9 %all-to-all-done.2 = bf16[32,2,32,128]{3,2,1,0:T(8,128)(2,1)S(1)} async-done(((bf16[32,2,32,128]{3,2,1,0:T(8,128)(2,1)}), bf16[32,2,32,128]{3,2,1,0:T(8,128)(2,1)S(1)}, u32[]{:S(2)}, u32[]{:S(2)}) %all-to-all-start.2) | async-done | bytes 524320 | tf_op jit(solution)/shard_map/all_to_all | solution.py:38
  156.7 7.0 %round0.1 = (f32[32,4096]{1,0:T(8,128)S(1)}, bf16[32,32,128]{2,1,0:T(8,128)(2,1)S(1)}, bf16[64,32,128]{2,1,0:T(8,128)(2,1)}) custom-call(s32[3,512]{1,0:T(4,128)S(1)} %pad_add_fusion.work, s32[1]{0:T(128)} %bitcast.5.count, s32[64]{0:T(128)S(1)} %copy-done.3, bf16[64,32,128]{2,1,0:T(8,128)(2,1)S(1)} %bitcast.42, f32[32,32,128]{2,1,0:T(8,128)S(1)} %own0.1.total_in, ...), custom_call_target="tpu_custom_call" | custom-call | flops 268435456 | bytes 8388608 | tf_op jit(solution)/shard_map/round0/pallas_call | solution.py:442
  163.7 2.6 %all-to-all-start.3 = ((bf16[32,2,32,128]{3,2,1,0:T(8,128)(2,1)}), bf16[32,2,32,128]{3,2,1,0:T(8,128)(2,1)S(1)}, u32[]{:S(2)}, u32[]{:S(2)}) async-start(bf16[32,2,32,128]{3,2,1,0:T(8,128)(2,1)} %bitcast.23), calls=%async_computation.3 | async-start | bytes 1048576 | tf_op jit(solution)/shard_map/all_to_all | solution.py:38
  166.4 6.3 %own1.1.total_in = f32[32,32,128]{2,1,0:T(8,128)S(1)} custom-call(s32[3,512]{1,0:T(4,128)S(1)} %pad_add_fusion.1.work, s32[1]{0:T(128)} %bitcast.20.count, bf16[32,32,128]{2,1,0:T(8,128)(2,1)S(1)} %get-tuple-element.26.scaled, bf16[512,128,128]{2,1,0:T(8,128)(2,1)} %get-tuple-element.22.tiles), custom_call_target="tpu_custom_call" | custom-call | flops 268435456 | bytes 8388608 | tf_op jit(solution)/shard_map/own1/pallas_call | solution.py:431
  172.7 9.9 %all-to-all-done.3 = bf16[32,2,32,128]{3,2,1,0:T(8,128)(2,1)S(1)} async-done(((bf16[32,2,32,128]{3,2,1,0:T(8,128)(2,1)}), bf16[32,2,32,128]{3,2,1,0:T(8,128)(2,1)S(1)}, u32[]{:S(2)}, u32[]{:S(2)}) %all-to-all-start.3) | async-done | bytes 524320 | tf_op jit(solution)/shard_map/all_to_all | solution.py:38
  182.6 7.1 %round1.1 = (f32[32,4096]{1,0:T(8,128)S(1)}, bf16[32,32,128]{2,1,0:T(8,128)(2,1)S(1)}, bf16[64,32,128]{2,1,0:T(8,128)(2,1)}) custom-call(s32[3,512]{1,0:T(4,128)S(1)} %pad_add_fusion.work, s32[1]{0:T(128)} %bitcast.5.count, s32[64]{0:T(128)S(1)} %copy-done.3, bf16[64,32,128]{2,1,0:T(8,128)(2,1)S(1)} %bitcast.44, f32[32,32,128]{2,1,0:T(8,128)S(1)} %own1.1.total_in, ...), custom_call_target="tpu_custom_call" | custom-call | flops 268435456 | bytes 8388608 | tf_op jit(solution)/shard_map/round1/pallas_call | solution.py:442
  189.7 2.6 %all-to-all-start.4 = ((bf16[32,2,32,128]{3,2,1,0:T(8,128)(2,1)}), bf16[32,2,32,128]{3,2,1,0:T(8,128)(2,1)S(1)}, u32[]{:S(2)}, u32[]{:S(2)}) async-start(bf16[32,2,32,128]{3,2,1,0:T(8,128)(2,1)} %bitcast.25), calls=%async_computation.4 | async-start | bytes 1048576 | tf_op jit(solution)/shard_map/all_to_all | solution.py:38
  192.3 6.3 %own2.1.total_in = f32[32,32,128]{2,1,0:T(8,128)S(1)} custom-call(s32[3,512]{1,0:T(4,128)S(1)} %pad_add_fusion.1.work, s32[1]{0:T(128)} %bitcast.20.count, bf16[32,32,128]{2,1,0:T(8,128)(2,1)S(1)} %get-tuple-element.29.scaled, bf16[512,128,128]{2,1,0:T(8,128)(2,1)} %get-tuple-element.22.tiles), custom_call_target="tpu_custom_call" | custom-call | flops 268435456 | bytes 8388608 | tf_op jit(solution)/shard_map/own2/pallas_call | solution.py:431
  198.6 9.9 %all-to-all-done.4 = bf16[32,2,32,128]{3,2,1,0:T(8,128)(2,1)S(1)} async-done(((bf16[32,2,32,128]{3,2,1,0:T(8,128)(2,1)}), bf16[32,2,32,128]{3,2,1,0:T(8,128)(2,1)S(1)}, u32[]{:S(2)}, u32[]{:S(2)}) %all-to-all-start.4) | async-done | bytes 524320 | tf_op jit(solution)/shard_map/all_to_all | solution.py:38
  208.6 7.1 %round2.1 = (f32[32,4096]{1,0:T(8,128)S(1)}, bf16[32,32,128]{2,1,0:T(8,128)(2,1)S(1)}, bf16[64,32,128]{2,1,0:T(8,128)(2,1)}) custom-call(s32[3,512]{1,0:T(4,128)S(1)} %pad_add_fusion.work, s32[1]{0:T(128)} %bitcast.5.count, s32[64]{0:T(128)S(1)} %copy-done.3, bf16[64,32,128]{2,1,0:T(8,128)(2,1)S(1)} %bitcast.43, f32[32,32,128]{2,1,0:T(8,128)S(1)} %own2.1.total_in, ...), custom_call_target="tpu_custom_call" | custom-call | flops 268435456 | bytes 8388608 | tf_op jit(solution)/shard_map/round2/pallas_call | solution.py:442
  215.6 2.6 %all-to-all-start.5 = ((bf16[32,2,32,128]{3,2,1,0:T(8,128)(2,1)}), bf16[32,2,32,128]{3,2,1,0:T(8,128)(2,1)S(1)}, u32[]{:S(2)}, u32[]{:S(2)}) async-start(bf16[32,2,32,128]{3,2,1,0:T(8,128)(2,1)} %bitcast.27), calls=%async_computation.5 | async-start | bytes 1048576 | tf_op jit(solution)/shard_map/all_to_all | solution.py:38
  218.3 6.3 %own3.1.total_in = f32[32,32,128]{2,1,0:T(8,128)S(1)} custom-call(s32[3,512]{1,0:T(4,128)S(1)} %pad_add_fusion.1.work, s32[1]{0:T(128)} %bitcast.20.count, bf16[32,32,128]{2,1,0:T(8,128)(2,1)S(1)} %get-tuple-element.32.scaled, bf16[512,128,128]{2,1,0:T(8,128)(2,1)} %get-tuple-element.22.tiles), custom_call_target="tpu_custom_call" | custom-call | flops 268435456 | bytes 8388608 | tf_op jit(solution)/shard_map/own3/pallas_call | solution.py:431
  224.6 9.9 %all-to-all-done.5 = bf16[32,2,32,128]{3,2,1,0:T(8,128)(2,1)S(1)} async-done(((bf16[32,2,32,128]{3,2,1,0:T(8,128)(2,1)}), bf16[32,2,32,128]{3,2,1,0:T(8,128)(2,1)S(1)}, u32[]{:S(2)}, u32[]{:S(2)}) %all-to-all-start.5) | async-done | bytes 524320 | tf_op jit(solution)/shard_map/all_to_all | solution.py:38
  234.5 6.7 %round3.1 = (f32[32,4096]{1,0:T(8,128)S(1)}, f32[32,8,128]{2,1,0:T(8,128)S(1)}) custom-call(s32[3,512]{1,0:T(4,128)S(1)} %pad_add_fusion.work, s32[1]{0:T(128)} %bitcast.5.count, s32[64]{0:T(128)S(1)} %copy-done.3, bf16[64,32,128]{2,1,0:T(8,128)(2,1)S(1)} %bitcast.41, f32[32,32,128]{2,1,0:T(8,128)S(1)} %own3.1.total_in, ...), custom_call_target="tpu_custom_call" | custom-call | flops 268435456 | bytes 8388608 | tf_op jit(solution)/shard_map/round3/pallas_call | solution.py:442
  241.2 10.4 %all_to_all.39.parts = f32[32,8,128]{2,1,0:T(8,128)S(1)} all-to-all(f32[32,8,128]{2,1,0:T(8,128)S(1)} %get-tuple-element.34), channel_id=1, replica_groups=mesh['gx'=4,'gy'=8] {'gx','gy'}, dimensions={0} | all-to-all | bytes 262144 | tf_op jit(solution)/shard_map/all_to_all | solution.py:38
  251.7 4.2 %finish.1 = (f32[32,4096]{1,0:T(8,128)}, f32[32,32]{1,0:T(8,128)}) custom-call(f32[32,8,128]{2,1,0:T(8,128)S(1)} %all_to_all.39.parts, f32[32,4096]{1,0:T(8,128)S(1)} %get-tuple-element.35.flat), custom_call_target="tpu_custom_call" | custom-call | tf_op jit(solution)/shard_map/finish/pallas_call | solution.py:458
  (24 shorter events, 0.3 us)
Async XLA Ops:
  2.2 14.4 %all-to-all-start = ((s32[32,1,32]{2,1,0:T(1,128)}), s32[32,1,32]{2,1,0:T(1,128)S(1)}, u32[]{:S(2)}, u32[]{:S(2)}) async-start(s32[32,1,32]{2,1,0:T(1,128)} %bitcast.49), calls=%async_computation | async-start | bytes 32768 | tf_op jit(solution)/shard_map/all_to_all | solution.py:38
  22.3 3.8 %copy-start.5 = (s32[32,16]{0,1:T(8,128)S(1)}, s32[32,16]{0,1:T(8,128)}, u32[]{:S(2)}) copy-start(s32[32,16]{0,1:T(8,128)} %param.8) | copy-start | bytes 6148
  22.3 3.9 %copy-start.7 = (s32[32,16]{0,1:T(8,128)S(1)}, s32[32,16]{0,1:T(8,128)}, u32[]{:S(2)}) copy-start(s32[32,16]{0,1:T(8,128)} %param.9) | copy-start | bytes 6148
  22.4 4.1 %copy-start.4 = (s32[32,32]{1,0:T(8,128)S(1)}, s32[32,32]{1,0:T(8,128)}, u32[]{:S(2)}) copy-start(s32[32,32]{1,0:T(8,128)} %need.1) | copy-start | bytes 12292
  22.4 11.0 %copy-start.6 = (bf16[4096]{0:T(1024)(128)(2,1)S(1)}, bf16[4096]{0:T(1024)(128)(2,1)}, u32[]{:S(2)}) copy-start(bf16[4096]{0:T(1024)(128)(2,1)} %param.6) | copy-start | bytes 24580
  22.4 11.0 %copy-start = (bf16[4096,256]{1,0:T(8,128)(2,1)S(1)}, bf16[4096,256]{1,0:T(8,128)(2,1)}, u32[]{:S(2)}) copy-start(bf16[4096,256]{1,0:T(8,128)(2,1)} %param.5) | copy-start | bytes 6291460
  22.4 11.0 %copy-start.2 = (bf16[32,8,128]{2,1,0:T(8,128)(2,1)S(1)}, bf16[32,8,128]{2,1,0:T(8,128)(2,1)}, u32[]{:S(2)}) copy-start(bf16[32,8,128]{2,1,0:T(8,128)(2,1)} %stack.35.sides) | copy-start | bytes 196612
  22.4 101.5 %all-to-all-start.1 = ((bf16[32,264,256]{2,1,0:T(8,128)(2,1)}), bf16[32,264,256]{2,1,0:T(8,128)(2,1)}, u32[]{:S(2)}, u32[]{:S(2)}) async-start(bf16[32,264,256]{2,1,0:T(8,128)(2,1)} %pack.1), calls=%async_computation.1 | async-start | bytes 8650752 | tf_op jit(solution)/shard_map/all_to_all | solution.py:38
  29.9 94.0 %copy-start.1 = (f32[32,4096]{1,0:T(8,128)S(1)}, f32[32,4096]{1,0:T(8,128)}, u32[]{:S(2)}) copy-start(f32[32,4096]{1,0:T(8,128)} %prev.3) | copy-start | bytes 1572868
  29.9 94.0 %copy-start.3 = (s32[64]{0:T(128)S(1)}, s32[64]{0:T(128)}, u32[]{:S(2)}) copy-start(s32[64]{0:T(128)} %reshape.395.send_index) | copy-start | bytes 772
  137.8 18.9 %all-to-all-start.2 = ((bf16[32,2,32,128]{3,2,1,0:T(8,128)(2,1)}), bf16[32,2,32,128]{3,2,1,0:T(8,128)(2,1)S(1)}, u32[]{:S(2)}, u32[]{:S(2)}) async-start(bf16[32,2,32,128]{3,2,1,0:T(8,128)(2,1)} %bitcast.21), calls=%async_computation.2 | async-start | bytes 1048576 | tf_op jit(solution)/shard_map/all_to_all | solution.py:38
  163.7 18.9 %all-to-all-start.3 = ((bf16[32,2,32,128]{3,2,1,0:T(8,128)(2,1)}), bf16[32,2,32,128]{3,2,1,0:T(8,128)(2,1)S(1)}, u32[]{:S(2)}, u32[]{:S(2)}) async-start(bf16[32,2,32,128]{3,2,1,0:T(8,128)(2,1)} %bitcast.23), calls=%async_computation.3 | async-start | bytes 1048576 | tf_op jit(solution)/shard_map/all_to_all | solution.py:38
  189.7 18.9 %all-to-all-start.4 = ((bf16[32,2,32,128]{3,2,1,0:T(8,128)(2,1)}), bf16[32,2,32,128]{3,2,1,0:T(8,128)(2,1)S(1)}, u32[]{:S(2)}, u32[]{:S(2)}) async-start(bf16[32,2,32,128]{3,2,1,0:T(8,128)(2,1)} %bitcast.25), calls=%async_computation.4 | async-start | bytes 1048576 | tf_op jit(solution)/shard_map/all_to_all | solution.py:38
  215.6 18.9 %all-to-all-start.5 = ((bf16[32,2,32,128]{3,2,1,0:T(8,128)(2,1)}), bf16[32,2,32,128]{3,2,1,0:T(8,128)(2,1)S(1)}, u32[]{:S(2)}, u32[]{:S(2)}) async-start(bf16[32,2,32,128]{3,2,1,0:T(8,128)(2,1)} %bitcast.27), calls=%async_computation.5 | async-start | bytes 1048576 | tf_op jit(solution)/shard_map/all_to_all | solution.py:38

commit v4 on v3

--- a/solution.py
+++ b/solution.py
@@ -15,6 +15,7 @@
 GROUP = 16
 STAGES = 4
 EXTRA = 8
+AHEAD = 8
 LIMIT = 50 * 1024 * 1024
 
 LOW_EDGE = 0.2
@@ -68,7 +69,7 @@
     def bands_of(d):
         return [
             pltpu.make_async_copy(
-                features.at[send_index[d * MOST + h]],
+                features.at[send_index[d, h]],
                 send.at[d, pl.ds(h * BAND, BAND)],
                 sems.at[h, d],
             )
@@ -83,7 +84,7 @@
     def first(d, carry):
         for copy in bands_of(d):
             copy.start()
-        tails[d] = jnp.concatenate([sides[send_index[d * MOST + h]] for h in range(MOST)], axis=1)
+        tails[d] = jnp.concatenate([sides[send_index[d, h]] for h in range(MOST)], axis=1)
         return carry
 
     def second(d, carry):
@@ -112,8 +113,8 @@
     )
 
 
-def tile_groups(work, count, rows, coords_of, cols, rvec, tiles, deg, stage, sems):
-    groups = (count[0] + GROUP - 1) // GROUP
+def tile_groups(work, rows, coords_of, cols, rvec, tiles, deg, stage, sems, between):
+    groups = (work[3, 0] + GROUP - 1) // GROUP
 
     def copy_of(group):
         slot = lax.rem(group, STAGES)
@@ -147,13 +148,14 @@
         return carry
 
     lax.fori_loop(0, groups, body, 0)
+    between()
     for back in range(STAGES, 0, -1):
         @pl.when(groups >= back)
         def _():
             copy_of(groups - back).wait()
 
 
-def local_kernel(work, count, rows, sides, rvec, tiles, deg, cols, stage, sems):
+def local_kernel(work, rows, sides, rvec, tiles, deg, cols, stage, sems):
     deg[...] = jnp.zeros(deg.shape, deg.dtype)
 
     def fill(band, carry):
@@ -161,46 +163,65 @@
         return carry
 
     lax.fori_loop(0, rows.shape[0], fill, 0, unroll=4)
-    tile_groups(work, count, rows, lambda entry: rows[entry], cols, rvec, tiles, deg, stage, sems)
-
-
-def pack_rows(send_index, scaled, send):
+    tile_groups(work, rows, lambda entry: rows[entry], cols, rvec, tiles, deg, stage, sems, lambda: None)
+
+
+def pack_rows(work, scaled, send):
     def one(at, carry):
-        send[at] = scaled[send_index[at]]
+        send[at] = scaled[work[4, at]]
         return carry
 
     lax.fori_loop(0, send.shape[0], one, 0, unroll=8)
 
 
-def remote_kernel(work, count, send_index, rows, got, rvec, deg_in, start,
-                  tiles, root, scaled, send, deg, cols, stage, sems):
+def remote_kernel(work_in, rows, got_in, rvec, deg_in, start,
+                  tiles, root, scaled, send, work, got, deg, cols, stage, sems, work_sem, got_sems):
+    work_copy = pltpu.make_async_copy(work_in, work, work_sem)
+    work_copy.start()
+
+    def copy_of(owner):
+        return pltpu.make_async_copy(got_in.at[owner], got.at[owner], got_sems.at[owner])
+
+    def begin(owner, carry):
+        copy_of(owner).start()
+        return carry
+
+    lax.fori_loop(0, got.shape[0], begin, 0)
     deg[...] = deg_in[...]
     tail = MOST * BAND
-
-    def fill(owner, carry):
-        for h in range(MOST):
-            side = got[owner, tail : tail + EXTRA, h * BAND : (h + 1) * BAND]
-            cols[owner * MOST + h] = spread_column(side)
-        return carry
-
-    lax.fori_loop(0, got.shape[0], fill, 0, unroll=4)
+    step = 4
+
+    def fill(part, carry):
+        for k in range(step):
+            copy_of(part * step + k).wait()
+        for k in range(step):
+            owner = part * step + k
+            for h in range(MOST):
+                side = got[owner, tail : tail + EXTRA, h * BAND : (h + 1) * BAND]
+                cols[owner * MOST + h] = spread_column(side)
+        return carry
+
+    lax.fori_loop(0, got.shape[0] // step, fill, 0)
+    work_copy.wait()
 
     def coords_of(entry):
         at = pl.multiple_of(lax.rem(entry, MOST) * BAND, BAND)
         return got[entry // MOST, pl.ds(at, BAND), :]
 
-    tile_groups(work, count, rows, coords_of, cols, rvec, tiles, deg, stage, sems)
-    for band in range(deg.shape[0]):
-        total = jnp.sum(deg[band], axis=0, keepdims=True)
-        inverse = 1.0 / jnp.sqrt(total)
-        root[band : band + 1, :] = inverse
-        block = start[:, band * BAND : (band + 1) * BAND]
-        scaled[band] = (block * inverse).astype(jnp.bfloat16)
-    pack_rows(send_index, scaled, send)
-
-
-def gather_product(work, count, table, tiles, total, held, sems):
-    groups = (count[0] + GROUP - 1) // GROUP
+    def between():
+        for band in range(deg.shape[0]):
+            total = jnp.sum(deg[band], axis=0, keepdims=True)
+            inverse = 1.0 / jnp.sqrt(total)
+            root[band : band + 1, :] = inverse
+            block = start[:, band * BAND : (band + 1) * BAND]
+            scaled[band] = (block * inverse).astype(jnp.bfloat16)
+        pack_rows(work, scaled, send)
+
+    tile_groups(work, rows, coords_of, cols, rvec, tiles, deg, stage, sems, between)
+
+
+def gather_product(work_in, table, tiles, total, work, held, work_sem, sems):
+    work_copy = pltpu.make_async_copy(work_in, work, work_sem)
 
     def copy_of(group):
         part = pl.ds(group * GROUP, GROUP)
@@ -219,13 +240,24 @@
             )
         return carry
 
-    lax.fori_loop(0, groups, begin, 0)
+    def spare(group, carry):
+        copy_of(group).wait()
+        return carry
+
+    ahead = min(AHEAD, sems.shape[0])
+    work_copy.start()
+    for group in range(ahead):
+        copy_of(group).start()
+    work_copy.wait()
+    groups = (work[3, 0] + GROUP - 1) // GROUP
+    lax.fori_loop(ahead, groups, begin, 0)
     lax.fori_loop(0, groups, body, 0)
-
-
-def own_kernel(work, count, scaled, tiles, total, held, sems):
+    lax.fori_loop(groups, ahead, spare, 0)
+
+
+def own_kernel(work_in, scaled, tiles, total, work, held, work_sem, sems):
     total[...] = jnp.zeros(total.shape, total.dtype)
-    gather_product(work, count, scaled, tiles, total, held, sems)
+    gather_product(work_in, scaled, tiles, total, work, held, work_sem, sems)
 
 
 def fold(square):
@@ -236,14 +268,13 @@
     return jnp.concatenate([packed[:, side * q : side * (q + 1)] for q in range(side // 8)], axis=0)
 
 
-def round_kernel(first, last, gains, work, count, send_index, got, total_in, root, cur, prev, tiles,
-                 following, *rest):
+def round_kernel(first, last, gains, work_in, got, total_in, root, cur, prev, tiles, following, *rest):
     if last:
-        gram, total, held, sems = rest
+        gram, total, work, held, work_sem, sems = rest
     else:
-        scaled, send, total, held, sems = rest
+        scaled, send, total, work, held, work_sem, sems = rest
     total[...] = total_in[...]
-    gather_product(work, count, got, tiles, total, held, sems)
+    gather_product(work_in, got, tiles, total, work, held, work_sem, sems)
     own, mixed_gain, old = gains
     for band in range(total.shape[0]):
         inverse = root[band : band + 1, :]
@@ -262,7 +293,7 @@
         )
         gram[...] = jnp.broadcast_to(fold(square)[None], gram.shape)
     else:
-        pack_rows(send_index, scaled, send)
+        pack_rows(work, scaled, send)
 
 
 def finish_kernel(total_rows, parts, flat, basis, factor):
@@ -318,7 +349,7 @@
     )
     send_index = jnp.sum(
         picks.astype(jnp.int32) * jnp.arange(bands, dtype=jnp.int32)[None, None, :], axis=2
-    ).reshape(-1)
+    )
 
     feature_bands = features.reshape(bands, BAND, dims)
     widths = inv_width.reshape(bands, BAND).astype(jnp.float32)
@@ -340,6 +371,7 @@
             pltpu.VMEM((devices, EXTRA, dims), jnp.bfloat16),
             pltpu.SemaphoreType.DMA((MOST + 1, devices)),
         ],
+        compiler_params=pltpu.CompilerParams(vmem_limit_bytes=LIMIT),
         name="pack",
     )(send_index, feature_bands, sides)
     got_coords = exchange(send_coords)
@@ -362,13 +394,18 @@
         entry = jnp.sum(hit * entry_of[None, :], axis=1)
         count = jnp.sum(ones)
         keep = (order < count).astype(jnp.int32)
-        return jnp.stack([tile_id % bands, entry, keep]), count.reshape(1)
-
-    near_work, near_count = work_list(active & ~far)
-    far_work, far_count = work_list(far)
+        rows = jnp.stack([tile_id % bands, entry, keep, jnp.broadcast_to(count, order.shape)])
+        rows = jnp.pad(rows, ((0, 0), (0, width - count_all)))
+        return jnp.concatenate([rows, send_row], axis=0)
+
+    width = -(-max(count_all, entries) // BAND) * BAND
+    send_row = jnp.pad(send_index.reshape(1, entries), ((0, 0), (0, width - entries)))
+    near_work = work_list(active & ~far)
+    far_work = work_list(far)
 
     rvec = jnp.stack([0.5 * squares, (2.0 * math.log2(math.e)) * widths], axis=1)
 
+    work_space = pltpu.SMEM(far_work.shape, jnp.int32)
     tile_shape = jax.ShapeDtypeStruct((count_all, BAND, BAND), jnp.bfloat16)
 
     def building(columns):
@@ -386,33 +423,39 @@
     near_tiles, deg = pl.pallas_call(
         local_kernel,
         out_shape=(tile_shape, jax.ShapeDtypeStruct((bands, 8, BAND), jnp.float32)),
-        in_specs=[whole(SMEM)] * 2 + [whole()] * 3,
+        in_specs=[whole(SMEM)] + [whole()] * 3,
         out_specs=(whole(pl.ANY), whole()),
         scratch_shapes=building(bands),
         cost_estimate=build_cost,
         compiler_params=pltpu.CompilerParams(vmem_limit_bytes=LIMIT),
         name="local_tiles",
-    )(near_work, near_count, feature_bands, sides, rvec)
+    )(near_work, feature_bands, sides, rvec)
 
     row_shape = jax.ShapeDtypeStruct((bands, vectors, BAND), jnp.bfloat16)
     send_shape = jax.ShapeDtypeStruct((entries, vectors, BAND), jnp.bfloat16)
     far_tiles, root, scaled, send = pl.pallas_call(
         remote_kernel,
         out_shape=(tile_shape, jax.ShapeDtypeStruct((bands, BAND), jnp.float32), row_shape, send_shape),
-        in_specs=[whole(SMEM)] * 3 + [whole()] * 5,
+        in_specs=[whole(pltpu.HBM), whole(), whole(pltpu.HBM)] + [whole()] * 3,
         out_specs=(whole(pl.ANY), whole(), whole(), whole()),
-        scratch_shapes=[pltpu.VMEM((bands, 8, BAND), jnp.float32)] + building(entries),
+        scratch_shapes=[
+            work_space,
+            pltpu.VMEM(send_coords.shape, jnp.bfloat16),
+            pltpu.VMEM((bands, 8, BAND), jnp.float32),
+        ] + building(entries) + [pltpu.SemaphoreType.DMA, pltpu.SemaphoreType.DMA((devices,))],
         cost_estimate=build_cost,
         compiler_params=pltpu.CompilerParams(vmem_limit_bytes=max(LIMIT, remote_bytes)),
         name="remote_tiles",
-    )(far_work, far_count, send_index, feature_bands, got_coords, rvec, deg, start_block)
+    )(far_work, feature_bands, got_coords, rvec, deg, start_block)
 
     centre, halfwidth, values = chebyshev_terms()
     flat_shape = jax.ShapeDtypeStruct((vectors, bands * BAND), jnp.float32)
     total_shape = jax.ShapeDtypeStruct((bands, vectors, BAND), jnp.float32)
     gram_shape = jax.ShapeDtypeStruct((devices, 8, vectors * vectors // 8), jnp.float32)
     fetching = [
+        work_space,
         pltpu.VMEM((count_all, BAND, BAND), jnp.bfloat16),
+        pltpu.SemaphoreType.DMA,
         pltpu.SemaphoreType.DMA((count_all // GROUP,)),
     ]
     product_cost = pl.CostEstimate(
@@ -431,24 +474,24 @@
         own_total = pl.pallas_call(
             own_kernel,
             out_shape=total_shape,
-            in_specs=[whole(SMEM)] * 2 + [whole(), whole(pl.ANY)],
+            in_specs=[whole(pltpu.HBM), whole(), whole(pltpu.HBM)],
             out_specs=whole(),
             scratch_shapes=fetching,
             cost_estimate=product_cost,
             compiler_params=pltpu.CompilerParams(vmem_limit_bytes=LIMIT),
             name="own" + str(power),
-        )(near_work, near_count, scaled, near_tiles)
+        )(near_work, scaled, near_tiles)
         outs = (flat_shape, gram_shape) if last else (flat_shape, row_shape, send_shape)
         results = pl.pallas_call(
             functools.partial(round_kernel, first, last, gains),
             out_shape=outs,
-            in_specs=[whole(SMEM)] * 3 + [whole()] * 5 + [whole(pl.ANY)],
+            in_specs=[whole(pltpu.HBM)] + [whole()] * 5 + [whole(pltpu.HBM)],
             out_specs=tuple([whole()] * len(outs)),
             scratch_shapes=[pltpu.VMEM((bands, vectors, BAND), jnp.float32)] + fetching,
             cost_estimate=product_cost,
             compiler_params=pltpu.CompilerParams(vmem_limit_bytes=LIMIT),
             name="round" + str(power),
-        )(far_work, far_count, send_index, got, own_total, root, current, previous, far_tiles)
+        )(far_work, got, own_total, root, current, previous, far_tiles)
         previous, current = current, results[0]
         if last:
             parts = exchange(results[1])

time: 257 us -> 250 us (0.973)
  Pallas kernels: 88.7 us -> 73.1 us
  waiting for transfers between devices: 122 us -> 127 us
    pallas_call x4, Pallas kernels: 27.9 us -> 21.7 us  [on_device(): pl.pallas_call(functools.partial(round_kernel, first, last, gains), out_s...]
    all_to_all x6, waiting for transfers between devices: 122 us -> 127 us  [exchange(): return lax.all_to_all(blocks, AXES, split_axis=0, concat_axis=0, tiled=True)]
    pallas_call x4, Pallas kernels: 25.2 us -> 19.8 us  [on_device(): pl.pallas_call(own_kernel, out_shape=total_shape, in_specs=[whole(pltpu.H...]
  transfers between devices with their start and end apart: 6 -> 6, of which waited for: 6 -> 6; matrix products, arithmetic and copies ran while one was open for 5% -> 5% of each run, Pallas kernels for 14% -> 12%
where the time goes in v4:
time: 250 us; the launch traced here: 248 us
  waiting for transfers between devices  127 us (51%)
  Pallas kernels  73.1 us (29%)
  starting transfers between devices  21.5 us (9%)
  blocking collectives  10.4 us (4%)
  other arithmetic  7.29 us (3%)
  local copies, waits for them, and re-layouts  7.11 us (3%)
    all_to_all x6, waiting for transfers between devices, exchange(): return lax.all_to_all(blocks, AXES, split_axis=0, concat_axis=0, tiled=True)  127 us
    pallas_call x4, Pallas kernels, on_device(): pl.pallas_call(functools.partial(round_kernel, first, last, gains), out_s...  21.7 us
    all_to_all x6, starting transfers between devices, exchange(): return lax.all_to_all(blocks, AXES, split_axis=0, concat_axis=0, tiled=True)  21.5 us
    pallas_call x4, Pallas kernels, on_device(): pl.pallas_call(own_kernel, out_shape=total_shape, in_specs=[whole(pltpu.H...  19.8 us
    pallas_call x1, Pallas kernels, on_device(): pl.pallas_call(remote_kernel, out_shape=(tile_shape, jax.ShapeDtypeStruct...  11.7 us
    all_to_all x1, blocking collectives, exchange(): return lax.all_to_all(blocks, AXES, split_axis=0, concat_axis=0, tiled=True)  10.4 us
    pallas_call x1, Pallas kernels, on_device(): pl.pallas_call(local_kernel, out_shape=(tile_shape, jax.ShapeDtypeStruct(...  10.3 us
  transfers between devices with their start and end apart: 6, of which 6 were waited for; matrix products, arithmetic and copies ran while one was open for 5% of the time, Pallas kernels for 12%

profile of v4, /device:TPU:0, one launch (start us, length us, event | category | flops | bytes accessed | tf_op | source)
XLA Modules:
  0.0 247.5 jit_solution(9514067732492009067)
XLA Ops:
  0.6 1.6 need.1
  2.2 7.3 %all-to-all-start = ((s32[32,1,32]{2,1,0:T(1,128)}), s32[32,1,32]{2,1,0:T(1,128)S(1)}, u32[]{:S(2)}, u32[]{:S(2)}) async-start(s32[32,1,32]{2,1,0:T(1,128)} %bitcast.47), calls=%async_computation | async-start | bytes 32768 | tf_op jit(solution)/shard_map/all_to_all | solution.py:39
  9.6 2.2 multiply_reduce_fusion
  11.8 0.7 bitcast_convert_fusion
  12.5 0.7 copy.26
  13.3 0.1 stack.13.sides
  13.4 3.3 %all-to-all-done = s32[32,1,32]{2,1,0:T(1,128)S(1)} async-done(((s32[32,1,32]{2,1,0:T(1,128)}), s32[32,1,32]{2,1,0:T(1,128)S(1)}, u32[]{:S(2)}, u32[]{:S(2)}) %all-to-all-start) | async-done | bytes 4128 | tf_op jit(solution)/shard_map/all_to_all | solution.py:39
  16.7 0.2 reduce_window_sum.51
  16.9 0.1 select_reduce_fusion.4
  17.0 0.1 copy.24.send_index
  17.1 1.6 copy-done
  18.7 3.8 %pack.1 = bf16[32,264,256]{2,1,0:T(8,128)(2,1)} custom-call(s32[32,2]{1,0:T(8,128)S(1)} %copy.24.send_index, bf16[32,128,256]{2,1,0:T(8,128)(2,1)S(1)} %bitcast.36, bf16[32,8,128]{2,1,0:T(8,128)(2,1)S(1)} %stack.13.sides), custom_call_target="tpu_custom_call" | custom-call | tf_op jit(solution)/shard_map/pack/pallas_call | solution.py:365
  22.5 0.0 copy-start.4
  22.5 0.0 copy-start.6
  22.5 0.0 copy-start.3
  22.5 0.0 copy-start.5
  22.5 0.0 copy-start.1
  22.6 3.7 %all-to-all-start.1 = ((bf16[32,264,256]{2,1,0:T(8,128)(2,1)}), bf16[32,264,256]{2,1,0:T(8,128)(2,1)}, u32[]{:S(2)}, u32[]{:S(2)}) async-start(bf16[32,264,256]{2,1,0:T(8,128)(2,1)} %pack.1), calls=%async_computation.1 | async-start | bytes 8650752 | tf_op jit(solution)/shard_map/all_to_all | solution.py:39
  26.3 0.0 copy-done.4
  26.3 0.1 reshape.387
  26.4 0.1 reshape.385
  26.4 0.0 copy-done.6
  26.5 0.1 eq.75
  26.5 0.1 eq.79
  26.6 0.0 copy-done.3
  26.6 0.2 reduce_window_sum.49
  26.8 0.3 reduce-window.16
  27.2 0.3 reduce-window.24
  27.5 0.1 slice.16
  27.6 0.1 slice.14
  27.7 0.1 sub.57
  27.8 2.3 gather_fusion
  30.1 0.0 copy-start.2
  30.1 0.6 convert_reduce_fusion
  30.7 1.3 compare_convert_fusion
  32.0 0.1 slice_reduce_fusion
  32.1 0.1 slice_reduce_fusion.1
  32.4 0.1 add_bitcast_fusion
  32.4 1.0 select_reduce_fusion
  33.5 0.1 reshape.388
  33.6 0.6 lt.42
  34.3 0.6 lt.45
  35.0 0.0 copy-done.1
  35.0 10.3 %local_tiles.1 = (bf16[512,128,128]{2,1,0:T(8,128)(2,1)}, f32[32,8,128]{2,1,0:T(8,128)S(1)}) custom-call(s32[5,512]{1,0:T(8,128)S(1)} %concatenate.9.work.work_in, bf16[32,128,256]{2,1,0:T(8,128)(2,1)S(1)} %bitcast.37, bf16[32,8,128]{2,1,0:T(8,128)(2,1)S(1)} %stack.13.sides, f32[32,2,128]{2,1,0:T(2,128)S(1)} %pad_maximum_fusion.rvec), custom_call_target="tpu_custom_call" | custom-call | flops 2147483648 | bytes 8388608 | tf_op jit(solution)/shard_map/local_tiles/pallas_call | solution.py:423
  45.3 78.7 %all-to-all-done.1.got_in = bf16[32,264,256]{2,1,0:T(8,128)(2,1)} async-done(((bf16[32,264,256]{2,1,0:T(8,128)(2,1)}), bf16[32,264,256]{2,1,0:T(8,128)(2,1)}, u32[]{:S(2)}, u32[]{:S(2)}) %all-to-all-start.1) | async-done | bytes 4325408 | tf_op jit(solution)/shard_map/all_to_all | solution.py:39
  124.0 11.7 %remote_tiles.1 = (bf16[512,128,128]{2,1,0:T(8,128)(2,1)}, f32[32,128]{1,0:T(8,128)S(1)}, bf16[32,32,128]{2,1,0:T(8,128)(2,1)S(1)}, bf16[64,32,128]{2,1,0:T(8,128)(2,1)}) custom-call(s32[5,512]{1,0:T(8,128)S(1)} %concatenate.8.work_in, bf16[32,128,256]{2,1,0:T(8,128)(2,1)S(1)} %bitcast.38, bf16[32,264,256]{2,1,0:T(8,128)(2,1)} %all-to-all-done.1.got_in, ...), custom_call_target="tpu_custom_call" | custom-call | flops 2147483648 | bytes 8388608 | tf_op jit(solution)/shard_map/remote_tiles/pallas_call | solution.py:436
  135.7 2.6 %all-to-all-start.2 = ((bf16[32,2,32,128]{3,2,1,0:T(8,128)(2,1)}), bf16[32,2,32,128]{3,2,1,0:T(8,128)(2,1)S(1)}, u32[]{:S(2)}, u32[]{:S(2)}) async-start(bf16[32,2,32,128]{3,2,1,0:T(8,128)(2,1)} %bitcast.19), calls=%async_computation.2 | async-start | bytes 1048576 | tf_op jit(solution)/shard_map/all_to_all | solution.py:39
  138.3 5.0 %own0.1.total_in = f32[32,32,128]{2,1,0:T(8,128)S(1)} custom-call(s32[5,512]{1,0:T(8,128)S(1)} %concatenate.9.work.work_in, bf16[32,32,128]{2,1,0:T(8,128)(2,1)S(1)} %get-tuple-element.21.scaled, bf16[512,128,128]{2,1,0:T(8,128)(2,1)} %get-tuple-element.22.tiles), custom_call_target="tpu_custom_call" | custom-call | flops 268435456 | bytes 8388608 | tf_op jit(solution)/shard_map/own0/pallas_call | solution.py:474
  143.3 11.3 %all-to-all-done.2 = bf16[32,2,32,128]{3,2,1,0:T(8,128)(2,1)S(1)} async-done(((bf16[32,2,32,128]{3,2,1,0:T(8,128)(2,1)}), bf16[32,2,32,128]{3,2,1,0:T(8,128)(2,1)S(1)}, u32[]{:S(2)}, u32[]{:S(2)}) %all-to-all-start.2) | async-done | bytes 524320 | tf_op jit(solution)/shard_map/all_to_all | solution.py:39
  154.6 5.5 %round0.1 = (f32[32,4096]{1,0:T(8,128)S(1)}, bf16[32,32,128]{2,1,0:T(8,128)(2,1)S(1)}, bf16[64,32,128]{2,1,0:T(8,128)(2,1)}) custom-call(s32[5,512]{1,0:T(8,128)S(1)} %concatenate.8.work_in, bf16[64,32,128]{2,1,0:T(8,128)(2,1)S(1)} %bitcast.40, f32[32,32,128]{2,1,0:T(8,128)S(1)} %own0.1.total_in, f32[32,128]{1,0:T(8,128)S(1)} %get-tuple-element.23.root, ...), custom_call_target="tpu_custom_call" | custom-call | flops 268435456 | bytes 8388608 | tf_op jit(solution)/shard_map/round0/pallas_call | solution.py:485
  160.1 2.6 %all-to-all-start.3 = ((bf16[32,2,32,128]{3,2,1,0:T(8,128)(2,1)}), bf16[32,2,32,128]{3,2,1,0:T(8,128)(2,1)S(1)}, u32[]{:S(2)}, u32[]{:S(2)}) async-start(bf16[32,2,32,128]{3,2,1,0:T(8,128)(2,1)} %bitcast.21), calls=%async_computation.3 | async-start | bytes 1048576 | tf_op jit(solution)/shard_map/all_to_all | solution.py:39
  162.7 5.0 %own1.1.total_in = f32[32,32,128]{2,1,0:T(8,128)S(1)} custom-call(s32[5,512]{1,0:T(8,128)S(1)} %concatenate.9.work.work_in, bf16[32,32,128]{2,1,0:T(8,128)(2,1)S(1)} %get-tuple-element.26.scaled, bf16[512,128,128]{2,1,0:T(8,128)(2,1)} %get-tuple-element.22.tiles), custom_call_target="tpu_custom_call" | custom-call | flops 268435456 | bytes 8388608 | tf_op jit(solution)/shard_map/own1/pallas_call | solution.py:474
  167.7 11.3 %all-to-all-done.3 = bf16[32,2,32,128]{3,2,1,0:T(8,128)(2,1)S(1)} async-done(((bf16[32,2,32,128]{3,2,1,0:T(8,128)(2,1)}), bf16[32,2,32,128]{3,2,1,0:T(8,128)(2,1)S(1)}, u32[]{:S(2)}, u32[]{:S(2)}) %all-to-all-start.3) | async-done | bytes 524320 | tf_op jit(solution)/shard_map/all_to_all | solution.py:39
  179.0 5.5 %round1.1 = (f32[32,4096]{1,0:T(8,128)S(1)}, bf16[32,32,128]{2,1,0:T(8,128)(2,1)S(1)}, bf16[64,32,128]{2,1,0:T(8,128)(2,1)}) custom-call(s32[5,512]{1,0:T(8,128)S(1)} %concatenate.8.work_in, bf16[64,32,128]{2,1,0:T(8,128)(2,1)S(1)} %bitcast.42, f32[32,32,128]{2,1,0:T(8,128)S(1)} %own1.1.total_in, f32[32,128]{1,0:T(8,128)S(1)} %get-tuple-element.23.root, ...), custom_call_target="tpu_custom_call" | custom-call | flops 268435456 | bytes 8388608 | tf_op jit(solution)/shard_map/round1/pallas_call | solution.py:485
  184.5 2.6 %all-to-all-start.4 = ((bf16[32,2,32,128]{3,2,1,0:T(8,128)(2,1)}), bf16[32,2,32,128]{3,2,1,0:T(8,128)(2,1)S(1)}, u32[]{:S(2)}, u32[]{:S(2)}) async-start(bf16[32,2,32,128]{3,2,1,0:T(8,128)(2,1)} %bitcast.23), calls=%async_computation.4 | async-start | bytes 1048576 | tf_op jit(solution)/shard_map/all_to_all | solution.py:39
  187.2 5.0 %own2.1.total_in = f32[32,32,128]{2,1,0:T(8,128)S(1)} custom-call(s32[5,512]{1,0:T(8,128)S(1)} %concatenate.9.work.work_in, bf16[32,32,128]{2,1,0:T(8,128)(2,1)S(1)} %get-tuple-element.29.scaled, bf16[512,128,128]{2,1,0:T(8,128)(2,1)} %get-tuple-element.22.tiles), custom_call_target="tpu_custom_call" | custom-call | flops 268435456 | bytes 8388608 | tf_op jit(solution)/shard_map/own2/pallas_call | solution.py:474
  192.1 11.3 %all-to-all-done.4 = bf16[32,2,32,128]{3,2,1,0:T(8,128)(2,1)S(1)} async-done(((bf16[32,2,32,128]{3,2,1,0:T(8,128)(2,1)}), bf16[32,2,32,128]{3,2,1,0:T(8,128)(2,1)S(1)}, u32[]{:S(2)}, u32[]{:S(2)}) %all-to-all-start.4) | async-done | bytes 524320 | tf_op jit(solution)/shard_map/all_to_all | solution.py:39
  203.4 5.5 %round2.1 = (f32[32,4096]{1,0:T(8,128)S(1)}, bf16[32,32,128]{2,1,0:T(8,128)(2,1)S(1)}, bf16[64,32,128]{2,1,0:T(8,128)(2,1)}) custom-call(s32[5,512]{1,0:T(8,128)S(1)} %concatenate.8.work_in, bf16[64,32,128]{2,1,0:T(8,128)(2,1)S(1)} %bitcast.41, f32[32,32,128]{2,1,0:T(8,128)S(1)} %own2.1.total_in, f32[32,128]{1,0:T(8,128)S(1)} %get-tuple-element.23.root, ...), custom_call_target="tpu_custom_call" | custom-call | flops 268435456 | bytes 8388608 | tf_op jit(solution)/shard_map/round2/pallas_call | solution.py:485
  208.9 2.6 %all-to-all-start.5 = ((bf16[32,2,32,128]{3,2,1,0:T(8,128)(2,1)}), bf16[32,2,32,128]{3,2,1,0:T(8,128)(2,1)S(1)}, u32[]{:S(2)}, u32[]{:S(2)}) async-start(bf16[32,2,32,128]{3,2,1,0:T(8,128)(2,1)} %bitcast.25), calls=%async_computation.5 | async-start | bytes 1048576 | tf_op jit(solution)/shard_map/all_to_all | solution.py:39
  211.6 5.0 %own3.1.total_in = f32[32,32,128]{2,1,0:T(8,128)S(1)} custom-call(s32[5,512]{1,0:T(8,128)S(1)} %concatenate.9.work.work_in, bf16[32,32,128]{2,1,0:T(8,128)(2,1)S(1)} %get-tuple-element.32.scaled, bf16[512,128,128]{2,1,0:T(8,128)(2,1)} %get-tuple-element.22.tiles), custom_call_target="tpu_custom_call" | custom-call | flops 268435456 | bytes 8388608 | tf_op jit(solution)/shard_map/own3/pallas_call | solution.py:474
  216.5 11.3 %all-to-all-done.5 = bf16[32,2,32,128]{3,2,1,0:T(8,128)(2,1)S(1)} async-done(((bf16[32,2,32,128]{3,2,1,0:T(8,128)(2,1)}), bf16[32,2,32,128]{3,2,1,0:T(8,128)(2,1)S(1)}, u32[]{:S(2)}, u32[]{:S(2)}) %all-to-all-start.5) | async-done | bytes 524320 | tf_op jit(solution)/shard_map/all_to_all | solution.py:39
  227.8 5.1 %round3.1 = (f32[32,4096]{1,0:T(8,128)S(1)}, f32[32,8,128]{2,1,0:T(8,128)S(1)}) custom-call(s32[5,512]{1,0:T(8,128)S(1)} %concatenate.8.work_in, bf16[64,32,128]{2,1,0:T(8,128)(2,1)S(1)} %bitcast.39, f32[32,32,128]{2,1,0:T(8,128)S(1)} %own3.1.total_in, f32[32,128]{1,0:T(8,128)S(1)} %get-tuple-element.23.root, f32[32,4096]{1,0:T(8,128)S(1)} %get-tuple-element.33.cur, ...), custom_call_target="tpu_custom_call" | custom-call | flops 268435456 | bytes 8388608 | tf_op jit(solution)/shard_map/round3/pallas_call | solution.py:485
  232.9 10.4 %all_to_all.39.parts = f32[32,8,128]{2,1,0:T(8,128)S(1)} all-to-all(f32[32,8,128]{2,1,0:T(8,128)S(1)} %get-tuple-element.34), channel_id=1, replica_groups=mesh['gx'=4,'gy'=8] {'gx','gy'}, dimensions={0} | all-to-all | bytes 262144 | tf_op jit(solution)/shard_map/all_to_all | solution.py:39
  243.3 4.2 %finish.1 = (f32[32,4096]{1,0:T(8,128)}, f32[32,32]{1,0:T(8,128)}) custom-call(f32[32,8,128]{2,1,0:T(8,128)S(1)} %all_to_all.39.parts, f32[32,4096]{1,0:T(8,128)S(1)} %get-tuple-element.35.flat), custom_call_target="tpu_custom_call" | custom-call | tf_op jit(solution)/shard_map/finish/pallas_call | solution.py:501
  (25 shorter events, 0.4 us)
Async XLA Ops:
  2.2 14.4 %all-to-all-start = ((s32[32,1,32]{2,1,0:T(1,128)}), s32[32,1,32]{2,1,0:T(1,128)S(1)}, u32[]{:S(2)}, u32[]{:S(2)}) async-start(s32[32,1,32]{2,1,0:T(1,128)} %bitcast.47), calls=%async_computation | async-start | bytes 32768 | tf_op jit(solution)/shard_map/all_to_all | solution.py:39
  17.1 1.6 copy-start
  22.5 3.8 %copy-start.4 = (s32[32,16]{0,1:T(8,128)S(1)}, s32[32,16]{0,1:T(8,128)}, u32[]{:S(2)}) copy-start(s32[32,16]{0,1:T(8,128)} %param.8) | copy-start | bytes 6148
  22.5 3.9 %copy-start.6 = (s32[32,16]{0,1:T(8,128)S(1)}, s32[32,16]{0,1:T(8,128)}, u32[]{:S(2)}) copy-start(s32[32,16]{0,1:T(8,128)} %param.9) | copy-start | bytes 6148
  22.5 4.1 %copy-start.3 = (s32[32,32]{1,0:T(8,128)S(1)}, s32[32,32]{1,0:T(8,128)}, u32[]{:S(2)}) copy-start(s32[32,32]{1,0:T(8,128)} %need.1) | copy-start | bytes 12292
  22.5 9.7 %copy-start.5 = (bf16[4096]{0:T(1024)(128)(2,1)S(1)}, bf16[4096]{0:T(1024)(128)(2,1)}, u32[]{:S(2)}) copy-start(bf16[4096]{0:T(1024)(128)(2,1)} %param.6) | copy-start | bytes 24580
  22.5 12.4 %copy-start.1 = (bf16[4096,256]{1,0:T(8,128)(2,1)S(1)}, bf16[4096,256]{1,0:T(8,128)(2,1)}, u32[]{:S(2)}) copy-start(bf16[4096,256]{1,0:T(8,128)(2,1)} %param.5) | copy-start | bytes 6291460
  22.6 101.5 %all-to-all-start.1 = ((bf16[32,264,256]{2,1,0:T(8,128)(2,1)}), bf16[32,264,256]{2,1,0:T(8,128)(2,1)}, u32[]{:S(2)}, u32[]{:S(2)}) async-start(bf16[32,264,256]{2,1,0:T(8,128)(2,1)} %pack.1), calls=%async_computation.1 | async-start | bytes 8650752 | tf_op jit(solution)/shard_map/all_to_all | solution.py:39
  30.1 94.0 %copy-start.2 = (f32[32,4096]{1,0:T(8,128)S(1)}, f32[32,4096]{1,0:T(8,128)}, u32[]{:S(2)}) copy-start(f32[32,4096]{1,0:T(8,128)} %prev.3) | copy-start | bytes 1572868
  135.7 18.9 %all-to-all-start.2 = ((bf16[32,2,32,128]{3,2,1,0:T(8,128)(2,1)}), bf16[32,2,32,128]{3,2,1,0:T(8,128)(2,1)S(1)}, u32[]{:S(2)}, u32[]{:S(2)}) async-start(bf16[32,2,32,128]{3,2,1,0:T(8,128)(2,1)} %bitcast.19), calls=%async_computation.2 | async-start | bytes 1048576 | tf_op jit(solution)/shard_map/all_to_all | solution.py:39
  160.1 18.9 %all-to-all-start.3 = ((bf16[32,2,32,128]{3,2,1,0:T(8,128)(2,1)}), bf16[32,2,32,128]{3,2,1,0:T(8,128)(2,1)S(1)}, u32[]{:S(2)}, u32[]{:S(2)}) async-start(bf16[32,2,32,128]{3,2,1,0:T(8,128)(2,1)} %bitcast.21), calls=%async_computation.3 | async-start | bytes 1048576 | tf_op jit(solution)/shard_map/all_to_all | solution.py:39
  184.5 18.9 %all-to-all-start.4 = ((bf16[32,2,32,128]{3,2,1,0:T(8,128)(2,1)}), bf16[32,2,32,128]{3,2,1,0:T(8,128)(2,1)S(1)}, u32[]{:S(2)}, u32[]{:S(2)}) async-start(bf16[32,2,32,128]{3,2,1,0:T(8,128)(2,1)} %bitcast.23), calls=%async_computation.4 | async-start | bytes 1048576 | tf_op jit(solution)/shard_map/all_to_all | solution.py:39
  208.9 18.9 %all-to-all-start.5 = ((bf16[32,2,32,128]{3,2,1,0:T(8,128)(2,1)}), bf16[32,2,32,128]{3,2,1,0:T(8,128)(2,1)S(1)}, u32[]{:S(2)}, u32[]{:S(2)}) async-start(bf16[32,2,32,128]{3,2,1,0:T(8,128)(2,1)} %bitcast.25), calls=%async_computation.5 | async-start | bytes 1048576 | tf_op jit(solution)/shard_map/all_to_all | solution.py:39

commit v5 on v4

--- a/solution.py
+++ b/solution.py
@@ -12,10 +12,10 @@
 BAND = 128
 MOST = 2
 DEGREE = 4
-GROUP = 16
-STAGES = 4
+GROUP = 32
+STAGES = 3
 EXTRA = 8
-AHEAD = 8
+AHEAD = 4
 LIMIT = 50 * 1024 * 1024
 
 LOW_EDGE = 0.2
@@ -61,6 +61,36 @@
         preferred_element_type=jnp.float32,
     )
     need[...] = jnp.where(count > 0.0, 1, 0).astype(jnp.int32)
+
+
+def sides_kernel(features, widths, copied, sides, rvec):
+    dims = features.shape[2]
+    ones = jnp.ones((EXTRA, dims), jnp.bfloat16)
+    row = lax.broadcasted_iota(jnp.int32, (EXTRA, BAND), 0)
+
+    def row_sums(part):
+        return lax.dot_general(
+            ones, part, (((1,), (1,)), ((), ())), preferred_element_type=jnp.float32
+        )
+
+    for band in range(features.shape[0]):
+        block = features[band]
+        copied[band] = block
+        wide = block.astype(jnp.float32)
+        exact = wide * wide
+        high = exact.astype(jnp.bfloat16)
+        low = (exact - high.astype(jnp.float32)).astype(jnp.bfloat16)
+        half = 0.5 * (row_sums(high) + row_sums(low))
+        width = jnp.broadcast_to(widths[band : band + 1, :], (EXTRA, BAND))
+        product = half * width
+        first = product.astype(jnp.bfloat16).astype(jnp.float32)
+        left = product - first
+        second = left.astype(jnp.bfloat16).astype(jnp.float32)
+        third = left - second
+        side = jnp.where(row == 0, width, jnp.where(row == 1, first, 0.0))
+        side = jnp.where(row == 2, second, jnp.where(row == 3, third, side))
+        sides[band] = side.astype(jnp.bfloat16)
+        rvec[band] = jnp.where(row == 0, half, (2.0 * math.log2(math.e)) * width)
 
 
 def pack_kernel(send_index, features, sides, send, tails, sems):
@@ -353,15 +383,21 @@
 
     feature_bands = features.reshape(bands, BAND, dims)
     widths = inv_width.reshape(bands, BAND).astype(jnp.float32)
-    squares = jnp.sum(jnp.square(feature_bands.astype(jnp.float32)), axis=2)
-    product = 0.5 * squares * widths
-    high = lax.reduce_precision(product, 8, 7)
-    rest = product - high
-    middle = lax.reduce_precision(rest, 8, 7)
-    blank = jnp.zeros_like(widths)
-    sides = jnp.stack(
-        [widths, high, middle, rest - middle] + [blank] * (EXTRA - 4), axis=1
-    ).astype(jnp.bfloat16)
+    copied, sides, rvec = pl.pallas_call(
+        sides_kernel,
+        out_shape=(
+            jax.ShapeDtypeStruct(feature_bands.shape, jnp.bfloat16),
+            jax.ShapeDtypeStruct((bands, EXTRA, BAND), jnp.bfloat16),
+            jax.ShapeDtypeStruct((bands, EXTRA, BAND), jnp.float32),
+        ),
+        in_specs=[whole()] * 2,
+        out_specs=(whole(), whole(), whole()),
+        compiler_params=pltpu.CompilerParams(vmem_limit_bytes=LIMIT),
+        cost_estimate=pl.CostEstimate(
+            flops=4 * bands * BAND * BAND * dims, bytes_accessed=4 * features.size, transcendentals=0
+        ),
+        name="sides",
+    )(feature_bands, widths)
     send_coords = pl.pallas_call(
         pack_kernel,
         out_shape=jax.ShapeDtypeStruct((devices, MOST * BAND + EXTRA, dims), jnp.bfloat16),
@@ -373,7 +409,7 @@
         ],
         compiler_params=pltpu.CompilerParams(vmem_limit_bytes=LIMIT),
         name="pack",
-    )(send_index, feature_bands, sides)
+    )(send_index, copied, sides)
     got_coords = exchange(send_coords)
 
     flat_ids = ids.reshape(-1)
@@ -402,8 +438,6 @@
     send_row = jnp.pad(send_index.reshape(1, entries), ((0, 0), (0, width - entries)))
     near_work = work_list(active & ~far)
     far_work = work_list(far)
-
-    rvec = jnp.stack([0.5 * squares, (2.0 * math.log2(math.e)) * widths], axis=1)
 
     work_space = pltpu.SMEM(far_work.shape, jnp.int32)
     tile_shape = jax.ShapeDtypeStruct((count_all, BAND, BAND), jnp.bfloat16)

time: 250 us -> 245 us (0.980)
  waiting for transfers between devices: 127 us -> 132 us
  Pallas kernels: 73.1 us -> 70.4 us
    all_to_all x6, waiting for transfers between devices: 127 us -> 132 us  [exchange(): return lax.all_to_all(blocks, AXES, split_axis=0, concat_axis=0, tiled=True)]
    pallas_call x4, Pallas kernels: 19.8 us -> 16.6 us  [on_device(): pl.pallas_call(own_kernel, out_shape=total_shape, in_specs=[whole(pltpu.H...]
    pallas_call x0 -> x1, Pallas kernels: none -> 2.82 us  [on_device(): pl.pallas_call(sides_kernel, out_shape=(jax.ShapeDtypeStruct(feature_band...]
  transfers between devices with their start and end apart: 6 -> 6, of which waited for: 6 -> 6; matrix products, arithmetic and copies ran while one was open for 5% -> 4% of each run, Pallas kernels for 12% -> 12%
where the time goes in v5:
time: 245 us; the launch traced here: 244 us
  waiting for transfers between devices  132 us (54%)
  Pallas kernels  70.4 us (29%)
  starting transfers between devices  21.5 us (9%)
  blocking collectives  10.2 us (4%)
  other arithmetic  5 us (2%)
  local copies, waits for them, and re-layouts  4.65 us (2%)
    all_to_all x6, waiting for transfers between devices, exchange(): return lax.all_to_all(blocks, AXES, split_axis=0, concat_axis=0, tiled=True)  132 us
    all_to_all x6, starting transfers between devices, exchange(): return lax.all_to_all(blocks, AXES, split_axis=0, concat_axis=0, tiled=True)  21.5 us
    pallas_call x4, Pallas kernels, on_device(): pl.pallas_call(functools.partial(round_kernel, first, last, gains), out_s...  20.6 us
    pallas_call x4, Pallas kernels, on_device(): pl.pallas_call(own_kernel, out_shape=total_shape, in_specs=[whole(pltpu.H...  16.6 us
    pallas_call x1, Pallas kernels, on_device(): pl.pallas_call(remote_kernel, out_shape=(tile_shape, jax.ShapeDtypeStruct...  11.6 us
    all_to_all x1, blocking collectives, exchange(): return lax.all_to_all(blocks, AXES, split_axis=0, concat_axis=0, tiled=True)  10.2 us
    pallas_call x1, Pallas kernels, on_device(): pl.pallas_call(local_kernel, out_shape=(tile_shape, jax.ShapeDtypeStruct(...  9.19 us
  transfers between devices with their start and end apart: 6, of which 6 were waited for; matrix products, arithmetic and copies ran while one was open for 4% of the time, Pallas kernels for 12%

profile of v5, /device:TPU:0, one launch (start us, length us, event | category | flops | bytes accessed | tf_op | source)
XLA Modules:
  0.0 244.5 jit_solution(9063112707792891652)
XLA Ops:
  0.6 1.6 need.1
  2.2 7.3 %all-to-all-start = ((s32[32,1,32]{2,1,0:T(1,128)}), s32[32,1,32]{2,1,0:T(1,128)S(1)}, u32[]{:S(2)}, u32[]{:S(2)}) async-start(s32[32,1,32]{2,1,0:T(1,128)} %bitcast.41), calls=%async_computation | async-start | bytes 32768 | tf_op jit(solution)/shard_map/all_to_all | solution.py:39
  9.6 0.7 bitcast_convert_fusion.widths
  10.3 2.8 %sides.1 = (bf16[32,128,256]{2,1,0:T(8,128)(2,1)S(1)}, bf16[32,8,128]{2,1,0:T(8,128)(2,1)S(1)}, f32[32,8,128]{2,1,0:T(8,128)S(1)}) custom-call(bf16[32,128,256]{2,1,0:T(8,128)(2,1)} %bitcast.36, f32[32,128]{1,0:T(8,128)S(1)} %bitcast_convert_fusion.widths), custom_call_target="tpu_custom_call" | custom-call | flops 536870912 | bytes 4194304 | tf_op jit(solution)/shard_map/sides/pallas_call | solution.py:386
  13.1 3.6 %all-to-all-done = s32[32,1,32]{2,1,0:T(1,128)S(1)} async-done(((s32[32,1,32]{2,1,0:T(1,128)}), s32[32,1,32]{2,1,0:T(1,128)S(1)}, u32[]{:S(2)}, u32[]{:S(2)}) %all-to-all-start) | async-done | bytes 4128 | tf_op jit(solution)/shard_map/all_to_all | solution.py:39
  16.7 0.2 reduce_window_sum.51
  16.9 0.1 select_reduce_fusion.4
  17.0 0.1 copy.12.send_index
  17.1 3.8 %pack.1 = bf16[32,264,256]{2,1,0:T(8,128)(2,1)} custom-call(s32[32,2]{1,0:T(8,128)S(1)} %copy.12.send_index, bf16[32,128,256]{2,1,0:T(8,128)(2,1)S(1)} %get-tuple-element.22.features, bf16[32,8,128]{2,1,0:T(8,128)(2,1)S(1)} %get-tuple-element.23.sides), custom_call_target="tpu_custom_call" | custom-call | tf_op jit(solution)/shard_map/pack/pallas_call | solution.py:401
  20.9 0.0 copy-start.3
  20.9 0.0 copy-start.4
  20.9 0.0 copy-start.2
  20.9 0.0 copy-start.1
  20.9 3.7 %all-to-all-start.1 = ((bf16[32,264,256]{2,1,0:T(8,128)(2,1)}), bf16[32,264,256]{2,1,0:T(8,128)(2,1)}, u32[]{:S(2)}, u32[]{:S(2)}) async-start(bf16[32,264,256]{2,1,0:T(8,128)(2,1)} %pack.1), calls=%async_computation.1 | async-start | bytes 8650752 | tf_op jit(solution)/shard_map/all_to_all | solution.py:39
  24.7 0.0 copy-done.3
  24.7 0.1 reshape.314
  24.8 0.1 reshape.312
  24.8 0.0 copy-done.4
  24.9 0.1 eq.75
  24.9 0.1 eq.79
  25.0 0.0 copy-done.2
  25.0 0.2 reduce_window_sum.49
  25.2 0.3 reduce-window.16
  25.6 0.3 reduce-window.24
  25.9 0.1 slice.16
  26.0 0.1 slice.14
  26.1 0.1 sub.33
  26.2 2.3 gather_fusion
  28.5 0.0 copy-start
  28.5 0.6 convert_reduce_fusion
  29.1 1.3 compare_convert_fusion
  30.4 0.1 slice_reduce_fusion
  30.5 0.1 slice_reduce_fusion.1
  30.7 0.1 add_bitcast_fusion
  30.8 1.0 select_reduce_fusion
  31.8 0.1 reshape.315
  31.9 0.6 lt.42
  32.6 0.6 lt.45
  33.3 0.0 copy-done.1
  33.3 9.2 %local_tiles.1 = (bf16[512,128,128]{2,1,0:T(8,128)(2,1)}, f32[32,8,128]{2,1,0:T(8,128)S(1)}) custom-call(s32[5,512]{1,0:T(8,128)S(1)} %concatenate.9.work.work_in, bf16[32,128,256]{2,1,0:T(8,128)(2,1)S(1)} %bitcast.37, bf16[32,8,128]{2,1,0:T(8,128)(2,1)S(1)} %get-tuple-element.23.sides, f32[32,8,128]{2,1,0:T(8,128)S(1)} %get-tuple-element.24.rvec), custom_call_target="tpu_custom_call" | custom-call | flops 2147483648 | bytes 8388608 | tf_op jit(solution)/shard_map/local_tiles/pallas_call | solution.py:457
  42.5 79.9 %all-to-all-done.1.got_in = bf16[32,264,256]{2,1,0:T(8,128)(2,1)} async-done(((bf16[32,264,256]{2,1,0:T(8,128)(2,1)}), bf16[32,264,256]{2,1,0:T(8,128)(2,1)}, u32[]{:S(2)}, u32[]{:S(2)}) %all-to-all-start.1) | async-done | bytes 4325408 | tf_op jit(solution)/shard_map/all_to_all | solution.py:39
  122.4 0.0 copy-done
  122.4 11.6 %remote_tiles.1 = (bf16[512,128,128]{2,1,0:T(8,128)(2,1)}, f32[32,128]{1,0:T(8,128)S(1)}, bf16[32,32,128]{2,1,0:T(8,128)(2,1)S(1)}, bf16[64,32,128]{2,1,0:T(8,128)(2,1)}) custom-call(s32[5,512]{1,0:T(8,128)S(1)} %concatenate.8.work_in, bf16[32,128,256]{2,1,0:T(8,128)(2,1)S(1)} %bitcast.38, bf16[32,264,256]{2,1,0:T(8,128)(2,1)} %all-to-all-done.1.got_in, ...), custom_call_target="tpu_custom_call" | custom-call | flops 2147483648 | bytes 8388608 | tf_op jit(solution)/shard_map/remote_tiles/pallas_call | solution.py:470
  134.1 2.6 %all-to-all-start.2 = ((bf16[32,2,32,128]{3,2,1,0:T(8,128)(2,1)}), bf16[32,2,32,128]{3,2,1,0:T(8,128)(2,1)S(1)}, u32[]{:S(2)}, u32[]{:S(2)}) async-start(bf16[32,2,32,128]{3,2,1,0:T(8,128)(2,1)} %bitcast.15), calls=%async_computation.2 | async-start | bytes 1048576 | tf_op jit(solution)/shard_map/all_to_all | solution.py:39
  136.7 4.1 %own0.1.total_in = f32[32,32,128]{2,1,0:T(8,128)S(1)} custom-call(s32[5,512]{1,0:T(8,128)S(1)} %concatenate.9.work.work_in, bf16[32,32,128]{2,1,0:T(8,128)(2,1)S(1)} %get-tuple-element.27.scaled, bf16[512,128,128]{2,1,0:T(8,128)(2,1)} %get-tuple-element.28.tiles), custom_call_target="tpu_custom_call" | custom-call | flops 268435456 | bytes 8388608 | tf_op jit(solution)/shard_map/own0/pallas_call | solution.py:508
  140.8 12.1 %all-to-all-done.2 = bf16[32,2,32,128]{3,2,1,0:T(8,128)(2,1)S(1)} async-done(((bf16[32,2,32,128]{3,2,1,0:T(8,128)(2,1)}), bf16[32,2,32,128]{3,2,1,0:T(8,128)(2,1)S(1)}, u32[]{:S(2)}, u32[]{:S(2)}) %all-to-all-start.2) | async-done | bytes 524320 | tf_op jit(solution)/shard_map/all_to_all | solution.py:39
  152.9 5.2 %round0.1 = (f32[32,4096]{1,0:T(8,128)S(1)}, bf16[32,32,128]{2,1,0:T(8,128)(2,1)S(1)}, bf16[64,32,128]{2,1,0:T(8,128)(2,1)}) custom-call(s32[5,512]{1,0:T(8,128)S(1)} %concatenate.8.work_in, bf16[64,32,128]{2,1,0:T(8,128)(2,1)S(1)} %bitcast.33, f32[32,32,128]{2,1,0:T(8,128)S(1)} %own0.1.total_in, f32[32,128]{1,0:T(8,128)S(1)} %get-tuple-element.29.root, ...), custom_call_target="tpu_custom_call" | custom-call | flops 268435456 | bytes 8388608 | tf_op jit(solution)/shard_map/round0/pallas_call | solution.py:519
  158.2 2.6 %all-to-all-start.3 = ((bf16[32,2,32,128]{3,2,1,0:T(8,128)(2,1)}), bf16[32,2,32,128]{3,2,1,0:T(8,128)(2,1)S(1)}, u32[]{:S(2)}, u32[]{:S(2)}) async-start(bf16[32,2,32,128]{3,2,1,0:T(8,128)(2,1)} %bitcast.17), calls=%async_computation.3 | async-start | bytes 1048576 | tf_op jit(solution)/shard_map/all_to_all | solution.py:39
  160.8 4.1 %own1.1.total_in = f32[32,32,128]{2,1,0:T(8,128)S(1)} custom-call(s32[5,512]{1,0:T(8,128)S(1)} %concatenate.9.work.work_in, bf16[32,32,128]{2,1,0:T(8,128)(2,1)S(1)} %get-tuple-element.32.scaled, bf16[512,128,128]{2,1,0:T(8,128)(2,1)} %get-tuple-element.28.tiles), custom_call_target="tpu_custom_call" | custom-call | flops 268435456 | bytes 8388608 | tf_op jit(solution)/shard_map/own1/pallas_call | solution.py:508
  165.0 12.1 %all-to-all-done.3 = bf16[32,2,32,128]{3,2,1,0:T(8,128)(2,1)S(1)} async-done(((bf16[32,2,32,128]{3,2,1,0:T(8,128)(2,1)}), bf16[32,2,32,128]{3,2,1,0:T(8,128)(2,1)S(1)}, u32[]{:S(2)}, u32[]{:S(2)}) %all-to-all-start.3) | async-done | bytes 524320 | tf_op jit(solution)/shard_map/all_to_all | solution.py:39
  177.0 5.3 %round1.1 = (f32[32,4096]{1,0:T(8,128)S(1)}, bf16[32,32,128]{2,1,0:T(8,128)(2,1)S(1)}, bf16[64,32,128]{2,1,0:T(8,128)(2,1)}) custom-call(s32[5,512]{1,0:T(8,128)S(1)} %concatenate.8.work_in, bf16[64,32,128]{2,1,0:T(8,128)(2,1)S(1)} %bitcast.35, f32[32,32,128]{2,1,0:T(8,128)S(1)} %own1.1.total_in, f32[32,128]{1,0:T(8,128)S(1)} %get-tuple-element.29.root, ...), custom_call_target="tpu_custom_call" | custom-call | flops 268435456 | bytes 8388608 | tf_op jit(solution)/shard_map/round1/pallas_call | solution.py:519
  182.3 2.6 %all-to-all-start.4 = ((bf16[32,2,32,128]{3,2,1,0:T(8,128)(2,1)}), bf16[32,2,32,128]{3,2,1,0:T(8,128)(2,1)S(1)}, u32[]{:S(2)}, u32[]{:S(2)}) async-start(bf16[32,2,32,128]{3,2,1,0:T(8,128)(2,1)} %bitcast.19), calls=%async_computation.4 | async-start | bytes 1048576 | tf_op jit(solution)/shard_map/all_to_all | solution.py:39
  184.9 4.1 %own2.1.total_in = f32[32,32,128]{2,1,0:T(8,128)S(1)} custom-call(s32[5,512]{1,0:T(8,128)S(1)} %concatenate.9.work.work_in, bf16[32,32,128]{2,1,0:T(8,128)(2,1)S(1)} %get-tuple-element.35.scaled, bf16[512,128,128]{2,1,0:T(8,128)(2,1)} %get-tuple-element.28.tiles), custom_call_target="tpu_custom_call" | custom-call | flops 268435456 | bytes 8388608 | tf_op jit(solution)/shard_map/own2/pallas_call | solution.py:508
  189.1 12.1 %all-to-all-done.4 = bf16[32,2,32,128]{3,2,1,0:T(8,128)(2,1)S(1)} async-done(((bf16[32,2,32,128]{3,2,1,0:T(8,128)(2,1)}), bf16[32,2,32,128]{3,2,1,0:T(8,128)(2,1)S(1)}, u32[]{:S(2)}, u32[]{:S(2)}) %all-to-all-start.4) | async-done | bytes 524320 | tf_op jit(solution)/shard_map/all_to_all | solution.py:39
  201.2 5.3 %round2.1 = (f32[32,4096]{1,0:T(8,128)S(1)}, bf16[32,32,128]{2,1,0:T(8,128)(2,1)S(1)}, bf16[64,32,128]{2,1,0:T(8,128)(2,1)}) custom-call(s32[5,512]{1,0:T(8,128)S(1)} %concatenate.8.work_in, bf16[64,32,128]{2,1,0:T(8,128)(2,1)S(1)} %bitcast.34, f32[32,32,128]{2,1,0:T(8,128)S(1)} %own2.1.total_in, f32[32,128]{1,0:T(8,128)S(1)} %get-tuple-element.29.root, ...), custom_call_target="tpu_custom_call" | custom-call | flops 268435456 | bytes 8388608 | tf_op jit(solution)/shard_map/round2/pallas_call | solution.py:519
  206.5 2.6 %all-to-all-start.5 = ((bf16[32,2,32,128]{3,2,1,0:T(8,128)(2,1)}), bf16[32,2,32,128]{3,2,1,0:T(8,128)(2,1)S(1)}, u32[]{:S(2)}, u32[]{:S(2)}) async-start(bf16[32,2,32,128]{3,2,1,0:T(8,128)(2,1)} %bitcast.21), calls=%async_computation.5 | async-start | bytes 1048576 | tf_op jit(solution)/shard_map/all_to_all | solution.py:39
  209.1 4.1 %own3.1.total_in = f32[32,32,128]{2,1,0:T(8,128)S(1)} custom-call(s32[5,512]{1,0:T(8,128)S(1)} %concatenate.9.work.work_in, bf16[32,32,128]{2,1,0:T(8,128)(2,1)S(1)} %get-tuple-element.38.scaled, bf16[512,128,128]{2,1,0:T(8,128)(2,1)} %get-tuple-element.28.tiles), custom_call_target="tpu_custom_call" | custom-call | flops 268435456 | bytes 8388608 | tf_op jit(solution)/shard_map/own3/pallas_call | solution.py:508
  213.2 12.1 %all-to-all-done.5 = bf16[32,2,32,128]{3,2,1,0:T(8,128)(2,1)S(1)} async-done(((bf16[32,2,32,128]{3,2,1,0:T(8,128)(2,1)}), bf16[32,2,32,128]{3,2,1,0:T(8,128)(2,1)S(1)}, u32[]{:S(2)}, u32[]{:S(2)}) %all-to-all-start.5) | async-done | bytes 524320 | tf_op jit(solution)/shard_map/all_to_all | solution.py:39
  225.3 4.8 %round3.1 = (f32[32,4096]{1,0:T(8,128)S(1)}, f32[32,8,128]{2,1,0:T(8,128)S(1)}) custom-call(s32[5,512]{1,0:T(8,128)S(1)} %concatenate.8.work_in, bf16[64,32,128]{2,1,0:T(8,128)(2,1)S(1)} %bitcast.32, f32[32,32,128]{2,1,0:T(8,128)S(1)} %own3.1.total_in, f32[32,128]{1,0:T(8,128)S(1)} %get-tuple-element.29.root, f32[32,4096]{1,0:T(8,128)S(1)} %get-tuple-element.39.cur, ...), custom_call_target="tpu_custom_call" | custom-call | flops 268435456 | bytes 8388608 | tf_op jit(solution)/shard_map/round3/pallas_call | solution.py:519
  230.2 10.2 %all_to_all.39.parts = f32[32,8,128]{2,1,0:T(8,128)S(1)} all-to-all(f32[32,8,128]{2,1,0:T(8,128)S(1)} %get-tuple-element.40), channel_id=1, replica_groups=mesh['gx'=4,'gy'=8] {'gx','gy'}, dimensions={0} | all-to-all | bytes 262144 | tf_op jit(solution)/shard_map/all_to_all | solution.py:39
  240.3 4.2 %finish.1 = (f32[32,4096]{1,0:T(8,128)}, f32[32,32]{1,0:T(8,128)}) custom-call(f32[32,8,128]{2,1,0:T(8,128)S(1)} %all_to_all.39.parts, f32[32,4096]{1,0:T(8,128)S(1)} %get-tuple-element.41.flat), custom_call_target="tpu_custom_call" | custom-call | tf_op jit(solution)/shard_map/finish/pallas_call | solution.py:535
  (16 shorter events, 0.2 us)
Async XLA Ops:
  2.2 14.4 %all-to-all-start = ((s32[32,1,32]{2,1,0:T(1,128)}), s32[32,1,32]{2,1,0:T(1,128)S(1)}, u32[]{:S(2)}, u32[]{:S(2)}) async-start(s32[32,1,32]{2,1,0:T(1,128)} %bitcast.41), calls=%async_computation | async-start | bytes 32768 | tf_op jit(solution)/shard_map/all_to_all | solution.py:39
  20.9 3.8 %copy-start.3 = (s32[32,16]{0,1:T(8,128)S(1)}, s32[32,16]{0,1:T(8,128)}, u32[]{:S(2)}) copy-start(s32[32,16]{0,1:T(8,128)} %param.8) | copy-start | bytes 6148
  20.9 3.9 %copy-start.4 = (s32[32,16]{0,1:T(8,128)S(1)}, s32[32,16]{0,1:T(8,128)}, u32[]{:S(2)}) copy-start(s32[32,16]{0,1:T(8,128)} %param.9) | copy-start | bytes 6148
  20.9 4.1 %copy-start.2 = (s32[32,32]{1,0:T(8,128)S(1)}, s32[32,32]{1,0:T(8,128)}, u32[]{:S(2)}) copy-start(s32[32,32]{1,0:T(8,128)} %need.1) | copy-start | bytes 12292
  20.9 12.4 %copy-start.1 = (bf16[4096,256]{1,0:T(8,128)(2,1)S(1)}, bf16[4096,256]{1,0:T(8,128)(2,1)}, u32[]{:S(2)}) copy-start(bf16[4096,256]{1,0:T(8,128)(2,1)} %param.5) | copy-start | bytes 6291460
  20.9 101.5 %all-to-all-start.1 = ((bf16[32,264,256]{2,1,0:T(8,128)(2,1)}), bf16[32,264,256]{2,1,0:T(8,128)(2,1)}, u32[]{:S(2)}, u32[]{:S(2)}) async-start(bf16[32,264,256]{2,1,0:T(8,128)(2,1)} %pack.1), calls=%async_computation.1 | async-start | bytes 8650752 | tf_op jit(solution)/shard_map/all_to_all | solution.py:39
  28.5 94.0 %copy-start = (f32[32,4096]{1,0:T(8,128)S(1)}, f32[32,4096]{1,0:T(8,128)}, u32[]{:S(2)}) copy-start(f32[32,4096]{1,0:T(8,128)} %prev.3) | copy-start | bytes 1572868
  134.1 18.9 %all-to-all-start.2 = ((bf16[32,2,32,128]{3,2,1,0:T(8,128)(2,1)}), bf16[32,2,32,128]{3,2,1,0:T(8,128)(2,1)S(1)}, u32[]{:S(2)}, u32[]{:S(2)}) async-start(bf16[32,2,32,128]{3,2,1,0:T(8,128)(2,1)} %bitcast.15), calls=%async_computation.2 | async-start | bytes 1048576 | tf_op jit(solution)/shard_map/all_to_all | solution.py:39
  158.2 18.9 %all-to-all-start.3 = ((bf16[32,2,32,128]{3,2,1,0:T(8,128)(2,1)}), bf16[32,2,32,128]{3,2,1,0:T(8,128)(2,1)S(1)}, u32[]{:S(2)}, u32[]{:S(2)}) async-start(bf16[32,2,32,128]{3,2,1,0:T(8,128)(2,1)} %bitcast.17), calls=%async_computation.3 | async-start | bytes 1048576 | tf_op jit(solution)/shard_map/all_to_all | solution.py:39
  182.3 18.9 %all-to-all-start.4 = ((bf16[32,2,32,128]{3,2,1,0:T(8,128)(2,1)}), bf16[32,2,32,128]{3,2,1,0:T(8,128)(2,1)S(1)}, u32[]{:S(2)}, u32[]{:S(2)}) async-start(bf16[32,2,32,128]{3,2,1,0:T(8,128)(2,1)} %bitcast.19), calls=%async_computation.4 | async-start | bytes 1048576 | tf_op jit(solution)/shard_map/all_to_all | solution.py:39
  206.5 18.9 %all-to-all-start.5 = ((bf16[32,2,32,128]{3,2,1,0:T(8,128)(2,1)}), bf16[32,2,32,128]{3,2,1,0:T(8,128)(2,1)S(1)}, u32[]{:S(2)}, u32[]{:S(2)}) async-start(bf16[32,2,32,128]{3,2,1,0:T(8,128)(2,1)} %bitcast.21), calls=%async_computation.5 | async-start | bytes 1048576 | tf_op jit(solution)/shard_map/all_to_all | solution.py:39

commit v6 on v5

--- a/solution.py
+++ b/solution.py
@@ -75,7 +75,9 @@
 
     for band in range(features.shape[0]):
         block = features[band]
-        copied[band] = block
+        for part in range(dims // BAND):
+            lanes = slice(part * BAND, (part + 1) * BAND)
+            copied[band, lanes, :] = block[:, lanes]
         wide = block.astype(jnp.float32)
         exact = wide * wide
         high = exact.astype(jnp.bfloat16)
@@ -87,34 +89,36 @@
         left = product - first
         second = left.astype(jnp.bfloat16).astype(jnp.float32)
         third = left - second
-        side = jnp.where(row == 0, width, jnp.where(row == 1, first, 0.0))
-        side = jnp.where(row == 2, second, jnp.where(row == 3, third, side))
+        part = row % (EXTRA // MOST)
+        side = jnp.where(part == 0, width, first)
+        side = jnp.where(part == 2, second, jnp.where(part == 3, third, side))
         sides[band] = side.astype(jnp.bfloat16)
         rvec[band] = jnp.where(row == 0, half, (2.0 * math.log2(math.e)) * width)
 
 
 def pack_kernel(send_index, features, sides, send, tails, sems):
     devices = send.shape[0]
+    depth = features.shape[1]
 
     def bands_of(d):
         return [
             pltpu.make_async_copy(
-                features.at[send_index[d, h]],
-                send.at[d, pl.ds(h * BAND, BAND)],
-                sems.at[h, d],
+                features.at[send_index[d, h]], send.at[d, pl.ds(h * depth, depth)], sems.at[h, d]
             )
             for h in range(MOST)
         ]
 
     def tail_of(d):
         return pltpu.make_async_copy(
-            tails.at[d], send.at[d, pl.ds(MOST * BAND, EXTRA)], sems.at[MOST, d]
+            tails.at[d], send.at[d, pl.ds(MOST * depth, EXTRA)], sems.at[MOST, d]
         )
 
     def first(d, carry):
         for copy in bands_of(d):
             copy.start()
-        tails[d] = jnp.concatenate([sides[send_index[d, h]] for h in range(MOST)], axis=1)
+        row = lax.broadcasted_iota(jnp.int32, (EXTRA, BAND), 0)
+        near, far = [sides[send_index[d, h]].astype(jnp.float32) for h in range(MOST)]
+        tails[d] = jnp.where(row < EXTRA // MOST, near, far).astype(jnp.bfloat16)
         return carry
 
     def second(d, carry):
@@ -127,16 +131,17 @@
         tail_of(d).wait()
         return carry
 
-    lax.fori_loop(0, devices, first, 0)
-    lax.fori_loop(0, devices, second, 0)
-    lax.fori_loop(0, devices, third, 0)
-
-
-def spread_column(side):
+    lax.fori_loop(0, devices, first, 0, unroll=4)
+    lax.fori_loop(0, devices, second, 0, unroll=4)
+    lax.fori_loop(0, devices, third, 0, unroll=4)
+
+
+def spread_column(side, h):
     row = lax.broadcasted_iota(jnp.int32, (EXTRA, 2 * BAND), 0)
     lane = lax.broadcasted_iota(jnp.int32, (EXTRA, 2 * BAND), 1)
-    left = jnp.where((row == 0) & (lane < BAND), 1.0, 0.0)
-    right = jnp.where((row > 0) & (row < 4) & (lane >= BAND), 1.0, 0.0)
+    base = h * (EXTRA // MOST)
+    left = jnp.where((row == base) & (lane < BAND), 1.0, 0.0)
+    right = jnp.where((row > base) & (row < base + 4) & (lane >= BAND), 1.0, 0.0)
     return lax.dot_general(
         side, (left + right).astype(jnp.bfloat16), (((0,), (0,)), ((), ())),
         preferred_element_type=jnp.float32,
@@ -189,7 +194,7 @@
     deg[...] = jnp.zeros(deg.shape, deg.dtype)
 
     def fill(band, carry):
-        cols[band] = spread_column(sides[band])
+        cols[band] = spread_column(sides[band], 0)
         return carry
 
     lax.fori_loop(0, rows.shape[0], fill, 0, unroll=4)
@@ -205,7 +210,8 @@
 
 
 def remote_kernel(work_in, rows, got_in, rvec, deg_in, start,
-                  tiles, root, scaled, send, work, got, deg, cols, stage, sems, work_sem, got_sems):
+                  tiles, root, scaled, send_out, work, got, deg, send, cols, stage, sems,
+                  work_sem, got_sems, send_sem):
     work_copy = pltpu.make_async_copy(work_in, work, work_sem)
     work_copy.start()
 
@@ -218,7 +224,8 @@
 
     lax.fori_loop(0, got.shape[0], begin, 0)
     deg[...] = deg_in[...]
-    tail = MOST * BAND
+    halves = rows.shape[2] // BAND
+    tail = MOST * halves * BAND
     step = 4
 
     def fill(part, carry):
@@ -227,16 +234,17 @@
         for k in range(step):
             owner = part * step + k
             for h in range(MOST):
-                side = got[owner, tail : tail + EXTRA, h * BAND : (h + 1) * BAND]
-                cols[owner * MOST + h] = spread_column(side)
+                cols[owner * MOST + h] = spread_column(got[owner, tail : tail + EXTRA, :], h)
         return carry
 
     lax.fori_loop(0, got.shape[0] // step, fill, 0)
     work_copy.wait()
 
     def coords_of(entry):
-        at = pl.multiple_of(lax.rem(entry, MOST) * BAND, BAND)
-        return got[entry // MOST, pl.ds(at, BAND), :]
+        at = pl.multiple_of(lax.rem(entry, MOST) * (halves * BAND), BAND)
+        return jnp.concatenate(
+            [got[entry // MOST, pl.ds(at + part * BAND, BAND), :] for part in range(halves)], axis=1
+        )
 
     def between():
         for band in range(deg.shape[0]):
@@ -246,8 +254,11 @@
             block = start[:, band * BAND : (band + 1) * BAND]
             scaled[band] = (block * inverse).astype(jnp.bfloat16)
         pack_rows(work, scaled, send)
-
+        send_copy.start()
+
+    send_copy = pltpu.make_async_copy(send, send_out, send_sem)
     tile_groups(work, rows, coords_of, cols, rvec, tiles, deg, stage, sems, between)
+    send_copy.wait()
 
 
 def gather_product(work_in, table, tiles, total, work, held, work_sem, sems):
@@ -386,7 +397,7 @@
     copied, sides, rvec = pl.pallas_call(
         sides_kernel,
         out_shape=(
-            jax.ShapeDtypeStruct(feature_bands.shape, jnp.bfloat16),
+            jax.ShapeDtypeStruct((bands, dims, BAND), jnp.bfloat16),
             jax.ShapeDtypeStruct((bands, EXTRA, BAND), jnp.bfloat16),
             jax.ShapeDtypeStruct((bands, EXTRA, BAND), jnp.float32),
         ),
@@ -400,11 +411,11 @@
     )(feature_bands, widths)
     send_coords = pl.pallas_call(
         pack_kernel,
-        out_shape=jax.ShapeDtypeStruct((devices, MOST * BAND + EXTRA, dims), jnp.bfloat16),
+        out_shape=jax.ShapeDtypeStruct((devices, MOST * dims + EXTRA, BAND), jnp.bfloat16),
         in_specs=[whole(SMEM)] + [whole()] * 2,
         out_specs=whole(pl.ANY),
         scratch_shapes=[
-            pltpu.VMEM((devices, EXTRA, dims), jnp.bfloat16),
+            pltpu.VMEM((devices, EXTRA, BAND), jnp.bfloat16),
             pltpu.SemaphoreType.DMA((MOST + 1, devices)),
         ],
         compiler_params=pltpu.CompilerParams(vmem_limit_bytes=LIMIT),
@@ -471,12 +482,15 @@
         remote_kernel,
         out_shape=(tile_shape, jax.ShapeDtypeStruct((bands, BAND), jnp.float32), row_shape, send_shape),
         in_specs=[whole(pltpu.HBM), whole(), whole(pltpu.HBM)] + [whole()] * 3,
-        out_specs=(whole(pl.ANY), whole(), whole(), whole()),
+        out_specs=(whole(pl.ANY), whole(), whole(), whole(pl.ANY)),
         scratch_shapes=[
             work_space,
             pltpu.VMEM(send_coords.shape, jnp.bfloat16),
             pltpu.VMEM((bands, 8, BAND), jnp.float32),
-        ] + building(entries) + [pltpu.SemaphoreType.DMA, pltpu.SemaphoreType.DMA((devices,))],
+            pltpu.VMEM(send_shape.shape, jnp.bfloat16),
+        ] + building(entries) + [
+            pltpu.SemaphoreType.DMA, pltpu.SemaphoreType.DMA((devices,)), pltpu.SemaphoreType.DMA,
+        ],
         cost_estimate=build_cost,
         compiler_params=pltpu.CompilerParams(vmem_limit_bytes=max(LIMIT, remote_bytes)),
         name="remote_tiles",

time: 245 us -> 243 us (level)
  no operation moved by 1% of the time
where the time goes in v6:
time: 243 us
  waiting for transfers between devices  130 us (53%)
  Pallas kernels  70 us (29%)
  starting transfers between devices  21.5 us (9%)
  blocking collectives  10.2 us (4%)
  other arithmetic  5 us (2%)
  local copies, waits for them, and re-layouts  4.65 us (2%)
    all_to_all x6, waiting for transfers between devices, exchange(): return lax.all_to_all(blocks, AXES, split_axis=0, concat_axis=0, tiled=True)  130 us
    all_to_all x6, starting transfers between devices, exchange(): return lax.all_to_all(blocks, AXES, split_axis=0, concat_axis=0, tiled=True)  21.5 us
    pallas_call x4, Pallas kernels, on_device(): pl.pallas_call(functools.partial(round_kernel, first, last, gains), out_s...  20.6 us
    pallas_call x4, Pallas kernels, on_device(): pl.pallas_call(own_kernel, out_shape=total_shape, in_specs=[whole(pltpu.H...  16.6 us
    pallas_call x1, Pallas kernels, on_device(): pl.pallas_call(remote_kernel, out_shape=(tile_shape, jax.ShapeDtypeStruct...  11.3 us
    all_to_all x1, blocking collectives, exchange(): return lax.all_to_all(blocks, AXES, split_axis=0, concat_axis=0, tiled=True)  10.2 us
    pallas_call x1, Pallas kernels, on_device(): pl.pallas_call(local_kernel, out_shape=(tile_shape, jax.ShapeDtypeStruct(...  9.2 us
  transfers between devices with their start and end apart: 6, of which 6 were waited for; matrix products, arithmetic and copies ran while one was open for 4% of the time, Pallas kernels for 12%

profile of v6, /device:TPU:0, one launch (start us, length us, event | category | flops | bytes accessed | tf_op | source)
XLA Modules:
  0.0 242.7 jit_solution(2040461876693433889)
XLA Ops:
  0.6 1.6 need.1
  2.2 7.3 %all-to-all-start = ((s32[32,1,32]{2,1,0:T(1,128)}), s32[32,1,32]{2,1,0:T(1,128)S(1)}, u32[]{:S(2)}, u32[]{:S(2)}) async-start(s32[32,1,32]{2,1,0:T(1,128)} %bitcast.41), calls=%async_computation | async-start | bytes 32768 | tf_op jit(solution)/shard_map/all_to_all | solution.py:39
  9.6 0.7 bitcast_convert_fusion.widths
  10.3 2.8 %sides.1 = (bf16[32,256,128]{2,1,0:T(8,128)(2,1)S(1)}, bf16[32,8,128]{2,1,0:T(8,128)(2,1)S(1)}, f32[32,8,128]{2,1,0:T(8,128)S(1)}) custom-call(bf16[32,128,256]{2,1,0:T(8,128)(2,1)} %bitcast.36, f32[32,128]{1,0:T(8,128)S(1)} %bitcast_convert_fusion.widths), custom_call_target="tpu_custom_call" | custom-call | flops 536870912 | bytes 4194304 | tf_op jit(solution)/shard_map/sides/pallas_call | solution.py:397
  13.1 3.6 %all-to-all-done = s32[32,1,32]{2,1,0:T(1,128)S(1)} async-done(((s32[32,1,32]{2,1,0:T(1,128)}), s32[32,1,32]{2,1,0:T(1,128)S(1)}, u32[]{:S(2)}, u32[]{:S(2)}) %all-to-all-start) | async-done | bytes 4128 | tf_op jit(solution)/shard_map/all_to_all | solution.py:39
  16.7 0.2 reduce_window_sum.51
  16.9 0.1 select_reduce_fusion.4
  17.0 0.1 copy.12.send_index
  17.1 3.7 %pack.1 = bf16[32,520,128]{2,1,0:T(8,128)(2,1)} custom-call(s32[32,2]{1,0:T(8,128)S(1)} %copy.12.send_index, bf16[32,256,128]{2,1,0:T(8,128)(2,1)S(1)} %get-tuple-element.22.features, bf16[32,8,128]{2,1,0:T(8,128)(2,1)S(1)} %get-tuple-element.23.sides), custom_call_target="tpu_custom_call" | custom-call | tf_op jit(solution)/shard_map/pack/pallas_call | solution.py:412
  20.8 0.0 copy-start.3
  20.8 0.0 copy-start.4
  20.8 0.0 copy-start.2
  20.9 0.0 copy-start.1
  20.9 3.7 %all-to-all-start.1 = ((bf16[32,520,128]{2,1,0:T(8,128)(2,1)}), bf16[32,520,128]{2,1,0:T(8,128)(2,1)}, u32[]{:S(2)}, u32[]{:S(2)}) async-start(bf16[32,520,128]{2,1,0:T(8,128)(2,1)} %pack.1), calls=%async_computation.1 | async-start | bytes 8519680 | tf_op jit(solution)/shard_map/all_to_all | solution.py:39
  24.6 0.0 copy-done.3
  24.6 0.1 reshape.314
  24.7 0.1 reshape.312
  24.7 0.0 copy-done.4
  24.8 0.1 eq.75
  24.9 0.1 eq.79
  24.9 0.0 copy-done.2
  24.9 0.2 reduce_window_sum.49
  25.2 0.3 reduce-window.16
  25.5 0.3 reduce-window.24
  25.8 0.1 slice.16
  25.9 0.1 slice.14
  26.0 0.1 sub.33
  26.1 2.3 gather_fusion
  28.4 0.0 copy-start
  28.4 0.6 convert_reduce_fusion
  29.0 1.3 compare_convert_fusion
  30.3 0.1 slice_reduce_fusion
  30.4 0.1 slice_reduce_fusion.1
  30.6 0.1 add_bitcast_fusion
  30.7 1.0 select_reduce_fusion
  31.7 0.1 reshape.315
  31.8 0.6 lt.42
  32.5 0.6 lt.45
  33.2 0.0 copy-done.1
  33.2 9.2 %local_tiles.1 = (bf16[512,128,128]{2,1,0:T(8,128)(2,1)}, f32[32,8,128]{2,1,0:T(8,128)S(1)}) custom-call(s32[5,512]{1,0:T(8,128)S(1)} %concatenate.9.work.work_in, bf16[32,128,256]{2,1,0:T(8,128)(2,1)S(1)} %bitcast.37, bf16[32,8,128]{2,1,0:T(8,128)(2,1)S(1)} %get-tuple-element.23.sides, f32[32,8,128]{2,1,0:T(8,128)S(1)} %get-tuple-element.24.rvec), custom_call_target="tpu_custom_call" | custom-call | flops 2147483648 | bytes 8388608 | tf_op jit(solution)/shard_map/local_tiles/pallas_call | solution.py:468
  42.4 78.5 %all-to-all-done.1.got_in = bf16[32,520,128]{2,1,0:T(8,128)(2,1)} async-done(((bf16[32,520,128]{2,1,0:T(8,128)(2,1)}), bf16[32,520,128]{2,1,0:T(8,128)(2,1)}, u32[]{:S(2)}, u32[]{:S(2)}) %all-to-all-start.1) | async-done | bytes 4259872 | tf_op jit(solution)/shard_map/all_to_all | solution.py:39
  120.9 0.0 copy-done
  120.9 11.3 %remote_tiles.1 = (bf16[512,128,128]{2,1,0:T(8,128)(2,1)}, f32[32,128]{1,0:T(8,128)S(1)}, bf16[32,32,128]{2,1,0:T(8,128)(2,1)S(1)}, bf16[64,32,128]{2,1,0:T(8,128)(2,1)}) custom-call(s32[5,512]{1,0:T(8,128)S(1)} %concatenate.8.work_in, bf16[32,128,256]{2,1,0:T(8,128)(2,1)S(1)} %bitcast.38, bf16[32,520,128]{2,1,0:T(8,128)(2,1)} %all-to-all-done.1.got_in, ...), custom_call_target="tpu_custom_call" | custom-call | flops 2147483648 | bytes 8388608 | tf_op jit(solution)/shard_map/remote_tiles/pallas_call | solution.py:481
  132.3 2.6 %all-to-all-start.2 = ((bf16[32,2,32,128]{3,2,1,0:T(8,128)(2,1)}), bf16[32,2,32,128]{3,2,1,0:T(8,128)(2,1)S(1)}, u32[]{:S(2)}, u32[]{:S(2)}) async-start(bf16[32,2,32,128]{3,2,1,0:T(8,128)(2,1)} %bitcast.15), calls=%async_computation.2 | async-start | bytes 1048576 | tf_op jit(solution)/shard_map/all_to_all | solution.py:39
  134.9 4.2 %own0.1.total_in = f32[32,32,128]{2,1,0:T(8,128)S(1)} custom-call(s32[5,512]{1,0:T(8,128)S(1)} %concatenate.9.work.work_in, bf16[32,32,128]{2,1,0:T(8,128)(2,1)S(1)} %get-tuple-element.27.scaled, bf16[512,128,128]{2,1,0:T(8,128)(2,1)} %get-tuple-element.28.tiles), custom_call_target="tpu_custom_call" | custom-call | flops 268435456 | bytes 8388608 | tf_op jit(solution)/shard_map/own0/pallas_call | solution.py:522
  139.0 12.1 %all-to-all-done.2 = bf16[32,2,32,128]{3,2,1,0:T(8,128)(2,1)S(1)} async-done(((bf16[32,2,32,128]{3,2,1,0:T(8,128)(2,1)}), bf16[32,2,32,128]{3,2,1,0:T(8,128)(2,1)S(1)}, u32[]{:S(2)}, u32[]{:S(2)}) %all-to-all-start.2) | async-done | bytes 524320 | tf_op jit(solution)/shard_map/all_to_all | solution.py:39
  151.1 5.2 %round0.1 = (f32[32,4096]{1,0:T(8,128)S(1)}, bf16[32,32,128]{2,1,0:T(8,128)(2,1)S(1)}, bf16[64,32,128]{2,1,0:T(8,128)(2,1)}) custom-call(s32[5,512]{1,0:T(8,128)S(1)} %concatenate.8.work_in, bf16[64,32,128]{2,1,0:T(8,128)(2,1)S(1)} %bitcast.33, f32[32,32,128]{2,1,0:T(8,128)S(1)} %own0.1.total_in, f32[32,128]{1,0:T(8,128)S(1)} %get-tuple-element.29.root, ...), custom_call_target="tpu_custom_call" | custom-call | flops 268435456 | bytes 8388608 | tf_op jit(solution)/shard_map/round0/pallas_call | solution.py:533
  156.4 2.6 %all-to-all-start.3 = ((bf16[32,2,32,128]{3,2,1,0:T(8,128)(2,1)}), bf16[32,2,32,128]{3,2,1,0:T(8,128)(2,1)S(1)}, u32[]{:S(2)}, u32[]{:S(2)}) async-start(bf16[32,2,32,128]{3,2,1,0:T(8,128)(2,1)} %bitcast.17), calls=%async_computation.3 | async-start | bytes 1048576 | tf_op jit(solution)/shard_map/all_to_all | solution.py:39
  159.0 4.2 %own1.1.total_in = f32[32,32,128]{2,1,0:T(8,128)S(1)} custom-call(s32[5,512]{1,0:T(8,128)S(1)} %concatenate.9.work.work_in, bf16[32,32,128]{2,1,0:T(8,128)(2,1)S(1)} %get-tuple-element.32.scaled, bf16[512,128,128]{2,1,0:T(8,128)(2,1)} %get-tuple-element.28.tiles), custom_call_target="tpu_custom_call" | custom-call | flops 268435456 | bytes 8388608 | tf_op jit(solution)/shard_map/own1/pallas_call | solution.py:522
  163.2 12.1 %all-to-all-done.3 = bf16[32,2,32,128]{3,2,1,0:T(8,128)(2,1)S(1)} async-done(((bf16[32,2,32,128]{3,2,1,0:T(8,128)(2,1)}), bf16[32,2,32,128]{3,2,1,0:T(8,128)(2,1)S(1)}, u32[]{:S(2)}, u32[]{:S(2)}) %all-to-all-start.3) | async-done | bytes 524320 | tf_op jit(solution)/shard_map/all_to_all | solution.py:39
  175.2 5.3 %round1.1 = (f32[32,4096]{1,0:T(8,128)S(1)}, bf16[32,32,128]{2,1,0:T(8,128)(2,1)S(1)}, bf16[64,32,128]{2,1,0:T(8,128)(2,1)}) custom-call(s32[5,512]{1,0:T(8,128)S(1)} %concatenate.8.work_in, bf16[64,32,128]{2,1,0:T(8,128)(2,1)S(1)} %bitcast.35, f32[32,32,128]{2,1,0:T(8,128)S(1)} %own1.1.total_in, f32[32,128]{1,0:T(8,128)S(1)} %get-tuple-element.29.root, ...), custom_call_target="tpu_custom_call" | custom-call | flops 268435456 | bytes 8388608 | tf_op jit(solution)/shard_map/round1/pallas_call | solution.py:533
  180.5 2.6 %all-to-all-start.4 = ((bf16[32,2,32,128]{3,2,1,0:T(8,128)(2,1)}), bf16[32,2,32,128]{3,2,1,0:T(8,128)(2,1)S(1)}, u32[]{:S(2)}, u32[]{:S(2)}) async-start(bf16[32,2,32,128]{3,2,1,0:T(8,128)(2,1)} %bitcast.19), calls=%async_computation.4 | async-start | bytes 1048576 | tf_op jit(solution)/shard_map/all_to_all | solution.py:39
  183.1 4.2 %own2.1.total_in = f32[32,32,128]{2,1,0:T(8,128)S(1)} custom-call(s32[5,512]{1,0:T(8,128)S(1)} %concatenate.9.work.work_in, bf16[32,32,128]{2,1,0:T(8,128)(2,1)S(1)} %get-tuple-element.35.scaled, bf16[512,128,128]{2,1,0:T(8,128)(2,1)} %get-tuple-element.28.tiles), custom_call_target="tpu_custom_call" | custom-call | flops 268435456 | bytes 8388608 | tf_op jit(solution)/shard_map/own2/pallas_call | solution.py:522
  187.3 12.1 %all-to-all-done.4 = bf16[32,2,32,128]{3,2,1,0:T(8,128)(2,1)S(1)} async-done(((bf16[32,2,32,128]{3,2,1,0:T(8,128)(2,1)}), bf16[32,2,32,128]{3,2,1,0:T(8,128)(2,1)S(1)}, u32[]{:S(2)}, u32[]{:S(2)}) %all-to-all-start.4) | async-done | bytes 524320 | tf_op jit(solution)/shard_map/all_to_all | solution.py:39
  199.4 5.3 %round2.1 = (f32[32,4096]{1,0:T(8,128)S(1)}, bf16[32,32,128]{2,1,0:T(8,128)(2,1)S(1)}, bf16[64,32,128]{2,1,0:T(8,128)(2,1)}) custom-call(s32[5,512]{1,0:T(8,128)S(1)} %concatenate.8.work_in, bf16[64,32,128]{2,1,0:T(8,128)(2,1)S(1)} %bitcast.34, f32[32,32,128]{2,1,0:T(8,128)S(1)} %own2.1.total_in, f32[32,128]{1,0:T(8,128)S(1)} %get-tuple-element.29.root, ...), custom_call_target="tpu_custom_call" | custom-call | flops 268435456 | bytes 8388608 | tf_op jit(solution)/shard_map/round2/pallas_call | solution.py:533
  204.7 2.6 %all-to-all-start.5 = ((bf16[32,2,32,128]{3,2,1,0:T(8,128)(2,1)}), bf16[32,2,32,128]{3,2,1,0:T(8,128)(2,1)S(1)}, u32[]{:S(2)}, u32[]{:S(2)}) async-start(bf16[32,2,32,128]{3,2,1,0:T(8,128)(2,1)} %bitcast.21), calls=%async_computation.5 | async-start | bytes 1048576 | tf_op jit(solution)/shard_map/all_to_all | solution.py:39
  207.3 4.2 %own3.1.total_in = f32[32,32,128]{2,1,0:T(8,128)S(1)} custom-call(s32[5,512]{1,0:T(8,128)S(1)} %concatenate.9.work.work_in, bf16[32,32,128]{2,1,0:T(8,128)(2,1)S(1)} %get-tuple-element.38.scaled, bf16[512,128,128]{2,1,0:T(8,128)(2,1)} %get-tuple-element.28.tiles), custom_call_target="tpu_custom_call" | custom-call | flops 268435456 | bytes 8388608 | tf_op jit(solution)/shard_map/own3/pallas_call | solution.py:522
  211.4 12.1 %all-to-all-done.5 = bf16[32,2,32,128]{3,2,1,0:T(8,128)(2,1)S(1)} async-done(((bf16[32,2,32,128]{3,2,1,0:T(8,128)(2,1)}), bf16[32,2,32,128]{3,2,1,0:T(8,128)(2,1)S(1)}, u32[]{:S(2)}, u32[]{:S(2)}) %all-to-all-start.5) | async-done | bytes 524320 | tf_op jit(solution)/shard_map/all_to_all | solution.py:39
  223.5 4.8 %round3.1 = (f32[32,4096]{1,0:T(8,128)S(1)}, f32[32,8,128]{2,1,0:T(8,128)S(1)}) custom-call(s32[5,512]{1,0:T(8,128)S(1)} %concatenate.8.work_in, bf16[64,32,128]{2,1,0:T(8,128)(2,1)S(1)} %bitcast.32, f32[32,32,128]{2,1,0:T(8,128)S(1)} %own3.1.total_in, f32[32,128]{1,0:T(8,128)S(1)} %get-tuple-element.29.root, f32[32,4096]{1,0:T(8,128)S(1)} %get-tuple-element.39.cur, ...), custom_call_target="tpu_custom_call" | custom-call | flops 268435456 | bytes 8388608 | tf_op jit(solution)/shard_map/round3/pallas_call | solution.py:533
  228.3 10.2 %all_to_all.39.parts = f32[32,8,128]{2,1,0:T(8,128)S(1)} all-to-all(f32[32,8,128]{2,1,0:T(8,128)S(1)} %get-tuple-element.40), channel_id=1, replica_groups=mesh['gx'=4,'gy'=8] {'gx','gy'}, dimensions={0} | all-to-all | bytes 262144 | tf_op jit(solution)/shard_map/all_to_all | solution.py:39
  238.5 4.2 %finish.1 = (f32[32,4096]{1,0:T(8,128)}, f32[32,32]{1,0:T(8,128)}) custom-call(f32[32,8,128]{2,1,0:T(8,128)S(1)} %all_to_all.39.parts, f32[32,4096]{1,0:T(8,128)S(1)} %get-tuple-element.41.flat), custom_call_target="tpu_custom_call" | custom-call | tf_op jit(solution)/shard_map/finish/pallas_call | solution.py:549
  (16 shorter events, 0.2 us)
Async XLA Ops:
  2.2 14.4 %all-to-all-start = ((s32[32,1,32]{2,1,0:T(1,128)}), s32[32,1,32]{2,1,0:T(1,128)S(1)}, u32[]{:S(2)}, u32[]{:S(2)}) async-start(s32[32,1,32]{2,1,0:T(1,128)} %bitcast.41), calls=%async_computation | async-start | bytes 32768 | tf_op jit(solution)/shard_map/all_to_all | solution.py:39
  20.8 3.8 %copy-start.3 = (s32[32,16]{0,1:T(8,128)S(1)}, s32[32,16]{0,1:T(8,128)}, u32[]{:S(2)}) copy-start(s32[32,16]{0,1:T(8,128)} %param.8) | copy-start | bytes 6148
  20.8 3.9 %copy-start.4 = (s32[32,16]{0,1:T(8,128)S(1)}, s32[32,16]{0,1:T(8,128)}, u32[]{:S(2)}) copy-start(s32[32,16]{0,1:T(8,128)} %param.9) | copy-start | bytes 6148
  20.8 4.1 %copy-start.2 = (s32[32,32]{1,0:T(8,128)S(1)}, s32[32,32]{1,0:T(8,128)}, u32[]{:S(2)}) copy-start(s32[32,32]{1,0:T(8,128)} %need.1) | copy-start | bytes 12292
  20.9 12.4 %copy-start.1 = (bf16[4096,256]{1,0:T(8,128)(2,1)S(1)}, bf16[4096,256]{1,0:T(8,128)(2,1)}, u32[]{:S(2)}) copy-start(bf16[4096,256]{1,0:T(8,128)(2,1)} %param.5) | copy-start | bytes 6291460
  20.9 100.1 %all-to-all-start.1 = ((bf16[32,520,128]{2,1,0:T(8,128)(2,1)}), bf16[32,520,128]{2,1,0:T(8,128)(2,1)}, u32[]{:S(2)}, u32[]{:S(2)}) async-start(bf16[32,520,128]{2,1,0:T(8,128)(2,1)} %pack.1), calls=%async_computation.1 | async-start | bytes 8519680 | tf_op jit(solution)/shard_map/all_to_all | solution.py:39
  28.4 92.6 %copy-start = (f32[32,4096]{1,0:T(8,128)S(1)}, f32[32,4096]{1,0:T(8,128)}, u32[]{:S(2)}) copy-start(f32[32,4096]{1,0:T(8,128)} %prev.3) | copy-start | bytes 1572868
  132.3 18.9 %all-to-all-start.2 = ((bf16[32,2,32,128]{3,2,1,0:T(8,128)(2,1)}), bf16[32,2,32,128]{3,2,1,0:T(8,128)(2,1)S(1)}, u32[]{:S(2)}, u32[]{:S(2)}) async-start(bf16[32,2,32,128]{3,2,1,0:T(8,128)(2,1)} %bitcast.15), calls=%async_computation.2 | async-start | bytes 1048576 | tf_op jit(solution)/shard_map/all_to_all | solution.py:39
  156.4 18.9 %all-to-all-start.3 = ((bf16[32,2,32,128]{3,2,1,0:T(8,128)(2,1)}), bf16[32,2,32,128]{3,2,1,0:T(8,128)(2,1)S(1)}, u32[]{:S(2)}, u32[]{:S(2)}) async-start(bf16[32,2,32,128]{3,2,1,0:T(8,128)(2,1)} %bitcast.17), calls=%async_computation.3 | async-start | bytes 1048576 | tf_op jit(solution)/shard_map/all_to_all | solution.py:39
  180.5 18.9 %all-to-all-start.4 = ((bf16[32,2,32,128]{3,2,1,0:T(8,128)(2,1)}), bf16[32,2,32,128]{3,2,1,0:T(8,128)(2,1)S(1)}, u32[]{:S(2)}, u32[]{:S(2)}) async-start(bf16[32,2,32,128]{3,2,1,0:T(8,128)(2,1)} %bitcast.19), calls=%async_computation.4 | async-start | bytes 1048576 | tf_op jit(solution)/shard_map/all_to_all | solution.py:39
  204.7 18.9 %all-to-all-start.5 = ((bf16[32,2,32,128]{3,2,1,0:T(8,128)(2,1)}), bf16[32,2,32,128]{3,2,1,0:T(8,128)(2,1)S(1)}, u32[]{:S(2)}, u32[]{:S(2)}) async-start(bf16[32,2,32,128]{3,2,1,0:T(8,128)(2,1)} %bitcast.21), calls=%async_computation.5 | async-start | bytes 1048576 | tf_op jit(solution)/shard_map/all_to_all | solution.py:39
